TPU v7x, 128 devices: a whole 4x4x4 slice. The times are simulated.
128 devices in a mesh: dap: 32 (over z, x, y_lo), head: 4 (over y_hi, core).
Axes of the slice: x: 4, y: 4 (y_hi: 2, y_lo: 2; y = y_hi * 2 + y_lo), z: 4, core: 2. Of those that a mesh axis runs over, the one named last changes fastest.
Arguments:
- multiple_aligned_family: bfloat16 [512, 512, 256], P('dap')
- homolog_present_flags: int32 [512], replicated, may hold values from 0 to 1, as said below
- amino_present_flags: int32 [512], replicated, may hold values 0 or 1
- focus_layernorm_scaling: float32 [256], replicated, may hold values from 0.5 to 1.5
- focus_layernorm_offset: float32 [256], replicated, may hold values from -1.8 to 1.8
- combined_focus_matrices: bfloat16 [256, 4, 256], P(None, None, 'head')
- sigmoid_switch_offset: float32 [256], P('head'), may hold values from -4 to 4
- focus_final_matrix: bfloat16 [256, 256], P('head'), may hold values from -0.375 to 0.375
- focus_final_offset: float32 [256], replicated, may hold values from -3 to 3
- tensor_layernorm_scaling: float32 [256], replicated, may hold values from 0.5 to 1.5
- tensor_layernorm_offset: float32 [256], replicated, may hold values from -1.8 to 1.8
- tensor_product_factors: bfloat16 [256, 2, 32], replicated, may hold values from -0.375 to 0.375
- tensor_final_matrix: float32 [1024, 128], replicated, may hold values from -0.1875 to 0.1875
- tensor_final_offset: float32 [128], replicated, may hold values from -4 to 4
Outputs:
- alignment_output: bfloat16 [512, 512, 256], P(('dap', 'head'))
- pair_mean_update: float32 [512, 512, 128], P('dap', 'head')
Inputs may be any that keep to these rules, and one draw needn't show every extreme that they name: homolog_present_flags[0] is always 1.
All inputs are finite; a program needn't handle non-finite values.
Results may differ from a plain program's by a relative error of at most 0.005.
Values may be sent and summed in bfloat16 or wider, within the bound.
No kernel may reach another device: no remote copies, remote signals or barrier semaphores. Data moves between devices by JAX's collectives and lax.ppermute only.
A program may use at most 256 MiB of HBM per device.

v0:
```python
import math

import jax
import jax.numpy as jnp
from jax import lax
from jax.experimental import pallas as pl
from jax.experimental.pallas import tpu as pltpu
from jax.sharding import PartitionSpec as P

DH = 32
CO = 32
LOG2E = math.log2(math.e)
NT = (((1,), (1,)), ((), ()))
TN = (((0,), (0,)), ((), ()))
F32 = jnp.float32
BF16 = jnp.bfloat16


def layer_norm(value, gain, bias):
    mean = jnp.mean(value, -1, keepdims=True)
    centred = value - mean
    spread = jnp.mean(centred * centred, -1, keepdims=True)
    return centred * lax.rsqrt(spread + 1e-05) * gain + bias


def attend_kernel(
    amino_ref,
    x_ref,
    w_ref,
    shift_ref,
    gain_ref,
    bias_ref,
    out_bias_ref,
    gain2_ref,
    bias2_ref,
    keep_col_ref,
    keep_row_ref,
    right_weight_ref,
    left_weight_ref,
    rows_ref,
    left_ref,
    right_ref,
    q_ref,
    k_ref,
    v_ref,
    g_ref,
    a_ref,
    rows_scratch,
    right_scratch,
):
    step = pl.program_id(0)
    steps = pl.num_programs(0)
    groups, unit, chans = w_ref.shape
    width = chans // groups
    seqs = keep_col_ref.shape[0]
    x = x_ref[...].reshape(seqs, chans).astype(F32)
    normed = layer_norm(x, gain_ref[...], bias_ref[...]).astype(BF16)

    def weight(which):
        return w_ref[:, which * width : (which + 1) * width, :].reshape(groups * width, chans)

    def transposed(which):
        return lax.dot_general(weight(which), normed, NT, preferred_element_type=F32)

    q_ref[...] = (transposed(0) * (DH**-0.5 * LOG2E)).astype(BF16)
    k_ref[...] = lax.dot_general(normed, weight(1), NT, preferred_element_type=F32).astype(BF16)
    v_ref[...] = transposed(2).astype(BF16)
    g_ref[...] = jax.nn.sigmoid(transposed(3) + shift_ref[...])
    present = jnp.broadcast_to(keep_col_ref[...], (seqs, seqs)) > 0.0
    ones = jnp.ones((16, seqs), BF16)
    for head in range(chans // DH):
        low, high = head * DH, (head + 1) * DH
        scores = jnp.dot(k_ref[:, low:high], q_ref[low:high, :], preferred_element_type=F32)
        scores = jnp.where(present, scores, F32(-1e9 * LOG2E))
        top = jnp.max(scores, 0, keepdims=True)
        probs = jnp.exp2(scores - top).astype(BF16)
        both = jnp.concatenate([v_ref[low:high, :], ones], 0)
        mixed = jnp.dot(both, probs, preferred_element_type=F32)
        scale = 1.0 / mixed[DH : DH + 1, :]
        a_ref[low:high, :] = (mixed[:DH, :] * scale * g_ref[low:high, :]).astype(BF16)
    update = lax.dot_general(a_ref[...], weight(4), TN, preferred_element_type=F32)
    fresh = (x + update + out_bias_ref[...]).astype(BF16)
    wide = fresh.astype(F32)
    for part in range(chans // 128):
        rows_scratch[part, pl.ds(step, seqs, stride=steps), :] = wide[:, part * 128 : (part + 1) * 128]
    opm = layer_norm(wide, gain2_ref[...], bias2_ref[...]).astype(BF16)
    here = amino_ref[step].astype(F32)
    left = lax.dot_general(left_weight_ref[...], opm, NT, preferred_element_type=F32)
    left_ref[...] = (left * (keep_row_ref[...] * here)).astype(BF16)[None]
    right = jnp.dot(opm, right_weight_ref[...], preferred_element_type=F32)
    right = right * (keep_col_ref[...] * here)

    @pl.when(step == 0)
    def _():
        right_scratch[...] = right

    @pl.when(step > 0)
    def _():
        right_scratch[...] += right

    @pl.when(step == steps - 1)
    def _():
        right_ref[...] = right_scratch[...].astype(BF16)
        for part in range(chans // 128):
            rows_ref[:, part * 128 : (part + 1) * 128] = rows_scratch[part].astype(BF16)


def pair_kernel(left_ref, right_ref, weight_ref, bias_ref, inverse_ref, out_ref, mid_ref):
    step = pl.program_id(0)
    count, seqs, lanes = right_ref.shape
    rows = out_ref.shape[0]
    pieces = jnp.concatenate([right_ref[q] for q in range(count)], 1)
    outer = jnp.dot(left_ref[...], pieces, preferred_element_type=F32).astype(BF16)
    for q in range(count):
        at = pl.multiple_of((step * count + q) * rows, rows)
        for c in range(CO):
            mid_ref[pl.ds(at, rows), c * lanes : (c + 1) * lanes] = outer[
                c * rows : (c + 1) * rows, q * lanes : (q + 1) * lanes
            ]

    @pl.when(step == pl.num_programs(0) - 1)
    def _():
        total = jnp.dot(mid_ref[...], weight_ref[...], preferred_element_type=F32)
        depth = bias_ref.shape[1]
        blocks = total.shape[0] // rows
        inner = lanes // CO
        for k in range(inner):
            part = (total[:, k * depth : (k + 1) * depth] + bias_ref[...]) * inverse_ref[
                :, k : k + 1
            ]
            for b in range(blocks):
                out_ref[:, b * inner + k, :] = part[b * rows : (b + 1) * rows]


def whole(shape):
    return pl.BlockSpec(shape, lambda *_: (0,) * len(shape))


def per_device(
    msa,
    homolog,
    amino,
    gain,
    bias,
    focus,
    switch,
    final,
    final_bias,
    gain2,
    bias2,
    factors,
    pair_weight,
    pair_bias,
):
    n_dap, n_head = lax.axis_size("dap"), lax.axis_size("head")
    head_id, dap_id = lax.axis_index("head"), lax.axis_index("dap")
    own_seqs, residues, chans = msa.shape
    seqs = homolog.shape[0]
    width = focus.shape[2]
    col_width = residues // n_head
    mine = col_width // n_dap
    nz, nx, ny = 4, 4, 2

    parts = jnp.moveaxis(focus, 0, 2).reshape(4 * width, chans)
    first = lax.reduce_precision(switch, 8, 7)
    second = lax.reduce_precision(switch - first, 8, 7)
    third = switch - first - second
    offsets = jnp.zeros((16, chans), BF16)
    offsets = offsets.at[:3, :width].set(jnp.stack([first, second, third]).astype(BF16))
    bundle = jnp.concatenate([parts, final, offsets], 0)
    weights = lax.all_gather(bundle, "head", axis=0, tiled=False)
    base = 5 * width
    shift = weights[:, base : base + 3, :width].astype(F32)
    shift = ((shift[:, 0] + shift[:, 1]) + shift[:, 2]).reshape(chans, 1)
    shift = jnp.broadcast_to(shift, (chans, 1))

    block = lax.dynamic_slice_in_dim(msa, head_id * col_width, col_width, 1)
    block = block.reshape(own_seqs, nx, ny, nz, mine, chans)
    block = block.transpose(3, 1, 2, 4, 0, 5).reshape(n_dap, mine * own_seqs, chans)
    block = lax.all_to_all(block, "dap", split_axis=0, concat_axis=0, tiled=True)

    keep = homolog.astype(F32)
    eye = jnp.eye(mine, dtype=BF16)
    right_weight = (eye[:, None, :, None] * factors[:, 1][None, :, None, :]).reshape(
        mine, chans, mine * CO
    )
    left_weight = factors[:, 0].T
    zi, xi, yi = dap_id // (nx * ny), (dap_id // ny) % nx, dap_id % ny
    start = head_id * col_width + xi * (ny * nz * mine) + yi * (nz * mine) + zi * mine
    own_amino = lax.dynamic_slice_in_dim(amino, start, mine)
    row = lambda v: v.reshape(1, chans)
    lanes = mine * CO
    rows, left, right = pl.pallas_call(
        attend_kernel,
        grid=(mine,),
        in_specs=[
            pl.BlockSpec(memory_space=pltpu.SMEM),
            pl.BlockSpec((n_dap, own_seqs, chans), lambda k: (0, k, 0)),
            whole(weights.shape),
            whole((chans, 1)),
            whole((1, chans)),
            whole((1, chans)),
            whole((1, chans)),
            whole((1, chans)),
            whole((1, chans)),
            whole((seqs, 1)),
            whole((1, seqs)),
            pl.BlockSpec((None, chans, lanes), lambda k: (k, 0, 0)),
            whole((CO, chans)),
        ],
        out_specs=[
            whole((seqs * mine, chans)),
            pl.BlockSpec((1, CO, seqs), lambda k: (k, 0, 0)),
            whole((seqs, lanes)),
        ],
        out_shape=[
            jax.ShapeDtypeStruct((seqs * mine, chans), BF16),
            jax.ShapeDtypeStruct((mine, CO, seqs), BF16),
            jax.ShapeDtypeStruct((seqs, lanes), BF16),
        ],
        scratch_shapes=[
            pltpu.VMEM((chans, seqs), BF16),
            pltpu.VMEM((seqs, chans), BF16),
            pltpu.VMEM((chans, seqs), BF16),
            pltpu.VMEM((chans, seqs), F32),
            pltpu.VMEM((chans, seqs), BF16),
            pltpu.VMEM((chans // 128, seqs * mine, 128), F32),
            pltpu.VMEM((seqs, lanes), F32),
        ],
        compiler_params=pltpu.CompilerParams(
            dimension_semantics=("arbitrary",), vmem_limit_bytes=48 * 2**20
        ),
        cost_estimate=pl.CostEstimate(
            flops=16_000_000_000, bytes_accessed=4 * 2**20, transcendentals=9_000_000
        ),
        name="attend",
    )(
        own_amino,
        block,
        weights,
        shift,
        row(gain),
        row(bias),
        row(final_bias),
        row(gain2),
        row(bias2),
        keep.reshape(seqs, 1),
        keep.reshape(1, seqs),
        right_weight,
        left_weight,
    )

    spread = jnp.broadcast_to(right[None], (n_dap, seqs, lanes))
    gathered = lax.all_to_all(spread, "dap", split_axis=0, concat_axis=0, tiled=True)

    swap = []
    for z in range(nz):
        for rest in range(nx * ny):
            for h in range(n_head):
                swap.append(
                    ((z * nx * ny + rest) * n_head + h, (h * nx * ny + rest) * n_head + z)
                )
    left = lax.ppermute(left, ("dap", "head"), swap)
    left = lax.all_gather(left, "head", axis=0, tiled=True)
    i_rows = mine * n_head
    left = jnp.swapaxes(left, 0, 1).reshape(CO * i_rows, seqs)

    back = lax.all_to_all(
        rows.reshape(n_dap * n_head, seqs * mine // (n_dap * n_head), chans),
        ("dap", "head"),
        split_axis=0,
        concat_axis=0,
        tiled=True,
    )
    own = own_seqs // n_head
    back = back.reshape(nz, nx, ny, n_head, own, mine, chans)
    alignment = back.transpose(4, 3, 1, 2, 0, 5, 6).reshape(own, residues, chans)

    depth = pair_weight.shape[1]
    wide = pair_weight.astype(BF16).reshape(CO, 1, CO, 1, depth)
    wide = (eye[None, :, None, :, None] * wide).reshape(CO * lanes, mine * depth)
    total = jnp.sum(homolog).astype(F32)
    row_keep = lax.dynamic_slice_in_dim(amino, dap_id * i_rows, i_rows).astype(F32)
    col_keep = lax.dynamic_slice_in_dim(amino, head_id * col_width, col_width).astype(F32)
    norm = jnp.maximum(
        total * row_keep[None, :, None] * col_keep.reshape(n_dap, 1, mine), 1.0
    )
    inverse = (1.0 / norm).reshape(n_dap * i_rows, mine)
    count = 4
    order = lambda b: b
    gathered = gathered.reshape(nz, nx * ny, seqs, lanes)
    pair = pl.pallas_call(
        pair_kernel,
        grid=(n_dap // count,),
        in_specs=[
            whole((CO * i_rows, seqs)),
            pl.BlockSpec((nz, None, seqs, lanes), lambda k: (0, k, 0, 0)),
            whole(wide.shape),
            whole((1, depth)),
            whole(inverse.shape),
        ],
        out_specs=whole((i_rows, col_width, depth)),
        out_shape=jax.ShapeDtypeStruct((i_rows, col_width, depth), F32),
        scratch_shapes=[pltpu.VMEM((n_dap * i_rows, CO * lanes), BF16)],
        compiler_params=pltpu.CompilerParams(
            dimension_semantics=("arbitrary",), vmem_limit_bytes=48 * 2**20
        ),
        cost_estimate=pl.CostEstimate(
            flops=5_000_000_000, bytes_accessed=10 * 2**20, transcendentals=0
        ),
        name="pair",
    )(left, gathered, wide, pair_bias.reshape(1, depth), inverse)
    return alignment, pair


def solution(mesh):
    return jax.shard_map(
        per_device,
        mesh=mesh,
        in_specs=(
            P("dap", None, None),
            P(),
            P(),
            P(),
            P(),
            P(None, None, "head"),
            P("head"),
            P("head", None),
            P(),
            P(),
            P(),
            P(),
            P(),
            P(),
        ),
        out_specs=(P(("dap", "head"), None, None), P("dap", "head", None)),
        check_vma=False,
    )
```

profile of v0, /device:TPU:11, one launch (start us, length us, event | category | flops | bytes accessed | tf_op | source)
XLA Modules:
  0.0 169.9 jit_solution(13565076021454858214)
XLA Ops:
  0.6 0.0 copy-start.11
  0.6 0.0 copy-start.7
  0.7 0.0 copy-start.9
  0.7 1.4 constant_dynamic-slice_fusion
  2.0 0.0 copy-start.10
  2.0 0.0 copy-start.8
  2.0 0.0 copy-start.12
  2.1 0.0 copy-start
  2.1 0.0 copy-start.1
  2.1 0.0 copy-start.2
  2.1 0.0 copy-start.3
  2.1 0.0 copy-start.4
  2.1 0.6 copy.33
  2.7 1.1 copy.27
  3.8 8.8 %all-to-all-start = ((bf16[32,64,256]{2,1,0:T(8,128)(2,1)}), bf16[32,64,256]{2,1,0:T(8,128)(2,1)S(1)}, u32[]{:S(2)}, u32[]{:S(2)}) async-start(bf16[32,64,256]{2,1,0:T(8,128)(2,1)} %bitcast.2), calls=%async_computation | async-start | bytes 2097152 | tf_op jit(solution)/shard_map/all_to_all | solution.py:180
  12.6 0.0 copy-done.11
  12.6 0.0 copy-done.7
  12.6 0.0 copy-done.9
  12.7 19.3 %all-gather = bf16[1344,256]{1,0:T(8,128)(2,1)S(1)} all-gather(bf16[336,256]{1,0:T(8,128)(2,1)S(1)} %pad_maximum_fusion), channel_id=2, replica_groups=mesh['dap'=32,'head'=4] {'head'}, dimensions={0}, use_global_device_ids=true | all-gather | bytes 860160 | tf_op jit(solution)/shard_map/all_gather | solution.py:171
  32.0 0.1 add.67.shift_ref
  32.2 0.0 copy-done.10
  32.2 0.6 fusion.17
  32.8 0.1 copy.30.keep_col_ref
  33.0 0.0 copy-done.8
  33.0 0.1 copy.28
  33.1 0.1 mul.93
  33.2 0.1 mul.94
  33.3 0.0 copy-done.12
  33.3 0.1 dynamic_slice.12.amino_ref
  33.4 0.0 all-to-all-done.x_ref
  33.4 0.0 copy-done
  33.4 0.0 copy-done.1
  33.4 0.0 copy-done.2
  33.4 0.0 copy-done.3
  33.4 0.0 copy-done.4
  33.5 20.0 %attend.1 = (bf16[2048,256]{1,0:T(8,128)(2,1)S(1)}, bf16[4,32,512]{2,1,0:T(8,128)(2,1)S(1)}, bf16[512,128]{1,0:T(8,128)(2,1)S(1)}) custom-call(s32[4]{0:T(128)S(1)} %dynamic_slice.12.amino_ref, bf16[32,64,256]{2,1,0:T(8,128)(2,1)S(1)} %all-to-all-done.x_ref, bf16[4,336,256]{2,1,0:T(8,128)(2,1)S(1)} %bitcast.50, f32[256,1]{1,0:T(8,128)S(1)} %add.67.shift_ref, ...), custom_call_target="tpu_custom_call" | custom-call | flops 16000000000 | bytes 4194304 | tf_op jit(solution)/shard_map/attend/pallas_call | solution.py:193
  53.4 25.6 %all_to_all.15 = bf16[128,16,256]{2,1,0:T(8,128)(2,1)S(1)} all-to-all(bf16[128,16,256]{2,1,0:T(8,128)(2,1)S(1)} %bitcast.48), channel_id=1, replica_groups=mesh['dap'=32,'head'=4] {'dap','head'}, dimensions={0} | all-to-all | bytes 2097152 | tf_op jit(solution)/shard_map/all_to_all | solution.py:268
  79.0 2.9 %broadcast_in_dim.2 = bf16[32,512,128]{2,1,0:T(8,128)(2,1)} broadcast(bf16[512,128]{1,0:T(8,128)(2,1)S(1)} %get-tuple-element.19), dimensions={1,2} | broadcast | bytes 4325376 | tf_op jit(solution)/shard_map/broadcast_in_dim | solution.py:253
  81.9 0.0 copy-start.6
  81.9 6.5 %all-to-all-start.2 = ((bf16[32,512,128]{2,1,0:T(8,128)(2,1)}), bf16[32,512,128]{2,1,0:T(8,128)(2,1)}, u32[]{:S(2)}, u32[]{:S(2)}) async-start(bf16[32,512,128]{2,1,0:T(8,128)(2,1)} %broadcast_in_dim.2), calls=%async_computation.2 | async-start | bytes 8388608 | tf_op jit(solution)/shard_map/all_to_all | solution.py:254
  88.4 0.0 copy-done.6
  88.5 3.6 %broadcast_multiply_fusion = bf16[32,4,32,4,128]{4,3,2,1,0:T(4,128)(2,1)} fusion(bf16[32,32,128]{2,1,0:T(8,128)(2,1)S(1)} %bitcast.65, bf16[4,4]{1,0:T(4,128)(2,1)S(1)} %fusion.12), kind=kLoop, calls=%fused_computation.1 | loop fusion | flops 2097152 | bytes 4456480 | tf_op jit(solution)/shard_map/mul | solution.py:281
  92.0 4.5 %collective-permute-start = (bf16[4,32,512]{2,1,0:T(8,128)(2,1)S(1)}, bf16[4,32,512]{2,1,0:T(8,128)(2,1)S(1)}, u32[]{:S(2)}, u32[]{:S(2)}) collective-permute-start(bf16[4,32,512]{2,1,0:T(8,128)(2,1)S(1)} %get-tuple-element.18), channel_id=1, source_target_pairs={{0,0},{1,32},{2,64},{3,96},{4,4},{5,36},{6,68},{7,100},{8,8},{9,40... | collective-permute-start | bytes 393224 | tf_op jit(solution)/shard_map/ppermute | solution.py:263
  96.5 0.1 dynamic-slice_convert_fusion
  96.6 4.9 %copy.37 = bf16[512,8,4,128]{3,1,2,0:T(8,128)(2,1)} copy(bf16[512,8,4,128]{3,2,1,0:T(4,128)(2,1)} %bitcast.60) | data formatting | bytes 8388608
  101.5 0.0 copy-start.5
  101.5 0.1 mul.112
  102.3 0.1 convert_multiply_fusion
  102.4 0.1 mul.110
  102.4 0.1 fusion.1.inverse_ref
  102.6 21.6 %collective-permute-done = bf16[4,32,512]{2,1,0:T(8,128)(2,1)S(1)} collective-permute-done((bf16[4,32,512]{2,1,0:T(8,128)(2,1)S(1)}, bf16[4,32,512]{2,1,0:T(8,128)(2,1)S(1)}, u32[]{:S(2)}, u32[]{:S(2)}) %collective-permute-start) | collective-permute-done | bytes 131104 | tf_op jit(solution)/shard_map/ppermute | solution.py:263
  124.2 31.5 %all_gather.11 = bf16[16,32,512]{2,1,0:T(8,128)(2,1)S(1)} all-gather(bf16[4,32,512]{2,1,0:T(8,128)(2,1)S(1)} %collective-permute-done), channel_id=1, replica_groups=mesh['dap'=32,'head'=4] {'head'}, dimensions={0}, use_global_device_ids=true | all-gather | bytes 655360 | tf_op jit(solution)/shard_map/all_gather | solution.py:264
  155.7 0.3 copy.32
  156.0 0.3 reshape.158
  156.3 0.6 copy.38
  156.9 1.1 reshape.159
  158.0 0.0 all-to-all-done.2
  158.0 0.0 copy-done.5
  158.0 11.9 %pair.1 = f32[16,128,128]{2,1,0:T(8,128)} custom-call(bf16[512,512]{1,0:T(8,128)(2,1)S(1)} %bitcast.51, bf16[4,8,512,128]{3,2,1,0:T(8,128)(2,1)} %bitcast.24.right_ref, bf16[4096,512]{1,0:T(8,128)(2,1)} %bitcast.61, f32[1,128]{1,0:T(1,128)S(1)} %bitcast.59, f32[512,4]{1,0:T(8,128)S(1)} %fusion.1.inverse_ref), custom_call_target="tpu_custom_call" | custom-call | flops 5000000000 | bytes 10485760 | tf_op jit(solution)/shard_map/pair/pallas_call | solution.py:292
  (11 shorter events, 0.1 us)
Async XLA Ops:
  0.6 12.0 %copy-start.11 = (f32[64]{0:T(128)S(1)}, f32[64]{0:T(128)}, u32[]{:S(2)}) copy-start(f32[64]{0:T(128)} %param.22) | copy-start | bytes 772
  0.6 12.0 %copy-start.7 = (bf16[256,4,64]{0,2,1:T(8,128)(2,1)S(1)}, bf16[256,4,64]{0,2,1:T(8,128)(2,1)}, u32[]{:S(2)}) copy-start(bf16[256,4,64]{0,2,1:T(8,128)(2,1)} %param.21) | copy-start | bytes 393220
  0.7 12.0 %copy-start.9 = (bf16[64,256]{1,0:T(8,128)(2,1)S(1)}, bf16[64,256]{1,0:T(8,128)(2,1)}, u32[]{:S(2)}) copy-start(bf16[64,256]{1,0:T(8,128)(2,1)} %param.23) | copy-start | bytes 98308
  2.0 30.1 %copy-start.10 = (s32[512]{0:T(512)S(1)}, s32[512]{0:T(512)}, u32[]{:S(2)}) copy-start(s32[512]{0:T(512)} %param.17) | copy-start | bytes 6148
  2.0 30.9 %copy-start.8 = (bf16[256,2,32]{0,2,1:T(8,128)(2,1)S(1)}, bf16[256,2,32]{0,2,1:T(8,128)(2,1)}, u32[]{:S(2)}) copy-start(bf16[256,2,32]{0,2,1:T(8,128)(2,1)} %param.27) | copy-start | bytes 98308
  2.0 31.2 %copy-start.12 = (s32[512]{0:T(512)S(1)}, s32[512]{0:T(512)}, u32[]{:S(2)}) copy-start(s32[512]{0:T(512)} %param.18) | copy-start | bytes 6148
  2.1 31.4 %copy-start = (f32[256]{0:T(256)S(1)}, f32[256]{0:T(256)}, u32[]{:S(2)}) copy-start(f32[256]{0:T(256)} %param.19) | copy-start | bytes 3076
  2.1 31.4 %copy-start.1 = (f32[256]{0:T(256)S(1)}, f32[256]{0:T(256)}, u32[]{:S(2)}) copy-start(f32[256]{0:T(256)} %param.20) | copy-start | bytes 3076
  2.1 31.3 %copy-start.2 = (f32[256]{0:T(256)S(1)}, f32[256]{0:T(256)}, u32[]{:S(2)}) copy-start(f32[256]{0:T(256)} %param.24) | copy-start | bytes 3076
  2.1 31.3 %copy-start.3 = (f32[256]{0:T(256)S(1)}, f32[256]{0:T(256)}, u32[]{:S(2)}) copy-start(f32[256]{0:T(256)} %param.25) | copy-start | bytes 3076
  2.1 31.3 %copy-start.4 = (f32[256]{0:T(256)S(1)}, f32[256]{0:T(256)}, u32[]{:S(2)}) copy-start(f32[256]{0:T(256)} %param.26) | copy-start | bytes 3076
  3.8 29.6 %all-to-all-start = ((bf16[32,64,256]{2,1,0:T(8,128)(2,1)}), bf16[32,64,256]{2,1,0:T(8,128)(2,1)S(1)}, u32[]{:S(2)}, u32[]{:S(2)}) async-start(bf16[32,64,256]{2,1,0:T(8,128)(2,1)} %bitcast.2), calls=%async_computation | async-start | bytes 2097152 | tf_op jit(solution)/shard_map/all_to_all | solution.py:180
  81.9 6.5 %copy-start.6 = (f32[1024,128]{1,0:T(8,128)S(1)}, f32[1024,128]{1,0:T(8,128)}, u32[]{:S(2)}) copy-start(f32[1024,128]{1,0:T(8,128)} %param.28) | copy-start | bytes 1572868
  81.9 76.0 %all-to-all-start.2 = ((bf16[32,512,128]{2,1,0:T(8,128)(2,1)}), bf16[32,512,128]{2,1,0:T(8,128)(2,1)}, u32[]{:S(2)}, u32[]{:S(2)}) async-start(bf16[32,512,128]{2,1,0:T(8,128)(2,1)} %broadcast_in_dim.2), calls=%async_computation.2 | async-start | bytes 8388608 | tf_op jit(solution)/shard_map/all_to_all | solution.py:254
  92.0 32.2 %collective-permute-start = (bf16[4,32,512]{2,1,0:T(8,128)(2,1)S(1)}, bf16[4,32,512]{2,1,0:T(8,128)(2,1)S(1)}, u32[]{:S(2)}, u32[]{:S(2)}) collective-permute-start(bf16[4,32,512]{2,1,0:T(8,128)(2,1)S(1)} %get-tuple-element.18), channel_id=1, source_target_pairs={{0,0},{1,32},{2,64},{3,96},{4,4},{5,36},{6,68},{7,100},{8,8},{9,40... | collective-permute-start | bytes 393224 | tf_op jit(solution)/shard_map/ppermute | solution.py:263
  101.5 56.5 %copy-start.5 = (f32[128]{0:T(128)S(1)}, f32[128]{0:T(128)}, u32[]{:S(2)}) copy-start(f32[128]{0:T(128)} %param.29) | copy-start | bytes 1540
where the time goes:
time: 170 us
  blocking collectives  76.4 us (45%)
  Pallas kernels  31.8 us (19%)
  waiting for transfers between devices  21.6 us (13%)
  starting transfers between devices  19.8 us (12%)
  local copies, waits for them, and re-layouts  14 us (8%)
  other arithmetic  4.64 us (3%)
    all_gather x1, blocking collectives, per_device(): left = lax.all_gather(left, 'head', axis=0, tiled=True)  31.5 us
    all_to_all x1, blocking collectives, per_device(): lax.all_to_all(rows.reshape(n_dap * n_head, seqs * mine // (n_dap * n_hea...  25.6 us
    ppermute x1, waiting for transfers between devices, per_device(): left = lax.ppermute(left, ('dap', 'head'), swap)  21.6 us
    pallas_call x1, Pallas kernels, per_device(): pl.pallas_call(attend_kernel, grid=(mine,), in_specs=[pl.BlockSpec(memory...  20 us
    all_gather x1, blocking collectives, per_device(): weights = lax.all_gather(bundle, 'head', axis=0, tiled=False)  19.3 us
    pallas_call x1, Pallas kernels, per_device(): pl.pallas_call(pair_kernel, grid=(n_dap // count,), in_specs=[whole((CO *...  11.9 us
    all_to_all x1, starting transfers between devices, per_device(): lax.all_to_all(block, 'dap', split_axis=0, concat_axis=0, tiled=True)  8.8 us
    all_to_all x1, starting transfers between devices, per_device(): lax.all_to_all(spread, 'dap', split_axis=0, concat_axis=0, tiled=True)  6.46 us
  transfers between devices with their start and end apart: 3, of which 1 were waited for; matrix products, arithmetic and copies ran while one was open for 7% of the time, Pallas kernels for 0%

commit v1 on v0

v1 whole, which is shorter than its diff:
```python
import math

import jax
import jax.numpy as jnp
import numpy as np
from jax import lax
from jax.experimental import pallas as pl
from jax.experimental.pallas import tpu as pltpu
from jax.sharding import PartitionSpec as P

DH = 32
CO = 32
STEPS = (0, -1, 1, 2)
LOG2E = math.log2(math.e)


def bf16_terms(value):
    terms = []
    for _ in range(3):
        term = float(np.float32(value).astype(jnp.bfloat16))
        terms.append(term)
        value = float(np.float32(value)) - term
    return tuple(terms)


MASKS = bf16_terms(-1e9 * LOG2E)
NT = (((1,), (1,)), ((), ()))
TN = (((0,), (0,)), ((), ()))
F32 = jnp.float32
BF16 = jnp.bfloat16


def layer_norm(value, gain, bias):
    mean = jnp.mean(value, -1, keepdims=True)
    centred = value - mean
    spread = jnp.mean(centred * centred, -1, keepdims=True)
    return centred * lax.rsqrt(spread + 1e-05) * gain + bias


def attend_kernel(
    amino_ref,
    x_ref,
    w0_ref,
    w1_ref,
    w2_ref,
    w3_ref,
    shift_ref,
    gain_ref,
    bias_ref,
    out_bias_ref,
    gain2_ref,
    bias2_ref,
    keep_col_ref,
    keep_row_ref,
    right_weight_ref,
    left_weight_ref,
    rows_ref,
    left_ref,
    right_ref,
    q_ref,
    k_ref,
    v_ref,
    g_ref,
    a_ref,
    rows_scratch,
    right_scratch,
):
    steps = left_ref.shape[0]
    seqs = keep_col_ref.shape[0]
    w_refs = (w0_ref, w1_ref, w2_ref, w3_ref)
    chans = w0_ref.shape[1]
    width = chans // len(w_refs)
    own = seqs // x_ref.shape[0]

    def weight(which):
        return jnp.concatenate([w[which * width : (which + 1) * width, :] for w in w_refs], 0)

    absent = 1.0 - keep_col_ref[...]
    column = lax.broadcasted_iota(jnp.int32, (seqs, 128), 1) - DH
    extra = jnp.where(column == 0, MASKS[0], jnp.where(column == 1, MASKS[1], MASKS[2]))
    extra = jnp.where((column >= 0) & (column < 3), extra * absent, 0.0).astype(BF16)
    for head in range(chans // DH):
        k_ref[head] = extra
    row = lax.broadcasted_iota(jnp.int32, (16, seqs), 0)
    rest = jnp.where(row < 3, 1.0, 0.0).astype(BF16)
    ones = jnp.ones((16, seqs), BF16)

    def body(step, _):
        at = pl.multiple_of(step * own, own)
        x = x_ref[:, pl.ds(at, own), :].reshape(seqs, chans).astype(F32)
        normed = layer_norm(x, gain_ref[...], bias_ref[...]).astype(BF16)

        def transposed(which):
            return lax.dot_general(weight(which), normed, NT, preferred_element_type=F32)

        q_ref[...] = (transposed(0) * (DH**-0.5 * LOG2E)).astype(BF16)
        keys = lax.dot_general(normed, weight(1), NT, preferred_element_type=F32)
        keys = (keys * keep_col_ref[...]).astype(BF16)
        for head in range(chans // DH):
            k_ref[head, :, :DH] = keys[:, head * DH : (head + 1) * DH]
        v_ref[...] = transposed(2).astype(BF16)
        g_ref[...] = jax.nn.sigmoid(transposed(3) + shift_ref[...])

        def score(index):
            head, part = index // 1, index % 1
            cols = slice(part * (seqs // 1), (part + 1) * (seqs // 1))
            query = jnp.concatenate([q_ref[head * DH : (head + 1) * DH, cols], rest[:, cols]], 0)
            return jnp.dot(k_ref[head, :, : DH + 16], query, preferred_element_type=F32)

        def attend(index, scores):
            head, part = index // 1, index % 1
            cols = slice(part * (seqs // 1), (part + 1) * (seqs // 1))
            low, high = head * DH, (head + 1) * DH
            top = jnp.max(scores, 0, keepdims=True)
            probs = jnp.exp2(scores - top).astype(BF16)
            both = jnp.concatenate([v_ref[low:high, :], ones], 0)
            mixed = jnp.dot(both, probs, preferred_element_type=F32)
            scale = 1.0 / mixed[DH : DH + 1, :]
            a_ref[low:high, cols] = (mixed[:DH, :] * scale * g_ref[low:high, cols]).astype(BF16)

        count = chans // DH * 1
        ahead = score(0)
        for index in range(count):
            now = ahead
            if index + 1 < count:
                ahead = score(index + 1)
            attend(index, now)
        update = lax.dot_general(a_ref[...], weight(4), TN, preferred_element_type=F32)
        fresh = (x + update + out_bias_ref[...]).astype(BF16)
        wide = fresh.astype(F32)
        for part in range(chans // 128):
            rows_scratch[part, pl.ds(step, seqs, stride=steps), :] = wide[
                :, part * 128 : (part + 1) * 128
            ]
        opm = layer_norm(wide, gain2_ref[...], bias2_ref[...]).astype(BF16)
        here = amino_ref[step].astype(F32)
        left = lax.dot_general(left_weight_ref[...], opm, NT, preferred_element_type=F32)
        left_ref[step] = (left * (keep_row_ref[...] * here)).astype(BF16)
        right = jnp.dot(opm, right_weight_ref[step], preferred_element_type=F32)
        right_scratch[...] += right * (keep_col_ref[...] * here)
        return 0

    right_scratch[...] = jnp.zeros_like(right_scratch)
    lax.fori_loop(0, steps, body, 0)
    right_ref[...] = right_scratch[...].astype(BF16).reshape(right_ref.shape)
    for part in range(chans // 128):
        rows_ref[:, part * 128 : (part + 1) * 128] = rows_scratch[part].astype(BF16)


def join_kernel(*refs):
    half = (len(refs) - 2) // 2
    for colour in range(2):
        out_ref = refs[2 * half + colour]
        for index in range(half):
            piece = refs[colour * half + index]
            count = piece.shape[0]
            out_ref[index * count : (index + 1) * count] = piece[...]


def pair_kernel(
    place_ref,
    left_ref,
    bias_ref,
    inverse_ref,
    back_ref,
    compact_ref,
    z0_ref,
    z1_ref,
    z2_ref,
    z3_ref,
    x0_ref,
    x1_ref,
    x2_ref,
    x3_ref,
    out_ref,
    aligned_ref,
    mid_ref,
    weight_ref,
):
    rows = out_ref.shape[0]
    lanes = z0_ref.shape[2]

    def source(dz, dx, dy):
        first = (z0_ref, z1_ref, z2_ref, z3_ref)[dz][dx * 2 + dy]
        second = (x0_ref, x1_ref, x2_ref, x3_ref)[dx][dz * 2 + dy]
        return jnp.concatenate([first, second], 0)

    low = lax.broadcasted_iota(jnp.int32, (8, back_ref.shape[2]), 0) < 4

    def arrange(index, _):
        head, xy = index // 8, index % 8
        blocks = [
            back_ref[(z * 8 + xy) * 4 + head].astype(F32) for z in range(4)
        ]
        for upper in range(2):
            tiles = [b[upper * 8 : upper * 8 + 8] for b in blocks]
            turned = [pltpu.roll(t, 4, 0) for t in tiles]
            first = [jnp.where(low, tiles[z], turned[z + 1]) for z in (0, 2)]
            second = [jnp.where(low, turned[z], tiles[z + 1]) for z in (0, 2)]
            at = pl.multiple_of(head * 128 + xy * 16, 16)
            for seq, value in ((0, first), (1, second)):
                aligned_ref[upper * 2 + seq, pl.ds(at, 16), :] = jnp.concatenate(
                    value, 0
                ).astype(BF16)
        return 0

    lax.fori_loop(0, back_ref.shape[0] // 4, arrange, 0)
    depth = bias_ref.shape[1]
    inner = lanes // CO
    nothing = jnp.zeros((CO, depth), BF16)
    for c in range(CO):
        block = compact_ref[c * CO : (c + 1) * CO, :].astype(BF16)
        for k in range(inner):
            at = (c * inner + k) * CO
            for j in range(inner):
                weight_ref[at : at + CO, j * depth : (j + 1) * depth] = (
                    block if j == k else nothing
                )
    left = left_ref[...]
    for dz in range(4):
        for pair in range(2):
            slots = [(dz, pair * 2 + q // 2, q % 2) for q in range(4)]
            pieces = jnp.concatenate([source(*slot) for slot in slots], 1)
            outer = jnp.dot(left, pieces, preferred_element_type=F32).astype(BF16)
            for q, (z, x, y) in enumerate(slots):
                at = pl.multiple_of(place_ref[(z * 4 + x) * 2 + y] * rows, rows)
                for c in range(CO):
                    mid_ref[pl.ds(at, rows), c * lanes : (c + 1) * lanes] = outer[
                        c * rows : (c + 1) * rows, q * lanes : (q + 1) * lanes
                    ]
    blocks = mid_ref.shape[0] // rows
    for k in range(0, inner, 2):
        total = jnp.dot(
            mid_ref[...],
            weight_ref[:, k * depth : (k + 2) * depth],
            preferred_element_type=F32,
        )
        for j in range(2):
            value = total[:, j * depth : (j + 1) * depth]
            value = (value + bias_ref[...]) * inverse_ref[:, k + j : k + j + 1]
            for b in range(blocks):
                out_ref[:, b * inner + k + j, :] = value[b * rows : (b + 1) * rows]


def whole():
    return pl.BlockSpec(memory_space=pltpu.VMEM)


def per_device(
    msa,
    homolog,
    amino,
    gain,
    bias,
    focus,
    switch,
    final,
    final_bias,
    gain2,
    bias2,
    factors,
    pair_weight,
    pair_bias,
):
    n_dap, n_head = lax.axis_size("dap"), lax.axis_size("head")
    head_id, dap_id = lax.axis_index("head"), lax.axis_index("dap")
    own_seqs, residues, chans = msa.shape
    seqs = homolog.shape[0]
    width = focus.shape[2]
    col_width = residues // n_head
    mine = col_width // n_dap
    nz, nx, ny = 4, 4, 2

    parts = jnp.moveaxis(focus, 0, 2).reshape(4 * width, chans)
    first = lax.reduce_precision(switch, 8, 7)
    second = lax.reduce_precision(switch - first, 8, 7)
    third = switch - first - second
    offsets = jnp.zeros((16, chans), BF16)
    offsets = offsets.at[:3, :width].set(jnp.stack([first, second, third]).astype(BF16))
    bundle = jnp.concatenate([parts, final, offsets], 0)
    bundles = [bundle] + [
        lax.ppermute(bundle, "head", [(h, h ^ flip) for h in range(n_head)])
        for flip in range(1, n_head)
    ]
    base = 5 * width
    shift = jnp.stack([b[base : base + 3, :width] for b in bundles]).astype(F32)
    shift = ((shift[:, 0] + shift[:, 1]) + shift[:, 2]).reshape(chans, 1)

    block = lax.dynamic_slice_in_dim(msa, head_id * col_width, col_width, 1)
    block = block.reshape(own_seqs, nx, ny, nz, mine, chans)
    block = block.transpose(3, 1, 2, 4, 0, 5).reshape(n_dap, mine * own_seqs, chans)
    block = lax.all_to_all(block, "dap", split_axis=0, concat_axis=0, tiled=True)

    keep = homolog.astype(F32)
    eye = jnp.eye(mine, dtype=BF16)
    right_weight = (eye[:, None, :, None] * factors[:, 1][None, :, None, :]).reshape(
        mine, chans, mine * CO
    )
    left_weight = factors[:, 0].T
    zi, xi, yi = dap_id // (nx * ny), (dap_id // ny) % nx, dap_id % ny
    start = head_id * col_width + xi * (ny * nz * mine) + yi * (nz * mine) + zi * mine
    own_amino = lax.dynamic_slice_in_dim(amino, start, mine)
    row = lambda v: v.reshape(1, chans)
    lanes = mine * CO
    depth = pair_weight.shape[1]
    rows, left, right = pl.pallas_call(
        attend_kernel,
        in_specs=[
            pl.BlockSpec(memory_space=pltpu.SMEM),
            whole(),
            *[whole()] * n_head,
            whole(),
            whole(),
            whole(),
            whole(),
            whole(),
            whole(),
            whole(),
            whole(),
            whole(),
            whole(),
        ],
        out_specs=[whole(), whole(), whole()],
        out_shape=[
            jax.ShapeDtypeStruct((seqs * mine, chans), BF16),
            jax.ShapeDtypeStruct((mine, CO, seqs), BF16),
            jax.ShapeDtypeStruct((2, seqs // 2, lanes), BF16),
        ],
        scratch_shapes=[
            pltpu.VMEM((chans, seqs), BF16),
            pltpu.VMEM((chans // DH, seqs, 128), BF16),
            pltpu.VMEM((chans, seqs), BF16),
            pltpu.VMEM((chans, seqs), F32),
            pltpu.VMEM((chans, seqs), BF16),
            pltpu.VMEM((chans // 128, seqs * mine, 128), F32),
            pltpu.VMEM((seqs, lanes), F32),
        ],
        compiler_params=pltpu.CompilerParams(
            vmem_limit_bytes=24 * 2**20
        ),
        cost_estimate=pl.CostEstimate(
            flops=16_000_000_000, bytes_accessed=4 * 2**20, transcendentals=9_000_000
        ),
        name="attend",
    )(
        own_amino,
        block,
        *bundles,
        shift,
        row(gain),
        row(bias),
        row(final_bias),
        row(gain2),
        row(bias2),
        keep.reshape(seqs, 1),
        keep.reshape(1, seqs),
        right_weight,
        left_weight,
    )

    swap = []
    for z in range(nz):
        for rest in range(nx * ny):
            for h in range(n_head):
                swap.append(
                    ((z * nx * ny + rest) * n_head + h, (h * nx * ny + rest) * n_head + z)
                )
    left = lax.ppermute(left, ("dap", "head"), swap)

    def shifted(value, axis, by):
        pairs = []
        for z in range(nz):
            for x in range(nx):
                for y in range(ny):
                    to = [z, x, y]
                    to[axis] = (to[axis] + by) % (nz, nx, ny)[axis]
                    pairs.append(((z * nx + x) * ny + y, (to[0] * nx + to[1]) * ny + to[2]))
        return lax.ppermute(value, "dap", pairs)

    other = shifted(right, 2, 1)

    def first_stage(value, axis):
        return [value] + [shifted(value, axis, -step) for step in STEPS[1:]]

    def second_stage(value, axis):
        from_left, from_right = shifted(value, axis, 1), shifted(value, axis, -1)
        return value, from_left, from_right

    colours = [jnp.stack([right[part], other[part]]) for part in range(2)]
    parts = first_stage(colours[0], 1) + first_stage(colours[1], 0)
    shape = (len(STEPS) * ny, *parts[0].shape[1:])
    mids = pl.pallas_call(
        join_kernel,
        in_specs=[pl.BlockSpec(memory_space=pltpu.VMEM)] * len(parts),
        out_specs=[pl.BlockSpec(memory_space=pltpu.VMEM)] * 2,
        out_shape=[jax.ShapeDtypeStruct(shape, BF16)] * 2,
        compiler_params=pltpu.CompilerParams(vmem_limit_bytes=4 * 2**20),
        cost_estimate=pl.CostEstimate(
            flops=2_000_000, bytes_accessed=2 * 2**20, transcendentals=0
        ),
        name="join",
    )(*parts)
    (*mids, left, rows) = lax.optimization_barrier((*mids, left, rows))
    z_pieces = second_stage(mids[0], 0)
    x_pieces = second_stage(mids[1], 1)
    z_pieces = (*z_pieces, shifted(z_pieces[1], 0, 1))
    x_pieces = (*x_pieces, shifted(x_pieces[1], 1, 1))

    left = lax.all_gather(left, "head", axis=0, tiled=True)
    i_rows = mine * n_head
    left = jnp.swapaxes(left, 0, 1).reshape(CO * i_rows, seqs)

    back = lax.all_to_all(
        rows.reshape(n_dap * n_head, seqs * mine // (n_dap * n_head), chans),
        ("dap", "head"),
        split_axis=0,
        concat_axis=0,
        tiled=True,
    )
    own = own_seqs // n_head
    total = jnp.sum(homolog).astype(F32)
    row_keep = lax.dynamic_slice_in_dim(amino, dap_id * i_rows, i_rows).astype(F32)
    col_keep = lax.dynamic_slice_in_dim(amino, head_id * col_width, col_width).astype(F32)
    norm = jnp.maximum(
        total * row_keep[None, :, None] * col_keep.reshape(n_dap, 1, mine), 1.0
    )
    inverse = (1.0 / norm).reshape(n_dap * i_rows, mine)
    places = []
    for dz in STEPS:
        for dx in STEPS:
            for dy in range(ny):
                at_z, at_x, at_y = (zi + dz) % nz, (xi + dx) % nx, (yi + dy) % ny
                places.append((at_x * ny + at_y) * nz + at_z)
    pieces = (*z_pieces, *x_pieces)
    pair, alignment = pl.pallas_call(
        pair_kernel,
        in_specs=[
            pl.BlockSpec(memory_space=pltpu.SMEM),
            *[pl.BlockSpec(memory_space=pltpu.VMEM)] * (5 + len(pieces)),
        ],
        out_specs=[pl.BlockSpec(memory_space=pltpu.VMEM)] * 2,
        out_shape=[
            jax.ShapeDtypeStruct((i_rows, col_width, depth), F32),
            jax.ShapeDtypeStruct((own, residues, chans), BF16),
        ],
        scratch_shapes=[
            pltpu.VMEM((n_dap * i_rows, CO * lanes), BF16),
            pltpu.VMEM((CO * lanes, mine * depth), BF16),
        ],
        compiler_params=pltpu.CompilerParams(vmem_limit_bytes=18 * 2**20),
        cost_estimate=pl.CostEstimate(
            flops=5_000_000_000, bytes_accessed=10 * 2**20, transcendentals=0
        ),
        name="pair",
    )(
        jnp.stack(places).astype(jnp.int32),
        left,
        pair_bias.reshape(1, depth),
        inverse,
        back,
        pair_weight,
        *pieces,
    )
    return alignment, pair


def solution(mesh):
    return jax.shard_map(
        per_device,
        mesh=mesh,
        in_specs=(
            P("dap", None, None),
            P(),
            P(),
            P(),
            P(),
            P(None, None, "head"),
            P("head"),
            P("head", None),
            P(),
            P(),
            P(),
            P(),
            P(),
            P(),
        ),
        out_specs=(P(("dap", "head"), None, None), P("dap", "head", None)),
        check_vma=False,
    )
```

time: 170 us -> 124 us (0.73)
  the two profiles are of different devices: /device:TPU:11 before, /device:TPU:1 now
where the time goes in v1:
time: 124 us; the launch traced here: 123 us
  starting transfers between devices  44.8 us (36%)
  waiting for transfers between devices  32.1 us (26%)
  Pallas kernels  24.9 us (20%)
  blocking collectives  12.7 us (10%)
  local copies, waits for them, and re-layouts  4.27 us (3%)
  other arithmetic  2.7 us (2%)
  between operations  1.81 us (1%)
    pallas_call x1, Pallas kernels, per_device(): pl.pallas_call(attend_kernel, in_specs=[pl.BlockSpec(memory_space=pltpu.S...  15.6 us
    all_to_all x1, waiting for transfers between devices, per_device(): lax.all_to_all(block, 'dap', split_axis=0, concat_axis=0, tiled=True)  15.4 us
    all_to_all x1, starting transfers between devices, per_device(): lax.all_to_all(rows.reshape(n_dap * n_head, seqs * mine // (n_dap * n_hea...  14.7 us
    ppermute x13, waiting for transfers between devices, shifted(): return lax.ppermute(value, 'dap', pairs)  12.8 us
    all_gather x1, blocking collectives, per_device(): left = lax.all_gather(left, 'head', axis=0, tiled=True)  12.7 us
    ppermute x13, starting transfers between devices, shifted(): return lax.ppermute(value, 'dap', pairs)  11.1 us
    pallas_call x1, Pallas kernels, per_device(): pl.pallas_call(pair_kernel, in_specs=[pl.BlockSpec(memory_space=pltpu.SME...  9.23 us
    all_to_all x1, starting transfers between devices, per_device(): lax.all_to_all(block, 'dap', split_axis=0, concat_axis=0, tiled=True)  8.58 us
  transfers between devices with their start and end apart: 19, of which 7 were waited for; matrix products, arithmetic and copies ran while one was open for 4% of the time, Pallas kernels for 0%

profile of v1, /device:TPU:1, one launch (start us, length us, event | category | flops | bytes accessed | tf_op | source)
XLA Modules:
  0.0 123.3 jit_solution(9990217770663939007)
XLA Ops:
  0.6 0.7 fusion.16
  1.3 0.9 pad_maximum_fusion.w0_ref
  2.2 4.4 %collective-permute-start.2 = (bf16[336,256]{1,0:T(8,128)(2,1)S(1)}, bf16[336,256]{1,0:T(8,128)(2,1)S(1)}, u32[]{:S(2)}, u32[]{:S(2)}) collective-permute-start(bf16[336,256]{1,0:T(8,128)(2,1)S(1)} %pad_maximum_fusion.w0_ref), channel_id=1, source_target_pairs={{0,3},{1,2},{2,1},{3,0},{4,7},{5,6},{6,5},{7,4},{8,11},{9,10},{10,... | collective-permute-start | bytes 516104 | tf_op jit(solution)/shard_map/ppermute | solution.py:282
  6.6 0.0 collective-permute-start.1
  6.6 0.5 collective-permute-start
  7.1 1.3 %constant_dynamic-slice_fusion = bf16[16,128,256]{2,1,0:T(8,128)(2,1)S(1)} fusion(bf16[16,512,256]{2,1,0:T(8,128)(2,1)} %param.16, s32[]{:T(128)S(6)} %select_n.255), kind=kLoop, calls=%fused_computation.45 | loop fusion | bytes 2097156 | tf_op jit(solution)/shard_map/dynamic_slice | solution.py:289
  8.4 0.0 copy-start.1
  8.4 0.0 copy-start.2
  8.5 0.0 copy-start.3
  8.5 0.0 copy-start.4
  8.5 0.0 copy-start.5
  8.5 0.6 copy.30
  9.1 1.0 copy.25
  10.1 8.6 %all-to-all-start = ((bf16[32,64,256]{2,1,0:T(8,128)(2,1)}), bf16[32,64,256]{2,1,0:T(8,128)(2,1)S(1)}, u32[]{:S(2)}, u32[]{:S(2)}) async-start(bf16[32,64,256]{2,1,0:T(8,128)(2,1)} %bitcast.34), calls=%async_computation | async-start | bytes 2097152 | tf_op jit(solution)/shard_map/all_to_all | solution.py:292
  18.8 0.7 fusion.24
  19.5 0.1 mul.174
  19.6 0.1 mul.175
  19.7 0.1 copy.26
  19.8 0.2 copy.28.keep_col_ref
  20.0 0.1 dynamic_slice.12.amino_ref
  20.1 0.0 collective-permute-done.2.w3_ref
  20.1 0.0 collective-permute-done.w1_ref
  20.2 0.1 add.462.shift_ref
  20.3 15.4 %all-to-all-done.x_ref = bf16[32,64,256]{2,1,0:T(8,128)(2,1)S(1)} async-done(((bf16[32,64,256]{2,1,0:T(8,128)(2,1)}), bf16[32,64,256]{2,1,0:T(8,128)(2,1)S(1)}, u32[]{:S(2)}, u32[]{:S(2)}) %all-to-all-start) | async-done | bytes 1048608 | tf_op jit(solution)/shard_map/all_to_all | solution.py:292
  35.7 15.6 %attend.1 = (bf16[2048,256]{1,0:T(8,128)(2,1)}, bf16[4,32,512]{2,1,0:T(8,128)(2,1)S(1)}, bf16[2,256,128]{2,1,0:T(8,128)(2,1)S(1)}) custom-call(s32[4]{0:T(128)S(1)} %dynamic_slice.12.amino_ref, bf16[32,64,256]{2,1,0:T(8,128)(2,1)S(1)} %all-to-all-done.x_ref, bf16[336,256]{1,0:T(8,128)(2,1)S(1)} %pad_maximum_fusion.w0_ref, ...), custom_call_target="tpu_custom_call" | custom-call | flops 16000000000 | bytes 4194304 | tf_op jit(solution)/shard_map/attend/pallas_call | solution.py:306
  51.3 0.0 collective-permute-start.3
  51.4 3.8 %collective-permute-done.3 = bf16[2,256,128]{2,1,0:T(8,128)(2,1)S(1)} collective-permute-done((bf16[2,256,128]{2,1,0:T(8,128)(2,1)S(1)}, bf16[2,256,128]{2,1,0:T(8,128)(2,1)S(1)}, u32[]{:S(2)}, u32[]{:S(2)}) %collective-permute-start.3) | collective-permute-done | bytes 131104 | tf_op jit(solution)/shard_map/ppermute | solution.py:378
  55.2 0.1 collective-permute-start.6
  55.3 2.8 %collective-permute-start.5 = (bf16[2,256,128]{2,1,0:T(8,128)(2,1)S(1)}, bf16[2,256,128]{2,1,0:T(8,128)(2,1)S(1)}, u32[]{:S(2)}, u32[]{:S(2)}) collective-permute-start(bf16[2,256,128]{2,1,0:T(8,128)(2,1)S(1)} %pad_maximum_fusion.1.refs_0_), channel_id=1, source_target_pairs={{0,24},{4,28},{8,0},{12,4},{16,8},{20,12},{24,16},{28,20},{32,56},... | collective-permute-start | bytes 393224 | tf_op jit(solution)/shard_map/ppermute | solution.py:378
  58.1 0.0 collective-permute-start.4
  58.1 0.4 collective-permute-start.9
  58.6 1.4 %collective-permute-start.8 = (bf16[2,256,128]{2,1,0:T(8,128)(2,1)S(1)}, bf16[2,256,128]{2,1,0:T(8,128)(2,1)S(1)}, u32[]{:S(2)}, u32[]{:S(2)}) collective-permute-start(bf16[2,256,128]{2,1,0:T(8,128)(2,1)S(1)} %pad_maximum_fusion.2.refs_4_), channel_id=1, source_target_pairs={{0,96},{4,100},{8,104},{12,108},{16,112},{20,116},{24,120},{28,124... | collective-permute-start | bytes 393224 | tf_op jit(solution)/shard_map/ppermute | solution.py:378
  60.0 0.6 collective-permute-done.6.refs_3_
  60.6 0.0 collective-permute-start.7
  60.6 0.8 collective-permute-done.5.refs_2_
  61.4 5.6 %collective-permute-start.10 = (bf16[4,32,512]{2,1,0:T(8,128)(2,1)S(1)}, bf16[4,32,512]{2,1,0:T(8,128)(2,1)S(1)}, u32[]{:S(2)}, u32[]{:S(2)}) collective-permute-start(bf16[4,32,512]{2,1,0:T(8,128)(2,1)S(1)} %get-tuple-element.28), channel_id=1, source_target_pairs={{0,0},{1,32},{2,64},{3,96},{4,4},{5,36},{6,68},{7,100},{8,8},{9,40... | collective-permute-start | bytes 393224 | tf_op jit(solution)/shard_map/ppermute | solution.py:368
  67.1 0.0 collective-permute-done.4.refs_1_
  67.1 0.0 collective-permute-done.8.refs_6_
  67.1 0.0 collective-permute-done.7.refs_5_
  67.1 0.1 join.1
  67.2 3.9 %collective-permute-done.10 = bf16[4,32,512]{2,1,0:T(8,128)(2,1)S(1)} collective-permute-done((bf16[4,32,512]{2,1,0:T(8,128)(2,1)S(1)}, bf16[4,32,512]{2,1,0:T(8,128)(2,1)S(1)}, u32[]{:S(2)}, u32[]{:S(2)}) %collective-permute-start.10) | collective-permute-done | bytes 131104 | tf_op jit(solution)/shard_map/ppermute | solution.py:368
  71.1 0.0 collective-permute-start.11
  71.1 0.3 collective-permute-start.14
  71.4 14.7 %all-to-all-start.1 = ((bf16[128,16,256]{2,1,0:T(8,128)(2,1)}), bf16[128,16,256]{2,1,0:T(8,128)(2,1)S(1)}, u32[]{:S(2)}, u32[]{:S(2)}) async-start(bf16[128,16,256]{2,1,0:T(8,128)(2,1)} %bitcast.61), calls=%async_computation.1 | async-start | bytes 2097152 | tf_op jit(solution)/shard_map/all_to_all | solution.py:413
  86.1 3.3 %collective-permute-start.12 = (bf16[8,256,128]{2,1,0:T(8,128)(2,1)S(1)}, bf16[8,256,128]{2,1,0:T(8,128)(2,1)}, u32[]{:S(2)}, u32[]{:S(2)}) collective-permute-start(bf16[8,256,128]{2,1,0:T(8,128)(2,1)S(1)} %get-tuple-element.32.z0_ref), channel_id=1, source_target_pairs={{0,96},{4,100},{8,104},{12,108},{16,112},{20,116},{24,120},{28,124... | collective-permute-start | bytes 1572872 | tf_op jit(solution)/shard_map/ppermute | solution.py:378
  89.4 2.4 %collective-permute-start.15 = (bf16[8,256,128]{2,1,0:T(8,128)(2,1)S(1)}, bf16[8,256,128]{2,1,0:T(8,128)(2,1)}, u32[]{:S(2)}, u32[]{:S(2)}) collective-permute-start(bf16[8,256,128]{2,1,0:T(8,128)(2,1)S(1)} %get-tuple-element.33.x0_ref), channel_id=1, source_target_pairs={{0,24},{4,28},{8,0},{12,4},{16,8},{20,12},{24,16},{28,20},{32,56},... | collective-permute-start | bytes 1572872 | tf_op jit(solution)/shard_map/ppermute | solution.py:378
  91.8 0.0 collective-permute-done.11.z1_ref
  91.8 0.0 collective-permute-start.13
  91.9 0.0 collective-permute-done.14.x1_ref
  91.9 0.3 collective-permute-start.16
  92.9 0.1 convert_multiply_fusion
  93.0 0.1 mul.186
  93.1 0.1 dynamic-slice_convert_fusion
  93.2 0.1 mul.188
  93.3 0.1 fusion.1.inverse_ref
  93.4 0.1 stack.174.place_ref
  93.5 12.7 %all_gather.3 = bf16[16,32,512]{2,1,0:T(8,128)(2,1)S(1)} all-gather(bf16[4,32,512]{2,1,0:T(8,128)(2,1)S(1)} %collective-permute-done.10), channel_id=1, replica_groups=mesh['dap'=32,'head'=4] {'head'}, dimensions={0}, use_global_device_ids=true | all-gather | bytes 655360 | tf_op jit(solution)/shard_map/all_gather | solution.py:409
  106.2 0.3 copy.29
  106.5 3.9 %collective-permute-done.12.z2_ref = bf16[8,256,128]{2,1,0:T(8,128)(2,1)} collective-permute-done((bf16[8,256,128]{2,1,0:T(8,128)(2,1)S(1)}, bf16[8,256,128]{2,1,0:T(8,128)(2,1)}, u32[]{:S(2)}, u32[]{:S(2)}) %collective-permute-start.12) | collective-permute-done | bytes 524320 | tf_op jit(solution)/shard_map/ppermute | solution.py:378
  110.4 0.0 collective-permute-done.15.x2_ref
  110.4 0.0 all-to-all-done.1.back_ref
  110.4 3.7 %collective-permute-done.13.z3_ref = bf16[8,256,128]{2,1,0:T(8,128)(2,1)} collective-permute-done((bf16[8,256,128]{2,1,0:T(8,128)(2,1)}, bf16[8,256,128]{2,1,0:T(8,128)(2,1)}, u32[]{:S(2)}, u32[]{:S(2)}) %collective-permute-start.13) | collective-permute-done | bytes 524320 | tf_op jit(solution)/shard_map/ppermute | solution.py:378
  114.1 0.0 collective-permute-done.16.x3_ref
  114.1 9.2 %pair.1 = (f32[16,128,128]{2,1,0:T(8,128)}, bf16[4,512,256]{2,1,0:T(8,128)(2,1)}) custom-call(s32[32]{0:T(128)S(1)} %stack.174.place_ref, bf16[512,512]{1,0:T(8,128)(2,1)S(1)} %bitcast.81, f32[1,128]{1,0:T(1,128)S(1)} %bitcast.89, f32[512,4]{1,0:T(8,128)S(1)} %fusion.1.inverse_ref, bf16[128,16,256]{2,1,0:T(8,128)(2,1)S(1)} %all-to-all-done.1.back_ref, ...), custom_call_target="tpu_custom_call" | custom-call | flops 5000000000 | bytes 10485760 | tf_op jit(solution)/shard_map/pair/pallas_call | solution.py:435
  (31 shorter events, 0.2 us)
Async XLA Ops:
  2.2 17.8 %collective-permute-start.2 = (bf16[336,256]{1,0:T(8,128)(2,1)S(1)}, bf16[336,256]{1,0:T(8,128)(2,1)S(1)}, u32[]{:S(2)}, u32[]{:S(2)}) collective-permute-start(bf16[336,256]{1,0:T(8,128)(2,1)S(1)} %pad_maximum_fusion.w0_ref), channel_id=1, source_target_pairs={{0,3},{1,2},{2,1},{3,0},{4,7},{5,6},{6,5},{7,4},{8,11},{9,10},{10,... | collective-permute-start | bytes 516104 | tf_op jit(solution)/shard_map/ppermute | solution.py:282
  6.6 13.5 %collective-permute-start.1 = (bf16[336,256]{1,0:T(8,128)(2,1)S(1)}, bf16[336,256]{1,0:T(8,128)(2,1)S(1)}, u32[]{:S(2)}, u32[]{:S(2)}) collective-permute-start(bf16[336,256]{1,0:T(8,128)(2,1)S(1)} %pad_maximum_fusion.w0_ref), channel_id=1, source_target_pairs={{0,2},{1,3},{2,0},{3,1},{4,6},{5,7},{6,4},{7,5},{8,10},{9,11},{10,... | collective-permute-start | bytes 516104 | tf_op jit(solution)/shard_map/ppermute | solution.py:282
  6.6 13.5 %collective-permute-start = (bf16[336,256]{1,0:T(8,128)(2,1)S(1)}, bf16[336,256]{1,0:T(8,128)(2,1)S(1)}, u32[]{:S(2)}, u32[]{:S(2)}) collective-permute-start(bf16[336,256]{1,0:T(8,128)(2,1)S(1)} %pad_maximum_fusion.w0_ref), channel_id=1, source_target_pairs={{0,1},{1,0},{2,3},{3,2},{4,5},{5,4},{6,7},{7,6},{8,9},{9,8},{10,11... | collective-permute-start | bytes 516104 | tf_op jit(solution)/shard_map/ppermute | solution.py:282
  7.1 11.7 %copy-start.8 = (s32[512]{0:T(512)S(1)}, s32[512]{0:T(512)}, u32[]{:S(2)}) copy-start(s32[512]{0:T(512)} %param.17) | copy-start | bytes 6148
  7.1 12.4 %copy-start.7 = (bf16[256,2,32]{0,2,1:T(8,128)(2,1)S(1)}, bf16[256,2,32]{0,2,1:T(8,128)(2,1)}, u32[]{:S(2)}) copy-start(bf16[256,2,32]{0,2,1:T(8,128)(2,1)} %param.27) | copy-start | bytes 98308
  7.1 12.8 %copy-start.9 = (s32[512]{0:T(512)S(1)}, s32[512]{0:T(512)}, u32[]{:S(2)}) copy-start(s32[512]{0:T(512)} %param.18) | copy-start | bytes 6148
  8.4 27.3 %copy-start.1 = (f32[256]{0:T(256)S(1)}, f32[256]{0:T(256)}, u32[]{:S(2)}) copy-start(f32[256]{0:T(256)} %param.19) | copy-start | bytes 3076
  8.4 27.2 %copy-start.2 = (f32[256]{0:T(256)S(1)}, f32[256]{0:T(256)}, u32[]{:S(2)}) copy-start(f32[256]{0:T(256)} %param.20) | copy-start | bytes 3076
  8.5 27.2 %copy-start.3 = (f32[256]{0:T(256)S(1)}, f32[256]{0:T(256)}, u32[]{:S(2)}) copy-start(f32[256]{0:T(256)} %param.24) | copy-start | bytes 3076
  8.5 27.2 %copy-start.4 = (f32[256]{0:T(256)S(1)}, f32[256]{0:T(256)}, u32[]{:S(2)}) copy-start(f32[256]{0:T(256)} %param.25) | copy-start | bytes 3076
  8.5 27.2 %copy-start.5 = (f32[256]{0:T(256)S(1)}, f32[256]{0:T(256)}, u32[]{:S(2)}) copy-start(f32[256]{0:T(256)} %param.26) | copy-start | bytes 3076
  10.1 25.6 %all-to-all-start = ((bf16[32,64,256]{2,1,0:T(8,128)(2,1)}), bf16[32,64,256]{2,1,0:T(8,128)(2,1)S(1)}, u32[]{:S(2)}, u32[]{:S(2)}) async-start(bf16[32,64,256]{2,1,0:T(8,128)(2,1)} %bitcast.34), calls=%async_computation | async-start | bytes 2097152 | tf_op jit(solution)/shard_map/all_to_all | solution.py:292
  51.3 62.8 %copy-start = (f32[1024,128]{1,0:T(8,128)S(1)}, f32[1024,128]{1,0:T(8,128)}, u32[]{:S(2)}) copy-start(f32[1024,128]{1,0:T(8,128)} %compact_ref.1) | copy-start | bytes 1572868
  51.3 62.8 %copy-start.6 = (f32[128]{0:T(128)S(1)}, f32[128]{0:T(128)}, u32[]{:S(2)}) copy-start(f32[128]{0:T(128)} %param.29) | copy-start | bytes 1540
  51.3 3.8 %collective-permute-start.3 = (bf16[2,256,128]{2,1,0:T(8,128)(2,1)S(1)}, bf16[2,256,128]{2,1,0:T(8,128)(2,1)S(1)}, u32[]{:S(2)}, u32[]{:S(2)}) collective-permute-start(bf16[2,256,128]{2,1,0:T(8,128)(2,1)S(1)} %get-tuple-element.25), channel_id=1, source_target_pairs={{0,4},{4,0},{8,12},{12,8},{16,20},{20,16},{24,28},{28,24},{32,36},... | collective-permute-start | bytes 393224 | tf_op jit(solution)/shard_map/ppermute | solution.py:378
  55.2 5.4 %collective-permute-start.6 = (bf16[2,256,128]{2,1,0:T(8,128)(2,1)S(1)}, bf16[2,256,128]{2,1,0:T(8,128)(2,1)S(1)}, u32[]{:S(2)}, u32[]{:S(2)}) collective-permute-start(bf16[2,256,128]{2,1,0:T(8,128)(2,1)S(1)} %pad_maximum_fusion.1.refs_0_), channel_id=1, source_target_pairs={{0,16},{4,20},{8,24},{12,28},{16,0},{20,4},{24,8},{28,12},{32,48},... | collective-permute-start | bytes 393224 | tf_op jit(solution)/shard_map/ppermute | solution.py:378
  55.3 6.2 %collective-permute-start.5 = (bf16[2,256,128]{2,1,0:T(8,128)(2,1)S(1)}, bf16[2,256,128]{2,1,0:T(8,128)(2,1)S(1)}, u32[]{:S(2)}, u32[]{:S(2)}) collective-permute-start(bf16[2,256,128]{2,1,0:T(8,128)(2,1)S(1)} %pad_maximum_fusion.1.refs_0_), channel_id=1, source_target_pairs={{0,24},{4,28},{8,0},{12,4},{16,8},{20,12},{24,16},{28,20},{32,56},... | collective-permute-start | bytes 393224 | tf_op jit(solution)/shard_map/ppermute | solution.py:378
  58.1 9.0 %collective-permute-start.4 = (bf16[2,256,128]{2,1,0:T(8,128)(2,1)S(1)}, bf16[2,256,128]{2,1,0:T(8,128)(2,1)S(1)}, u32[]{:S(2)}, u32[]{:S(2)}) collective-permute-start(bf16[2,256,128]{2,1,0:T(8,128)(2,1)S(1)} %pad_maximum_fusion.1.refs_0_), channel_id=1, source_target_pairs={{0,8},{4,12},{8,16},{12,20},{16,24},{20,28},{24,0},{28,4},{32,40},... | collective-permute-start | bytes 393224 | tf_op jit(solution)/shard_map/ppermute | solution.py:378
  58.1 9.0 %collective-permute-start.9 = (bf16[2,256,128]{2,1,0:T(8,128)(2,1)S(1)}, bf16[2,256,128]{2,1,0:T(8,128)(2,1)S(1)}, u32[]{:S(2)}, u32[]{:S(2)}) collective-permute-start(bf16[2,256,128]{2,1,0:T(8,128)(2,1)S(1)} %pad_maximum_fusion.2.refs_4_), channel_id=1, source_target_pairs={{0,64},{4,68},{8,72},{12,76},{16,80},{20,84},{24,88},{28,92},{32,9... | collective-permute-start | bytes 393224 | tf_op jit(solution)/shard_map/ppermute | solution.py:378
  58.6 8.6 %collective-permute-start.8 = (bf16[2,256,128]{2,1,0:T(8,128)(2,1)S(1)}, bf16[2,256,128]{2,1,0:T(8,128)(2,1)S(1)}, u32[]{:S(2)}, u32[]{:S(2)}) collective-permute-start(bf16[2,256,128]{2,1,0:T(8,128)(2,1)S(1)} %pad_maximum_fusion.2.refs_4_), channel_id=1, source_target_pairs={{0,96},{4,100},{8,104},{12,108},{16,112},{20,116},{24,120},{28,124... | collective-permute-start | bytes 393224 | tf_op jit(solution)/shard_map/ppermute | solution.py:378
  60.6 6.5 %collective-permute-start.7 = (bf16[2,256,128]{2,1,0:T(8,128)(2,1)S(1)}, bf16[2,256,128]{2,1,0:T(8,128)(2,1)S(1)}, u32[]{:S(2)}, u32[]{:S(2)}) collective-permute-start(bf16[2,256,128]{2,1,0:T(8,128)(2,1)S(1)} %pad_maximum_fusion.2.refs_4_), channel_id=1, source_target_pairs={{0,32},{4,36},{8,40},{12,44},{16,48},{20,52},{24,56},{28,60},{32,6... | collective-permute-start | bytes 393224 | tf_op jit(solution)/shard_map/ppermute | solution.py:378
  61.4 9.7 %collective-permute-start.10 = (bf16[4,32,512]{2,1,0:T(8,128)(2,1)S(1)}, bf16[4,32,512]{2,1,0:T(8,128)(2,1)S(1)}, u32[]{:S(2)}, u32[]{:S(2)}) collective-permute-start(bf16[4,32,512]{2,1,0:T(8,128)(2,1)S(1)} %get-tuple-element.28), channel_id=1, source_target_pairs={{0,0},{1,32},{2,64},{3,96},{4,4},{5,36},{6,68},{7,100},{8,8},{9,40... | collective-permute-start | bytes 393224 | tf_op jit(solution)/shard_map/ppermute | solution.py:368
  71.1 20.7 %collective-permute-start.11 = (bf16[8,256,128]{2,1,0:T(8,128)(2,1)S(1)}, bf16[8,256,128]{2,1,0:T(8,128)(2,1)}, u32[]{:S(2)}, u32[]{:S(2)}) collective-permute-start(bf16[8,256,128]{2,1,0:T(8,128)(2,1)S(1)} %get-tuple-element.32.z0_ref), channel_id=1, source_target_pairs={{0,32},{4,36},{8,40},{12,44},{16,48},{20,52},{24,56},{28,60},{32,6... | collective-permute-start | bytes 1572872 | tf_op jit(solution)/shard_map/ppermute | solution.py:378
  71.1 20.7 %collective-permute-start.14 = (bf16[8,256,128]{2,1,0:T(8,128)(2,1)S(1)}, bf16[8,256,128]{2,1,0:T(8,128)(2,1)}, u32[]{:S(2)}, u32[]{:S(2)}) collective-permute-start(bf16[8,256,128]{2,1,0:T(8,128)(2,1)S(1)} %get-tuple-element.33.x0_ref), channel_id=1, source_target_pairs={{0,8},{4,12},{8,16},{12,20},{16,24},{20,28},{24,0},{28,4},{32,40},... | collective-permute-start | bytes 1572872 | tf_op jit(solution)/shard_map/ppermute | solution.py:378
  71.4 39.0 %all-to-all-start.1 = ((bf16[128,16,256]{2,1,0:T(8,128)(2,1)}), bf16[128,16,256]{2,1,0:T(8,128)(2,1)S(1)}, u32[]{:S(2)}, u32[]{:S(2)}) async-start(bf16[128,16,256]{2,1,0:T(8,128)(2,1)} %bitcast.61), calls=%async_computation.1 | async-start | bytes 2097152 | tf_op jit(solution)/shard_map/all_to_all | solution.py:413
  86.1 24.3 %collective-permute-start.12 = (bf16[8,256,128]{2,1,0:T(8,128)(2,1)S(1)}, bf16[8,256,128]{2,1,0:T(8,128)(2,1)}, u32[]{:S(2)}, u32[]{:S(2)}) collective-permute-start(bf16[8,256,128]{2,1,0:T(8,128)(2,1)S(1)} %get-tuple-element.32.z0_ref), channel_id=1, source_target_pairs={{0,96},{4,100},{8,104},{12,108},{16,112},{20,116},{24,120},{28,124... | collective-permute-start | bytes 1572872 | tf_op jit(solution)/shard_map/ppermute | solution.py:378
  89.4 21.0 %collective-permute-start.15 = (bf16[8,256,128]{2,1,0:T(8,128)(2,1)S(1)}, bf16[8,256,128]{2,1,0:T(8,128)(2,1)}, u32[]{:S(2)}, u32[]{:S(2)}) collective-permute-start(bf16[8,256,128]{2,1,0:T(8,128)(2,1)S(1)} %get-tuple-element.33.x0_ref), channel_id=1, source_target_pairs={{0,24},{4,28},{8,0},{12,4},{16,8},{20,12},{24,16},{28,20},{32,56},... | collective-permute-start | bytes 1572872 | tf_op jit(solution)/shard_map/ppermute | solution.py:378
  91.8 22.2 %collective-permute-start.13 = (bf16[8,256,128]{2,1,0:T(8,128)(2,1)}, bf16[8,256,128]{2,1,0:T(8,128)(2,1)}, u32[]{:S(2)}, u32[]{:S(2)}) collective-permute-start(bf16[8,256,128]{2,1,0:T(8,128)(2,1)} %collective-permute-done.11.z1_ref), channel_id=1, source_target_pairs={{0,32},{4,36},{8,40},{12,44},{16,48},{20,52},{24,56},{28,60},{32,6... | collective-permute-start | bytes 1572872 | tf_op jit(solution)/shard_map/ppermute | solution.py:378
  91.9 22.2 %collective-permute-start.16 = (bf16[8,256,128]{2,1,0:T(8,128)(2,1)}, bf16[8,256,128]{2,1,0:T(8,128)(2,1)}, u32[]{:S(2)}, u32[]{:S(2)}) collective-permute-start(bf16[8,256,128]{2,1,0:T(8,128)(2,1)} %collective-permute-done.14.x1_ref), channel_id=1, source_target_pairs={{0,8},{4,12},{8,16},{12,20},{16,24},{20,28},{24,0},{28,4},{32,40},... | collective-permute-start | bytes 1572872 | tf_op jit(solution)/shard_map/ppermute | solution.py:378

commit v2 on v1

--- a/solution.py
+++ b/solution.py
@@ -157,41 +157,81 @@
             out_ref[index * count : (index + 1) * count] = piece[...]
 
 
-def pair_kernel(
+def project(slots, groups, z_refs, x_refs, left_ref, bias_ref, inverse_ref, compact_ref,
+            place_ref, mid_ref, weight_ref, store):
+    lanes = z_refs[0].shape[2]
+    depth = bias_ref.shape[1]
+    inner = lanes // CO
+    rows = left_ref.shape[0] // CO
+    nothing = jnp.zeros((CO, depth), BF16)
+    for c in range(CO):
+        block = compact_ref[c * CO : (c + 1) * CO, :].astype(BF16)
+        for k in range(inner):
+            at = (c * inner + k) * CO
+            for j in range(inner):
+                weight_ref[at : at + CO, j * depth : (j + 1) * depth] = (
+                    block if j == k else nothing
+                )
+
+    def source(dz, dx, dy):
+        return jnp.concatenate([z_refs[dz][dx * 2 + dy], x_refs[dx][dz * 2 + dy]], 0)
+
+    left = left_ref[...]
+    size = len(slots) // groups
+    for group in range(groups):
+        batch = slots[group * size : (group + 1) * size]
+        pieces = jnp.concatenate([source(*slot) for slot in batch], 1)
+        outer = jnp.dot(left, pieces, preferred_element_type=F32).astype(BF16)
+        for q in range(size):
+            at = (group * size + q) * rows
+            for c in range(CO):
+                mid_ref[at : at + rows, c * lanes : (c + 1) * lanes] = outer[
+                    c * rows : (c + 1) * rows, q * lanes : (q + 1) * lanes
+                ]
+    for k in range(0, inner, 2):
+        total = jnp.dot(
+            mid_ref[...],
+            weight_ref[:, k * depth : (k + 2) * depth],
+            preferred_element_type=F32,
+        )
+        for n, (dz, dx, dy) in enumerate(slots):
+            place = place_ref[(dz * 4 + dx) * 2 + dy]
+            inverse = inverse_ref[pl.ds(pl.multiple_of(place * rows, rows), rows), :]
+            for j in range(2):
+                value = total[n * rows : (n + 1) * rows, j * depth : (j + 1) * depth]
+                value = (value + bias_ref[...]) * inverse[:, k + j : k + j + 1]
+                store(n, place, k + j, value)
+
+
+EARLY = tuple((dz, dx, dy) for dz in range(3) for dx in range(3) for dy in range(2))
+LATE = tuple(
+    (dz, dx, dy) for dz in range(4) for dx in range(4) for dy in range(2) if 3 in (dz, dx)
+)
+
+
+def early_kernel(
     place_ref,
     left_ref,
     bias_ref,
     inverse_ref,
+    compact_ref,
     back_ref,
-    compact_ref,
     z0_ref,
     z1_ref,
     z2_ref,
-    z3_ref,
     x0_ref,
     x1_ref,
     x2_ref,
-    x3_ref,
-    out_ref,
+    part_ref,
     aligned_ref,
     mid_ref,
     weight_ref,
 ):
-    rows = out_ref.shape[0]
-    lanes = z0_ref.shape[2]
-
-    def source(dz, dx, dy):
-        first = (z0_ref, z1_ref, z2_ref, z3_ref)[dz][dx * 2 + dy]
-        second = (x0_ref, x1_ref, x2_ref, x3_ref)[dx][dz * 2 + dy]
-        return jnp.concatenate([first, second], 0)
-
     low = lax.broadcasted_iota(jnp.int32, (8, back_ref.shape[2]), 0) < 4
 
     def arrange(index, _):
         head, xy = index // 8, index % 8
-        blocks = [
-            back_ref[(z * 8 + xy) * 4 + head].astype(F32) for z in range(4)
-        ]
+        blocks = [back_ref[(z * 8 + xy) * 4 + head].astype(F32) for z in range(4)]
         for upper in range(2):
             tiles = [b[upper * 8 : upper * 8 + 8] for b in blocks]
             turned = [pltpu.roll(t, 4, 0) for t in tiles]
@@ -205,41 +245,53 @@
         return 0
 
     lax.fori_loop(0, back_ref.shape[0] // 4, arrange, 0)
-    depth = bias_ref.shape[1]
-    inner = lanes // CO
-    nothing = jnp.zeros((CO, depth), BF16)
-    for c in range(CO):
-        block = compact_ref[c * CO : (c + 1) * CO, :].astype(BF16)
-        for k in range(inner):
-            at = (c * inner + k) * CO
-            for j in range(inner):
-                weight_ref[at : at + CO, j * depth : (j + 1) * depth] = (
-                    block if j == k else nothing
-                )
-    left = left_ref[...]
-    for dz in range(4):
-        for pair in range(2):
-            slots = [(dz, pair * 2 + q // 2, q % 2) for q in range(4)]
-            pieces = jnp.concatenate([source(*slot) for slot in slots], 1)
-            outer = jnp.dot(left, pieces, preferred_element_type=F32).astype(BF16)
-            for q, (z, x, y) in enumerate(slots):
-                at = pl.multiple_of(place_ref[(z * 4 + x) * 2 + y] * rows, rows)
-                for c in range(CO):
-                    mid_ref[pl.ds(at, rows), c * lanes : (c + 1) * lanes] = outer[
-                        c * rows : (c + 1) * rows, q * lanes : (q + 1) * lanes
-                    ]
-    blocks = mid_ref.shape[0] // rows
-    for k in range(0, inner, 2):
-        total = jnp.dot(
-            mid_ref[...],
-            weight_ref[:, k * depth : (k + 2) * depth],
-            preferred_element_type=F32,
-        )
-        for j in range(2):
-            value = total[:, j * depth : (j + 1) * depth]
-            value = (value + bias_ref[...]) * inverse_ref[:, k + j : k + j + 1]
-            for b in range(blocks):
-                out_ref[:, b * inner + k + j, :] = value[b * rows : (b + 1) * rows]
+    rows = left_ref.shape[0] // CO
+    inner = z0_ref.shape[2] // CO
+
+    def store(n, place, k, value):
+        at = (n * inner + k) * rows
+        part_ref[at : at + rows, :] = value
+
+    project(EARLY, 3, (z0_ref, z1_ref, z2_ref), (x0_ref, x1_ref, x2_ref), left_ref, bias_ref,
+            inverse_ref, compact_ref, place_ref, mid_ref, weight_ref, store)
+
+
+def late_kernel(
+    place_ref,
+    left_ref,
+    bias_ref,
+    inverse_ref,
+    compact_ref,
+    part_ref,
+    z0_ref,
+    z1_ref,
+    z2_ref,
+    z3_ref,
+    x0_ref,
+    x1_ref,
+    x2_ref,
+    x3_ref,
+    out_ref,
+    mid_ref,
+    weight_ref,
+    turn_ref,
+):
+    rows = left_ref.shape[0] // CO
+    inner = z0_ref.shape[2] // CO
+
+    def store(n, place, k, value):
+        at = pl.multiple_of((place * inner + k) * rows, rows)
+        turn_ref[pl.ds(at, rows), :] = value
+
+    project(LATE, 2, (z0_ref, z1_ref, z2_ref, z3_ref), (x0_ref, x1_ref, x2_ref, x3_ref),
+            left_ref, bias_ref, inverse_ref, compact_ref, place_ref, mid_ref, weight_ref, store)
+    block = inner * rows
+    for n, (dz, dx, dy) in enumerate(EARLY):
+        at = pl.multiple_of(place_ref[(dz * 4 + dx) * 2 + dy] * block, block)
+        turn_ref[pl.ds(at, block), :] = part_ref[n * block : (n + 1) * block, :]
+    columns = out_ref.shape[1]
+    for i in range(rows):
+        out_ref[i] = turn_ref[pl.ds(i, columns, stride=rows), :]
 
 
 def whole():
@@ -278,9 +330,18 @@
     offsets = jnp.zeros((16, chans), BF16)
     offsets = offsets.at[:3, :width].set(jnp.stack([first, second, third]).astype(BF16))
     bundle = jnp.concatenate([parts, final, offsets], 0)
-    bundles = [bundle] + [
-        lax.ppermute(bundle, "head", [(h, h ^ flip) for h in range(n_head)])
-        for flip in range(1, n_head)
+    swap_core = [(h, h ^ 1) for h in range(n_head)]
+    across = [
+        (d * n_head + h, (d ^ 1) * n_head + (h ^ 2))
+        for d in range(n_dap)
+        for h in range(n_head)
+    ]
+    far_bundle = lax.ppermute(bundle, ("dap", "head"), across)
+    bundles = [
+        bundle,
+        lax.ppermute(bundle, "head", swap_core),
+        far_bundle,
+        lax.ppermute(far_bundle, "head", swap_core),
     ]
     base = 5 * width
     shift = jnp.stack([b[base : base + 3, :width] for b in bundles]).astype(F32)
@@ -431,36 +492,53 @@
             for dy in range(ny):
                 at_z, at_x, at_y = (zi + dz) % nz, (xi + dx) % nx, (yi + dy) % ny
                 places.append((at_x * ny + at_y) * nz + at_z)
-    pieces = (*z_pieces, *x_pieces)
-    pair, alignment = pl.pallas_call(
-        pair_kernel,
-        in_specs=[
-            pl.BlockSpec(memory_space=pltpu.SMEM),
-            *[pl.BlockSpec(memory_space=pltpu.VMEM)] * (5 + len(pieces)),
-        ],
-        out_specs=[pl.BlockSpec(memory_space=pltpu.VMEM)] * 2,
-        out_shape=[
-            jax.ShapeDtypeStruct((i_rows, col_width, depth), F32),
-            jax.ShapeDtypeStruct((own, residues, chans), BF16),
-        ],
-        scratch_shapes=[
-            pltpu.VMEM((n_dap * i_rows, CO * lanes), BF16),
-            pltpu.VMEM((CO * lanes, mine * depth), BF16),
-        ],
-        compiler_params=pltpu.CompilerParams(vmem_limit_bytes=18 * 2**20),
-        cost_estimate=pl.CostEstimate(
-            flops=5_000_000_000, bytes_accessed=10 * 2**20, transcendentals=0
-        ),
-        name="pair",
-    )(
+    shared = (
         jnp.stack(places).astype(jnp.int32),
         left,
         pair_bias.reshape(1, depth),
         inverse,
-        back,
         pair_weight,
-        *pieces,
     )
+    early, alignment = pl.pallas_call(
+        early_kernel,
+        in_specs=[
+            pl.BlockSpec(memory_space=pltpu.SMEM),
+            *[pl.BlockSpec(memory_space=pltpu.VMEM)] * 11,
+        ],
+        out_specs=[pl.BlockSpec(memory_space=pltpu.VMEM)] * 2,
+        out_shape=[
+            jax.ShapeDtypeStruct((len(EARLY) * mine * i_rows, depth), F32),
+            jax.ShapeDtypeStruct((own, residues, chans), BF16),
+        ],
+        scratch_shapes=[
+            pltpu.VMEM((len(EARLY) * i_rows, CO * lanes), BF16),
+            pltpu.VMEM((CO * lanes, mine * depth), BF16),
+        ],
+        compiler_params=pltpu.CompilerParams(vmem_limit_bytes=18 * 2**20),
+        cost_estimate=pl.CostEstimate(
+            flops=3_000_000_000, bytes_accessed=6 * 2**20, transcendentals=0
+        ),
+        name="early",
+    )(*shared, back, *z_pieces[:3], *x_pieces[:3])
+    pair = pl.pallas_call(
+        late_kernel,
+        in_specs=[
+            pl.BlockSpec(memory_space=pltpu.SMEM),
+            *[pl.BlockSpec(memory_space=pltpu.VMEM)] * 13,
+        ],
+        out_specs=pl.BlockSpec(memory_space=pltpu.VMEM),
+        out_shape=jax.ShapeDtypeStruct((i_rows, col_width, depth), F32),
+        scratch_shapes=[
+            pltpu.VMEM((len(LATE) * i_rows, CO * lanes), BF16),
+            pltpu.VMEM((CO * lanes, mine * depth), BF16),
+            pltpu.VMEM((col_width * i_rows, depth), F32),
+        ],
+        compiler_params=pltpu.CompilerParams(vmem_limit_bytes=18 * 2**20),
+        cost_estimate=pl.CostEstimate(
+            flops=3_000_000_000, bytes_accessed=6 * 2**20, transcendentals=0
+        ),
+        name="late",
+    )(*shared, early, *z_pieces, *x_pieces)
     return alignment, pair
 
 

time: 124 us -> 132 us (1.065)
  the two profiles are of different devices: /device:TPU:1 before, /device:TPU:11 now
where the time goes in v2:
time: 132 us; the launch traced here: 130 us
  starting transfers between devices  46.1 us (35%)
  waiting for transfers between devices  39 us (30%)
  Pallas kernels  27.2 us (21%)
  blocking collectives  8.78 us (7%)
  local copies, waits for them, and re-layouts  4.28 us (3%)
  other arithmetic  2.64 us (2%)
  between operations  1.77 us (1%)
    ppermute x13, waiting for transfers between devices, shifted(): return lax.ppermute(value, 'dap', pairs)  23.2 us
    pallas_call x1, Pallas kernels, per_device(): pl.pallas_call(attend_kernel, in_specs=[pl.BlockSpec(memory_space=pltpu.S...  15.6 us
    ppermute x13, starting transfers between devices, shifted(): return lax.ppermute(value, 'dap', pairs)  13.7 us
    all_to_all x1, starting transfers between devices, per_device(): lax.all_to_all(rows.reshape(n_dap * n_head, seqs * mine // (n_dap * n_hea...  13.4 us
    all_to_all x1, waiting for transfers between devices, per_device(): lax.all_to_all(block, 'dap', split_axis=0, concat_axis=0, tiled=True)  11.2 us
    all_to_all x1, starting transfers between devices, per_device(): lax.all_to_all(block, 'dap', split_axis=0, concat_axis=0, tiled=True)  9.23 us
    all_gather x1, blocking collectives, per_device(): left = lax.all_gather(left, 'head', axis=0, tiled=True)  8.78 us
    ppermute x1, starting transfers between devices, per_device(): left = lax.ppermute(left, ('dap', 'head'), swap)  6.69 us
  transfers between devices with their start and end apart: 19, of which 5 were waited for; matrix products, arithmetic and copies ran while one was open for 4% of the time, Pallas kernels for 5%

profile of v2, /device:TPU:11, one launch (start us, length us, event | category | flops | bytes accessed | tf_op | source)
XLA Modules:
  0.0 129.8 jit_solution(9244869059717060366)
XLA Ops:
  0.6 0.7 fusion.16
  1.3 0.9 pad_maximum_fusion.w0_ref
  2.2 0.8 collective-permute-start
  3.0 1.3 collective-permute-start.1
  4.3 1.3 %constant_dynamic-slice_fusion = bf16[16,128,256]{2,1,0:T(8,128)(2,1)S(1)} fusion(bf16[16,512,256]{2,1,0:T(8,128)(2,1)} %param.16, s32[]{:T(128)S(6)} %select_n.255), kind=kLoop, calls=%fused_computation.45 | loop fusion | bytes 2097156 | tf_op jit(solution)/shard_map/dynamic_slice | solution.py:350
  5.6 0.0 copy-start.1
  5.6 0.0 copy-start.2
  5.6 0.0 copy-start.3
  5.7 0.0 copy-start.4
  5.7 0.0 copy-start.5
  5.7 0.6 copy.30
  6.3 1.1 copy.25
  7.4 9.2 %all-to-all-start = ((bf16[32,64,256]{2,1,0:T(8,128)(2,1)}), bf16[32,64,256]{2,1,0:T(8,128)(2,1)S(1)}, u32[]{:S(2)}, u32[]{:S(2)}) async-start(bf16[32,64,256]{2,1,0:T(8,128)(2,1)} %bitcast.34), calls=%async_computation | async-start | bytes 2097152 | tf_op jit(solution)/shard_map/all_to_all | solution.py:353
  16.7 0.6 fusion.24
  17.3 0.1 copy.28.keep_col_ref
  17.5 0.1 copy.26
  17.6 0.1 mul.174
  17.7 0.1 mul.175
  17.8 0.1 dynamic_slice.12.amino_ref
  17.9 0.0 collective-permute-done.1.w2_ref
  17.9 1.0 collective-permute-start.2
  18.9 0.0 collective-permute-done.w1_ref
  18.9 1.0 collective-permute-done.2.w3_ref
  20.0 0.1 add.462.shift_ref
  20.1 11.2 %all-to-all-done.x_ref = bf16[32,64,256]{2,1,0:T(8,128)(2,1)S(1)} async-done(((bf16[32,64,256]{2,1,0:T(8,128)(2,1)}), bf16[32,64,256]{2,1,0:T(8,128)(2,1)S(1)}, u32[]{:S(2)}, u32[]{:S(2)}) %all-to-all-start) | async-done | bytes 1048608 | tf_op jit(solution)/shard_map/all_to_all | solution.py:353
  31.3 15.6 %attend.1 = (bf16[2048,256]{1,0:T(8,128)(2,1)}, bf16[4,32,512]{2,1,0:T(8,128)(2,1)S(1)}, bf16[2,256,128]{2,1,0:T(8,128)(2,1)S(1)}) custom-call(s32[4]{0:T(128)S(1)} %dynamic_slice.12.amino_ref, bf16[32,64,256]{2,1,0:T(8,128)(2,1)S(1)} %all-to-all-done.x_ref, bf16[336,256]{1,0:T(8,128)(2,1)S(1)} %pad_maximum_fusion.w0_ref, ...), custom_call_target="tpu_custom_call" | custom-call | flops 16000000000 | bytes 4194304 | tf_op jit(solution)/shard_map/attend/pallas_call | solution.py:367
  46.9 1.7 %collective-permute-start.3 = (bf16[2,256,128]{2,1,0:T(8,128)(2,1)S(1)}, bf16[2,256,128]{2,1,0:T(8,128)(2,1)S(1)}, u32[]{:S(2)}, u32[]{:S(2)}) collective-permute-start(bf16[2,256,128]{2,1,0:T(8,128)(2,1)S(1)} %get-tuple-element.25), channel_id=1, source_target_pairs={{0,4},{4,0},{8,12},{12,8},{16,20},{20,16},{24,28},{28,24},{32,36},... | collective-permute-start | bytes 393224 | tf_op jit(solution)/shard_map/ppermute | solution.py:439
  48.7 2.3 %collective-permute-done.3 = bf16[2,256,128]{2,1,0:T(8,128)(2,1)S(1)} collective-permute-done((bf16[2,256,128]{2,1,0:T(8,128)(2,1)S(1)}, bf16[2,256,128]{2,1,0:T(8,128)(2,1)S(1)}, u32[]{:S(2)}, u32[]{:S(2)}) %collective-permute-start.3) | collective-permute-done | bytes 131104 | tf_op jit(solution)/shard_map/ppermute | solution.py:439
  51.1 0.1 collective-permute-start.4
  51.2 1.5 %collective-permute-start.5 = (bf16[2,256,128]{2,1,0:T(8,128)(2,1)S(1)}, bf16[2,256,128]{2,1,0:T(8,128)(2,1)S(1)}, u32[]{:S(2)}, u32[]{:S(2)}) collective-permute-start(bf16[2,256,128]{2,1,0:T(8,128)(2,1)S(1)} %pad_maximum_fusion.1.refs_0_), channel_id=1, source_target_pairs={{0,24},{4,28},{8,0},{12,4},{16,8},{20,12},{24,16},{28,20},{32,56},... | collective-permute-start | bytes 393224 | tf_op jit(solution)/shard_map/ppermute | solution.py:439
  52.6 1.7 %collective-permute-start.6 = (bf16[2,256,128]{2,1,0:T(8,128)(2,1)S(1)}, bf16[2,256,128]{2,1,0:T(8,128)(2,1)S(1)}, u32[]{:S(2)}, u32[]{:S(2)}) collective-permute-start(bf16[2,256,128]{2,1,0:T(8,128)(2,1)S(1)} %pad_maximum_fusion.1.refs_0_), channel_id=1, source_target_pairs={{0,16},{4,20},{8,24},{12,28},{16,0},{20,4},{24,8},{28,12},{32,48},... | collective-permute-start | bytes 393224 | tf_op jit(solution)/shard_map/ppermute | solution.py:439
  54.3 0.6 collective-permute-start.7
  54.9 2.1 %collective-permute-start.8 = (bf16[2,256,128]{2,1,0:T(8,128)(2,1)S(1)}, bf16[2,256,128]{2,1,0:T(8,128)(2,1)S(1)}, u32[]{:S(2)}, u32[]{:S(2)}) collective-permute-start(bf16[2,256,128]{2,1,0:T(8,128)(2,1)S(1)} %pad_maximum_fusion.2.refs_4_), channel_id=1, source_target_pairs={{0,96},{4,100},{8,104},{12,108},{16,112},{20,116},{24,120},{28,124... | collective-permute-start | bytes 393224 | tf_op jit(solution)/shard_map/ppermute | solution.py:439
  57.0 0.0 collective-permute-done.4.refs_1_
  57.0 0.0 collective-permute-start.9
  57.1 0.0 collective-permute-done.5.refs_2_
  57.1 6.7 %collective-permute-start.10 = (bf16[4,32,512]{2,1,0:T(8,128)(2,1)S(1)}, bf16[4,32,512]{2,1,0:T(8,128)(2,1)S(1)}, u32[]{:S(2)}, u32[]{:S(2)}) collective-permute-start(bf16[4,32,512]{2,1,0:T(8,128)(2,1)S(1)} %get-tuple-element.28), channel_id=1, source_target_pairs={{0,0},{1,32},{2,64},{3,96},{4,4},{5,36},{6,68},{7,100},{8,8},{9,40... | collective-permute-start | bytes 393224 | tf_op jit(solution)/shard_map/ppermute | solution.py:429
  63.8 0.0 collective-permute-done.6.refs_3_
  63.8 0.0 collective-permute-done.7.refs_5_
  63.8 0.0 collective-permute-done.8.refs_6_
  63.8 0.0 collective-permute-done.9.refs_7_
  63.8 0.1 join.1
  63.9 3.6 %collective-permute-done.10 = bf16[4,32,512]{2,1,0:T(8,128)(2,1)S(1)} collective-permute-done((bf16[4,32,512]{2,1,0:T(8,128)(2,1)S(1)}, bf16[4,32,512]{2,1,0:T(8,128)(2,1)S(1)}, u32[]{:S(2)}, u32[]{:S(2)}) %collective-permute-start.10) | collective-permute-done | bytes 131104 | tf_op jit(solution)/shard_map/ppermute | solution.py:429
  67.5 13.4 %all-to-all-start.1 = ((bf16[128,16,256]{2,1,0:T(8,128)(2,1)}), bf16[128,16,256]{2,1,0:T(8,128)(2,1)S(1)}, u32[]{:S(2)}, u32[]{:S(2)}) async-start(bf16[128,16,256]{2,1,0:T(8,128)(2,1)} %bitcast.61), calls=%async_computation.1 | async-start | bytes 2097152 | tf_op jit(solution)/shard_map/all_to_all | solution.py:474
  80.9 1.5 %collective-permute-start.11 = (bf16[8,256,128]{2,1,0:T(8,128)(2,1)S(1)}, bf16[8,256,128]{2,1,0:T(8,128)(2,1)}, u32[]{:S(2)}, u32[]{:S(2)}) collective-permute-start(bf16[8,256,128]{2,1,0:T(8,128)(2,1)S(1)} %get-tuple-element.32.z0_ref), channel_id=1, source_target_pairs={{0,32},{4,36},{8,40},{12,44},{16,48},{20,52},{24,56},{28,60},{32,6... | collective-permute-start | bytes 1572872 | tf_op jit(solution)/shard_map/ppermute | solution.py:439
  82.4 1.2 collective-permute-start.13
  83.6 1.8 %collective-permute-start.12 = (bf16[8,256,128]{2,1,0:T(8,128)(2,1)S(1)}, bf16[8,256,128]{2,1,0:T(8,128)(2,1)}, u32[]{:S(2)}, u32[]{:S(2)}) collective-permute-start(bf16[8,256,128]{2,1,0:T(8,128)(2,1)S(1)} %get-tuple-element.32.z0_ref), channel_id=1, source_target_pairs={{0,96},{4,100},{8,104},{12,108},{16,112},{20,116},{24,120},{28,124... | collective-permute-start | bytes 1572872 | tf_op jit(solution)/shard_map/ppermute | solution.py:439
  85.4 0.3 collective-permute-start.14
  86.3 0.1 dynamic-slice_convert_fusion
  86.4 20.8 %collective-permute-done.11.z1_ref = bf16[8,256,128]{2,1,0:T(8,128)(2,1)} collective-permute-done((bf16[8,256,128]{2,1,0:T(8,128)(2,1)S(1)}, bf16[8,256,128]{2,1,0:T(8,128)(2,1)}, u32[]{:S(2)}, u32[]{:S(2)}) %collective-permute-start.11) | collective-permute-done | bytes 524320 | tf_op jit(solution)/shard_map/ppermute | solution.py:439
  107.2 0.0 collective-permute-done.13.x1_ref
  107.2 1.2 collective-permute-start.16
  108.5 0.1 convert_multiply_fusion
  108.6 0.1 mul.188
  108.8 0.1 mul.186
  108.8 0.1 fusion.1.inverse_ref
  109.0 0.1 stack.174.place_ref
  109.1 8.8 %all_gather.3 = bf16[16,32,512]{2,1,0:T(8,128)(2,1)S(1)} all-gather(bf16[4,32,512]{2,1,0:T(8,128)(2,1)S(1)} %collective-permute-done.10), channel_id=1, replica_groups=mesh['dap'=32,'head'=4] {'head'}, dimensions={0}, use_global_device_ids=true | all-gather | bytes 655360 | tf_op jit(solution)/shard_map/all_gather | solution.py:470
  117.9 0.3 copy.29
  118.2 0.0 collective-permute-done.14.x2_ref
  118.2 0.0 all-to-all-done.1.back_ref
  118.2 6.0 %early.1 = (f32[1152,128]{1,0:T(8,128)S(1)}, bf16[4,512,256]{2,1,0:T(8,128)(2,1)}) custom-call(s32[32]{0:T(128)S(1)} %stack.174.place_ref, bf16[512,512]{1,0:T(8,128)(2,1)S(1)} %bitcast.81, f32[1,128]{1,0:T(1,128)S(1)} %bitcast.90, f32[512,4]{1,0:T(8,128)S(1)} %fusion.1.inverse_ref, f32[1024,128]{1,0:T(8,128)S(1)} %copy-done, ...), custom_call_target="tpu_custom_call" | custom-call | flops 3000000000 | bytes 6291456 | tf_op jit(solution)/shard_map/early/pallas_call | solution.py:502
  124.2 0.0 collective-permute-done.15.z3_ref
  124.2 5.6 %late.1 = f32[16,128,128]{2,1,0:T(8,128)} custom-call(s32[32]{0:T(128)S(1)} %stack.174.place_ref, bf16[512,512]{1,0:T(8,128)(2,1)S(1)} %bitcast.82, f32[1,128]{1,0:T(1,128)S(1)} %bitcast.91, f32[512,4]{1,0:T(8,128)S(1)} %fusion.1.inverse_ref, f32[1024,128]{1,0:T(8,128)S(1)} %copy-done, f32[1152,128]{1,0:T(8,128)S(1)} %get-tuple-element.35.part_ref, ...), custom_call_target="tpu_custom_call" | custom-call | flops 3000000000 | bytes 6291456 | tf_op jit(solution)/shard_map/late/pallas_call | solution.py:523
  (32 shorter events, 0.2 us)
Async XLA Ops:
  2.2 16.7 %collective-permute-start = (bf16[336,256]{1,0:T(8,128)(2,1)S(1)}, bf16[336,256]{1,0:T(8,128)(2,1)S(1)}, u32[]{:S(2)}, u32[]{:S(2)}) collective-permute-start(bf16[336,256]{1,0:T(8,128)(2,1)S(1)} %pad_maximum_fusion.w0_ref), channel_id=1, source_target_pairs={{0,1},{1,0},{2,3},{3,2},{4,5},{5,4},{6,7},{7,6},{8,9},{9,8},{10,11... | collective-permute-start | bytes 516104 | tf_op jit(solution)/shard_map/ppermute | solution.py:342
  3.0 14.9 %collective-permute-start.1 = (bf16[336,256]{1,0:T(8,128)(2,1)S(1)}, bf16[336,256]{1,0:T(8,128)(2,1)S(1)}, u32[]{:S(2)}, u32[]{:S(2)}) collective-permute-start(bf16[336,256]{1,0:T(8,128)(2,1)S(1)} %pad_maximum_fusion.w0_ref), channel_id=1, source_target_pairs={{0,6},{1,7},{2,4},{3,5},{4,2},{5,3},{6,0},{7,1},{8,14},{9,15},{10,... | collective-permute-start | bytes 516104 | tf_op jit(solution)/shard_map/ppermute | solution.py:339
  4.3 12.3 %copy-start.8 = (s32[512]{0:T(512)S(1)}, s32[512]{0:T(512)}, u32[]{:S(2)}) copy-start(s32[512]{0:T(512)} %param.17) | copy-start | bytes 6148
  4.3 13.1 %copy-start.7 = (bf16[256,2,32]{0,2,1:T(8,128)(2,1)S(1)}, bf16[256,2,32]{0,2,1:T(8,128)(2,1)}, u32[]{:S(2)}) copy-start(bf16[256,2,32]{0,2,1:T(8,128)(2,1)} %param.27) | copy-start | bytes 98308
  4.3 13.5 %copy-start.9 = (s32[512]{0:T(512)S(1)}, s32[512]{0:T(512)}, u32[]{:S(2)}) copy-start(s32[512]{0:T(512)} %param.18) | copy-start | bytes 6148
  5.6 25.7 %copy-start.1 = (f32[256]{0:T(256)S(1)}, f32[256]{0:T(256)}, u32[]{:S(2)}) copy-start(f32[256]{0:T(256)} %param.19) | copy-start | bytes 3076
  5.6 25.7 %copy-start.2 = (f32[256]{0:T(256)S(1)}, f32[256]{0:T(256)}, u32[]{:S(2)}) copy-start(f32[256]{0:T(256)} %param.20) | copy-start | bytes 3076
  5.6 25.7 %copy-start.3 = (f32[256]{0:T(256)S(1)}, f32[256]{0:T(256)}, u32[]{:S(2)}) copy-start(f32[256]{0:T(256)} %param.24) | copy-start | bytes 3076
  5.7 25.7 %copy-start.4 = (f32[256]{0:T(256)S(1)}, f32[256]{0:T(256)}, u32[]{:S(2)}) copy-start(f32[256]{0:T(256)} %param.25) | copy-start | bytes 3076
  5.7 25.7 %copy-start.5 = (f32[256]{0:T(256)S(1)}, f32[256]{0:T(256)}, u32[]{:S(2)}) copy-start(f32[256]{0:T(256)} %param.26) | copy-start | bytes 3076
  7.4 23.9 %all-to-all-start = ((bf16[32,64,256]{2,1,0:T(8,128)(2,1)}), bf16[32,64,256]{2,1,0:T(8,128)(2,1)S(1)}, u32[]{:S(2)}, u32[]{:S(2)}) async-start(bf16[32,64,256]{2,1,0:T(8,128)(2,1)} %bitcast.34), calls=%async_computation | async-start | bytes 2097152 | tf_op jit(solution)/shard_map/all_to_all | solution.py:353
  17.9 2.1 %collective-permute-start.2 = (bf16[336,256]{1,0:T(8,128)(2,1)S(1)}, bf16[336,256]{1,0:T(8,128)(2,1)S(1)}, u32[]{:S(2)}, u32[]{:S(2)}) collective-permute-start(bf16[336,256]{1,0:T(8,128)(2,1)S(1)} %collective-permute-done.1.w2_ref), channel_id=1, source_target_pairs={{0,1},{1,0},{2,3},{3,2},{4,5},{5,4},{6,7},{7,6},{8,9},{9,8},{10,11... | collective-permute-start | bytes 516104 | tf_op jit(solution)/shard_map/ppermute | solution.py:344
  46.9 71.3 %copy-start = (f32[1024,128]{1,0:T(8,128)S(1)}, f32[1024,128]{1,0:T(8,128)}, u32[]{:S(2)}) copy-start(f32[1024,128]{1,0:T(8,128)} %compact_ref.3) | copy-start | bytes 1572868
  46.9 71.3 %copy-start.6 = (f32[128]{0:T(128)S(1)}, f32[128]{0:T(128)}, u32[]{:S(2)}) copy-start(f32[128]{0:T(128)} %param.29) | copy-start | bytes 1540
  46.9 4.1 %collective-permute-start.3 = (bf16[2,256,128]{2,1,0:T(8,128)(2,1)S(1)}, bf16[2,256,128]{2,1,0:T(8,128)(2,1)S(1)}, u32[]{:S(2)}, u32[]{:S(2)}) collective-permute-start(bf16[2,256,128]{2,1,0:T(8,128)(2,1)S(1)} %get-tuple-element.25), channel_id=1, source_target_pairs={{0,4},{4,0},{8,12},{12,8},{16,20},{20,16},{24,28},{28,24},{32,36},... | collective-permute-start | bytes 393224 | tf_op jit(solution)/shard_map/ppermute | solution.py:439
  51.1 6.0 %collective-permute-start.4 = (bf16[2,256,128]{2,1,0:T(8,128)(2,1)S(1)}, bf16[2,256,128]{2,1,0:T(8,128)(2,1)S(1)}, u32[]{:S(2)}, u32[]{:S(2)}) collective-permute-start(bf16[2,256,128]{2,1,0:T(8,128)(2,1)S(1)} %pad_maximum_fusion.1.refs_0_), channel_id=1, source_target_pairs={{0,8},{4,12},{8,16},{12,20},{16,24},{20,28},{24,0},{28,4},{32,40},... | collective-permute-start | bytes 393224 | tf_op jit(solution)/shard_map/ppermute | solution.py:439
  51.2 5.9 %collective-permute-start.5 = (bf16[2,256,128]{2,1,0:T(8,128)(2,1)S(1)}, bf16[2,256,128]{2,1,0:T(8,128)(2,1)S(1)}, u32[]{:S(2)}, u32[]{:S(2)}) collective-permute-start(bf16[2,256,128]{2,1,0:T(8,128)(2,1)S(1)} %pad_maximum_fusion.1.refs_0_), channel_id=1, source_target_pairs={{0,24},{4,28},{8,0},{12,4},{16,8},{20,12},{24,16},{28,20},{32,56},... | collective-permute-start | bytes 393224 | tf_op jit(solution)/shard_map/ppermute | solution.py:439
  52.6 11.2 %collective-permute-start.6 = (bf16[2,256,128]{2,1,0:T(8,128)(2,1)S(1)}, bf16[2,256,128]{2,1,0:T(8,128)(2,1)S(1)}, u32[]{:S(2)}, u32[]{:S(2)}) collective-permute-start(bf16[2,256,128]{2,1,0:T(8,128)(2,1)S(1)} %pad_maximum_fusion.1.refs_0_), channel_id=1, source_target_pairs={{0,16},{4,20},{8,24},{12,28},{16,0},{20,4},{24,8},{28,12},{32,48},... | collective-permute-start | bytes 393224 | tf_op jit(solution)/shard_map/ppermute | solution.py:439
  54.3 9.5 %collective-permute-start.7 = (bf16[2,256,128]{2,1,0:T(8,128)(2,1)S(1)}, bf16[2,256,128]{2,1,0:T(8,128)(2,1)S(1)}, u32[]{:S(2)}, u32[]{:S(2)}) collective-permute-start(bf16[2,256,128]{2,1,0:T(8,128)(2,1)S(1)} %pad_maximum_fusion.2.refs_4_), channel_id=1, source_target_pairs={{0,32},{4,36},{8,40},{12,44},{16,48},{20,52},{24,56},{28,60},{32,6... | collective-permute-start | bytes 393224 | tf_op jit(solution)/shard_map/ppermute | solution.py:439
  54.9 8.9 %collective-permute-start.8 = (bf16[2,256,128]{2,1,0:T(8,128)(2,1)S(1)}, bf16[2,256,128]{2,1,0:T(8,128)(2,1)S(1)}, u32[]{:S(2)}, u32[]{:S(2)}) collective-permute-start(bf16[2,256,128]{2,1,0:T(8,128)(2,1)S(1)} %pad_maximum_fusion.2.refs_4_), channel_id=1, source_target_pairs={{0,96},{4,100},{8,104},{12,108},{16,112},{20,116},{24,120},{28,124... | collective-permute-start | bytes 393224 | tf_op jit(solution)/shard_map/ppermute | solution.py:439
  57.0 6.7 %collective-permute-start.9 = (bf16[2,256,128]{2,1,0:T(8,128)(2,1)S(1)}, bf16[2,256,128]{2,1,0:T(8,128)(2,1)S(1)}, u32[]{:S(2)}, u32[]{:S(2)}) collective-permute-start(bf16[2,256,128]{2,1,0:T(8,128)(2,1)S(1)} %pad_maximum_fusion.2.refs_4_), channel_id=1, source_target_pairs={{0,64},{4,68},{8,72},{12,76},{16,80},{20,84},{24,88},{28,92},{32,9... | collective-permute-start | bytes 393224 | tf_op jit(solution)/shard_map/ppermute | solution.py:439
  57.1 10.4 %collective-permute-start.10 = (bf16[4,32,512]{2,1,0:T(8,128)(2,1)S(1)}, bf16[4,32,512]{2,1,0:T(8,128)(2,1)S(1)}, u32[]{:S(2)}, u32[]{:S(2)}) collective-permute-start(bf16[4,32,512]{2,1,0:T(8,128)(2,1)S(1)} %get-tuple-element.28), channel_id=1, source_target_pairs={{0,0},{1,32},{2,64},{3,96},{4,4},{5,36},{6,68},{7,100},{8,8},{9,40... | collective-permute-start | bytes 393224 | tf_op jit(solution)/shard_map/ppermute | solution.py:429
  67.5 50.7 %all-to-all-start.1 = ((bf16[128,16,256]{2,1,0:T(8,128)(2,1)}), bf16[128,16,256]{2,1,0:T(8,128)(2,1)S(1)}, u32[]{:S(2)}, u32[]{:S(2)}) async-start(bf16[128,16,256]{2,1,0:T(8,128)(2,1)} %bitcast.61), calls=%async_computation.1 | async-start | bytes 2097152 | tf_op jit(solution)/shard_map/all_to_all | solution.py:474
  80.9 26.3 %collective-permute-start.11 = (bf16[8,256,128]{2,1,0:T(8,128)(2,1)S(1)}, bf16[8,256,128]{2,1,0:T(8,128)(2,1)}, u32[]{:S(2)}, u32[]{:S(2)}) collective-permute-start(bf16[8,256,128]{2,1,0:T(8,128)(2,1)S(1)} %get-tuple-element.32.z0_ref), channel_id=1, source_target_pairs={{0,32},{4,36},{8,40},{12,44},{16,48},{20,52},{24,56},{28,60},{32,6... | collective-permute-start | bytes 1572872 | tf_op jit(solution)/shard_map/ppermute | solution.py:439
  82.4 24.8 %collective-permute-start.13 = (bf16[8,256,128]{2,1,0:T(8,128)(2,1)S(1)}, bf16[8,256,128]{2,1,0:T(8,128)(2,1)}, u32[]{:S(2)}, u32[]{:S(2)}) collective-permute-start(bf16[8,256,128]{2,1,0:T(8,128)(2,1)S(1)} %get-tuple-element.33.x0_ref), channel_id=1, source_target_pairs={{0,8},{4,12},{8,16},{12,20},{16,24},{20,28},{24,0},{28,4},{32,40},... | collective-permute-start | bytes 1572872 | tf_op jit(solution)/shard_map/ppermute | solution.py:439
  83.6 34.6 %collective-permute-start.12 = (bf16[8,256,128]{2,1,0:T(8,128)(2,1)S(1)}, bf16[8,256,128]{2,1,0:T(8,128)(2,1)}, u32[]{:S(2)}, u32[]{:S(2)}) collective-permute-start(bf16[8,256,128]{2,1,0:T(8,128)(2,1)S(1)} %get-tuple-element.32.z0_ref), channel_id=1, source_target_pairs={{0,96},{4,100},{8,104},{12,108},{16,112},{20,116},{24,120},{28,124... | collective-permute-start | bytes 1572872 | tf_op jit(solution)/shard_map/ppermute | solution.py:439
  85.4 32.8 %collective-permute-start.14 = (bf16[8,256,128]{2,1,0:T(8,128)(2,1)S(1)}, bf16[8,256,128]{2,1,0:T(8,128)(2,1)}, u32[]{:S(2)}, u32[]{:S(2)}) collective-permute-start(bf16[8,256,128]{2,1,0:T(8,128)(2,1)S(1)} %get-tuple-element.33.x0_ref), channel_id=1, source_target_pairs={{0,24},{4,28},{8,0},{12,4},{16,8},{20,12},{24,16},{28,20},{32,56},... | collective-permute-start | bytes 1572872 | tf_op jit(solution)/shard_map/ppermute | solution.py:439
  107.2 17.0 %collective-permute-start.15 = (bf16[8,256,128]{2,1,0:T(8,128)(2,1)}, bf16[8,256,128]{2,1,0:T(8,128)(2,1)}, u32[]{:S(2)}, u32[]{:S(2)}) collective-permute-start(bf16[8,256,128]{2,1,0:T(8,128)(2,1)} %collective-permute-done.11.z1_ref), channel_id=1, source_target_pairs={{0,32},{4,36},{8,40},{12,44},{16,48},{20,52},{24,56},{28,60},{32,6... | collective-permute-start | bytes 1572872 | tf_op jit(solution)/shard_map/ppermute | solution.py:439
  107.2 17.0 %collective-permute-start.16 = (bf16[8,256,128]{2,1,0:T(8,128)(2,1)}, bf16[8,256,128]{2,1,0:T(8,128)(2,1)}, u32[]{:S(2)}, u32[]{:S(2)}) collective-permute-start(bf16[8,256,128]{2,1,0:T(8,128)(2,1)} %collective-permute-done.13.x1_ref), channel_id=1, source_target_pairs={{0,8},{4,12},{8,16},{12,20},{16,24},{20,28},{24,0},{28,4},{32,40},... | collective-permute-start | bytes 1572872 | tf_op jit(solution)/shard_map/ppermute | solution.py:439

commit v3 on v2

--- a/solution.py
+++ b/solution.py
@@ -209,24 +209,7 @@
 )
 
 
-def early_kernel(
-    place_ref,
-    left_ref,
-    bias_ref,
-    inverse_ref,
-    compact_ref,
-    back_ref,
-    z0_ref,
-    z1_ref,
-    z2_ref,
-    x0_ref,
-    x1_ref,
-    x2_ref,
-    part_ref,
-    aligned_ref,
-    mid_ref,
-    weight_ref,
-):
+def arrange_kernel(back_ref, aligned_ref):
     low = lax.broadcasted_iota(jnp.int32, (8, back_ref.shape[2]), 0) < 4
 
     def arrange(index, _):
@@ -245,6 +228,24 @@
         return 0
 
     lax.fori_loop(0, back_ref.shape[0] // 4, arrange, 0)
+
+
+def early_kernel(
+    place_ref,
+    left_ref,
+    bias_ref,
+    inverse_ref,
+    compact_ref,
+    z0_ref,
+    z1_ref,
+    z2_ref,
+    x0_ref,
+    x1_ref,
+    x2_ref,
+    part_ref,
+    mid_ref,
+    weight_ref,
+):
     rows = left_ref.shape[0] // CO
     inner = z0_ref.shape[2] // CO
 
@@ -291,7 +292,8 @@
         turn_ref[pl.ds(at, block), :] = part_ref[n * block : (n + 1) * block, :]
     columns = out_ref.shape[1]
     for i in range(rows):
-        out_ref[i] = turn_ref[pl.ds(i, columns, stride=rows), :]
+        head = place_ref[len(EARLY) + len(LATE) + i // inner]
+        out_ref[head * inner + i % inner] = turn_ref[pl.ds(i, columns, stride=rows), :]
 
 
 def whole():
@@ -461,14 +463,17 @@
         ),
         name="join",
     )(*parts)
-    (*mids, left, rows) = lax.optimization_barrier((*mids, left, rows))
+    (*mids, left) = lax.optimization_barrier((*mids, left))
     z_pieces = second_stage(mids[0], 0)
     x_pieces = second_stage(mids[1], 1)
     z_pieces = (*z_pieces, shifted(z_pieces[1], 0, 1))
     x_pieces = (*x_pieces, shifted(x_pieces[1], 1, 1))
 
-    left = lax.all_gather(left, "head", axis=0, tiled=True)
+    left_core = lax.ppermute(left, "head", swap_core)
+    left_far = lax.ppermute(left, "head", [(h, h ^ 2) for h in range(n_head)])
+    left_corner = lax.ppermute(left_far, "head", swap_core)
     i_rows = mine * n_head
+    left = jnp.concatenate([left, left_core, left_far, left_corner], 0)
     left = jnp.swapaxes(left, 0, 1).reshape(CO * i_rows, seqs)
 
     back = lax.all_to_all(
@@ -481,6 +486,10 @@
     own = own_seqs // n_head
     total = jnp.sum(homolog).astype(F32)
     row_keep = lax.dynamic_slice_in_dim(amino, dap_id * i_rows, i_rows).astype(F32)
+    heads = [head_id ^ flip for flip in range(n_head)]
+    row_keep = jnp.concatenate(
+        [lax.dynamic_slice_in_dim(row_keep, h * mine, mine) for h in heads]
+    )
     col_keep = lax.dynamic_slice_in_dim(amino, head_id * col_width, col_width).astype(F32)
     norm = jnp.maximum(
         total * row_keep[None, :, None] * col_keep.reshape(n_dap, 1, mine), 1.0
@@ -493,23 +502,20 @@
                 at_z, at_x, at_y = (zi + dz) % nz, (xi + dx) % nx, (yi + dy) % ny
                 places.append((at_x * ny + at_y) * nz + at_z)
     shared = (
-        jnp.stack(places).astype(jnp.int32),
+        jnp.stack([*places, *heads]).astype(jnp.int32),
         left,
         pair_bias.reshape(1, depth),
         inverse,
         pair_weight,
     )
-    early, alignment = pl.pallas_call(
+    early = pl.pallas_call(
         early_kernel,
         in_specs=[
             pl.BlockSpec(memory_space=pltpu.SMEM),
-            *[pl.BlockSpec(memory_space=pltpu.VMEM)] * 11,
-        ],
-        out_specs=[pl.BlockSpec(memory_space=pltpu.VMEM)] * 2,
-        out_shape=[
-            jax.ShapeDtypeStruct((len(EARLY) * mine * i_rows, depth), F32),
-            jax.ShapeDtypeStruct((own, residues, chans), BF16),
-        ],
+            *[pl.BlockSpec(memory_space=pltpu.VMEM)] * 10,
+        ],
+        out_specs=pl.BlockSpec(memory_space=pltpu.VMEM),
+        out_shape=jax.ShapeDtypeStruct((len(EARLY) * mine * i_rows, depth), F32),
         scratch_shapes=[
             pltpu.VMEM((len(EARLY) * i_rows, CO * lanes), BF16),
             pltpu.VMEM((CO * lanes, mine * depth), BF16),
@@ -519,7 +525,18 @@
             flops=3_000_000_000, bytes_accessed=6 * 2**20, transcendentals=0
         ),
         name="early",
-    )(*shared, back, *z_pieces[:3], *x_pieces[:3])
+    )(*shared, *z_pieces[:3], *x_pieces[:3])
+    alignment = pl.pallas_call(
+        arrange_kernel,
+        in_specs=[pl.BlockSpec(memory_space=pltpu.VMEM)],
+        out_specs=pl.BlockSpec(memory_space=pltpu.VMEM),
+        out_shape=jax.ShapeDtypeStruct((own, residues, chans), BF16),
+        compiler_params=pltpu.CompilerParams(vmem_limit_bytes=8 * 2**20),
+        cost_estimate=pl.CostEstimate(
+            flops=500_000_000, bytes_accessed=2 * 2**20, transcendentals=0
+        ),
+        name="arrange",
+    )(back)
     pair = pl.pallas_call(
         late_kernel,
         in_specs=[

time: 132 us -> 130 us (0.985)
  the two profiles are of different devices: /device:TPU:11 before, /device:TPU:1 now
where the time goes in v3:
time: 130 us; the launch traced here: 129 us
  starting transfers between devices  50.3 us (39%)
  waiting for transfers between devices  40.8 us (31%)
  Pallas kernels  27.4 us (21%)
  local copies, waits for them, and re-layouts  6.25 us (5%)
  other arithmetic  2.8 us (2%)
  between operations  1.75 us (1%)
    pallas_call x1, Pallas kernels, per_device(): pl.pallas_call(attend_kernel, in_specs=[pl.BlockSpec(memory_space=pltpu.S...  15.6 us
    all_to_all x1, starting transfers between devices, per_device(): lax.all_to_all(rows.reshape(n_dap * n_head, seqs * mine // (n_dap * n_hea...  14.9 us
    all_to_all x1, waiting for transfers between devices, per_device(): lax.all_to_all(block, 'dap', split_axis=0, concat_axis=0, tiled=True)  14.4 us
    ppermute x13, starting transfers between devices, shifted(): return lax.ppermute(value, 'dap', pairs)  12.2 us
    ppermute x13, waiting for transfers between devices, shifted(): return lax.ppermute(value, 'dap', pairs)  12.2 us
    ppermute x1, waiting for transfers between devices, per_device(): left_far = lax.ppermute(left, 'head', [(h, h ^ 2) for h in range(n_head)])  10.1 us
    all_to_all x1, starting transfers between devices, per_device(): lax.all_to_all(block, 'dap', split_axis=0, concat_axis=0, tiled=True)  7.88 us
    pallas_call x1, Pallas kernels, per_device(): pl.pallas_call(late_kernel, in_specs=[pl.BlockSpec(memory_space=pltpu.SME...  5.61 us
  transfers between devices with their start and end apart: 22, of which 11 were waited for; matrix products, arithmetic and copies ran while one was open for 4% of the time, Pallas kernels for 5%

profile of v3, /device:TPU:1, one launch (start us, length us, event | category | flops | bytes accessed | tf_op | source)
XLA Modules:
  0.0 129.3 jit_solution(9653474445337202411)
XLA Ops:
  0.6 0.7 fusion.16
  1.3 0.9 pad_maximum_fusion.w0_ref
  2.2 3.6 %collective-permute-start.1 = (bf16[336,256]{1,0:T(8,128)(2,1)S(1)}, bf16[336,256]{1,0:T(8,128)(2,1)S(1)}, u32[]{:S(2)}, u32[]{:S(2)}) collective-permute-start(bf16[336,256]{1,0:T(8,128)(2,1)S(1)} %pad_maximum_fusion.w0_ref), channel_id=1, source_target_pairs={{0,6},{1,7},{2,4},{3,5},{4,2},{5,3},{6,0},{7,1},{8,14},{9,15},{10,... | collective-permute-start | bytes 516104 | tf_op jit(solution)/shard_map/ppermute | solution.py:341
  5.9 1.0 collective-permute-start
  6.8 1.3 %constant_dynamic-slice_fusion = bf16[16,128,256]{2,1,0:T(8,128)(2,1)S(1)} fusion(bf16[16,512,256]{2,1,0:T(8,128)(2,1)} %param.16, s32[]{:T(128)S(6)} %select_n.257), kind=kLoop, calls=%fused_computation.47 | loop fusion | bytes 2097156 | tf_op jit(solution)/shard_map/dynamic_slice | solution.py:352
  8.2 0.0 copy-start.1
  8.2 0.0 copy-start.2
  8.2 0.0 copy-start.3
  8.2 0.0 copy-start.4
  8.2 0.0 copy-start.5
  8.2 0.6 copy.24
  8.8 1.1 copy.19
  9.9 7.9 %all-to-all-start = ((bf16[32,64,256]{2,1,0:T(8,128)(2,1)}), bf16[32,64,256]{2,1,0:T(8,128)(2,1)S(1)}, u32[]{:S(2)}, u32[]{:S(2)}) async-start(bf16[32,64,256]{2,1,0:T(8,128)(2,1)} %bitcast.2), calls=%async_computation | async-start | bytes 2097152 | tf_op jit(solution)/shard_map/all_to_all | solution.py:355
  17.9 0.7 fusion.24
  18.5 0.1 mul.87
  18.6 0.1 mul.88
  18.7 0.1 copy.20
  18.8 0.1 copy.22.keep_col_ref
  19.0 0.1 dynamic_slice.24.amino_ref
  19.1 0.0 collective-permute-done.1.w2_ref
  19.1 0.4 collective-permute-start.2
  19.5 1.1 collective-permute-done.2.w3_ref
  20.6 0.1 add.478.shift_ref
  20.8 14.4 %all-to-all-done.x_ref = bf16[32,64,256]{2,1,0:T(8,128)(2,1)S(1)} async-done(((bf16[32,64,256]{2,1,0:T(8,128)(2,1)}), bf16[32,64,256]{2,1,0:T(8,128)(2,1)S(1)}, u32[]{:S(2)}, u32[]{:S(2)}) %all-to-all-start) | async-done | bytes 1048608 | tf_op jit(solution)/shard_map/all_to_all | solution.py:355
  35.2 15.6 %attend.1 = (bf16[2048,256]{1,0:T(8,128)(2,1)}, bf16[4,32,512]{2,1,0:T(8,128)(2,1)S(1)}, bf16[2,256,128]{2,1,0:T(8,128)(2,1)S(1)}) custom-call(s32[4]{0:T(128)S(1)} %dynamic_slice.24.amino_ref, bf16[32,64,256]{2,1,0:T(8,128)(2,1)S(1)} %all-to-all-done.x_ref, bf16[336,256]{1,0:T(8,128)(2,1)S(1)} %pad_maximum_fusion.w0_ref, ...), custom_call_target="tpu_custom_call" | custom-call | flops 16000000000 | bytes 4194304 | tf_op jit(solution)/shard_map/attend/pallas_call | solution.py:369
  50.8 0.2 collective-permute-start.3
  51.0 3.6 %collective-permute-done.3 = bf16[2,256,128]{2,1,0:T(8,128)(2,1)S(1)} collective-permute-done((bf16[2,256,128]{2,1,0:T(8,128)(2,1)S(1)}, bf16[2,256,128]{2,1,0:T(8,128)(2,1)S(1)}, u32[]{:S(2)}, u32[]{:S(2)}) %collective-permute-start.3) | collective-permute-done | bytes 131104 | tf_op jit(solution)/shard_map/ppermute | solution.py:441
  54.6 0.1 collective-permute-start.6
  54.7 2.7 %collective-permute-start.5 = (bf16[2,256,128]{2,1,0:T(8,128)(2,1)S(1)}, bf16[2,256,128]{2,1,0:T(8,128)(2,1)S(1)}, u32[]{:S(2)}, u32[]{:S(2)}) collective-permute-start(bf16[2,256,128]{2,1,0:T(8,128)(2,1)S(1)} %pad_maximum_fusion.1.refs_0_), channel_id=1, source_target_pairs={{0,24},{4,28},{8,0},{12,4},{16,8},{20,12},{24,16},{28,20},{32,56},... | collective-permute-start | bytes 393224 | tf_op jit(solution)/shard_map/ppermute | solution.py:441
  57.4 0.6 collective-permute-start.9
  58.0 1.1 collective-permute-start.8
  59.1 1.0 collective-permute-done.6.refs_3_
  60.0 0.7 collective-permute-done.5.refs_2_
  60.7 5.4 %collective-permute-start.10 = (bf16[4,32,512]{2,1,0:T(8,128)(2,1)S(1)}, bf16[4,32,512]{2,1,0:T(8,128)(2,1)S(1)}, u32[]{:S(2)}, u32[]{:S(2)}) collective-permute-start(bf16[4,32,512]{2,1,0:T(8,128)(2,1)S(1)} %get-tuple-element.26), channel_id=1, source_target_pairs={{0,0},{1,32},{2,64},{3,96},{4,4},{5,36},{6,68},{7,100},{8,8},{9,40... | collective-permute-start | bytes 393224 | tf_op jit(solution)/shard_map/ppermute | solution.py:431
  66.2 0.1 join.1
  66.2 3.1 %collective-permute-done.10 = bf16[4,32,512]{2,1,0:T(8,128)(2,1)S(1)} collective-permute-done((bf16[4,32,512]{2,1,0:T(8,128)(2,1)S(1)}, bf16[4,32,512]{2,1,0:T(8,128)(2,1)S(1)}, u32[]{:S(2)}, u32[]{:S(2)}) %collective-permute-start.10) | collective-permute-done | bytes 131104 | tf_op jit(solution)/shard_map/ppermute | solution.py:431
  69.3 0.2 collective-permute-start.16
  69.5 14.9 %all-to-all-start.1 = ((bf16[128,16,256]{2,1,0:T(8,128)(2,1)}), bf16[128,16,256]{2,1,0:T(8,128)(2,1)S(1)}, u32[]{:S(2)}, u32[]{:S(2)}) async-start(bf16[128,16,256]{2,1,0:T(8,128)(2,1)} %bitcast.25), calls=%async_computation.1 | async-start | bytes 2097152 | tf_op jit(solution)/shard_map/all_to_all | solution.py:479
  84.4 2.9 %collective-permute-start.12 = (bf16[4,32,512]{2,1,0:T(8,128)(2,1)S(1)}, bf16[4,32,512]{2,1,0:T(8,128)(2,1)S(1)}, u32[]{:S(2)}, u32[]{:S(2)}) collective-permute-start(bf16[4,32,512]{2,1,0:T(8,128)(2,1)S(1)} %collective-permute-done.10), channel_id=1, source_target_pairs={{0,2},{1,3},{2,0},{3,1},{4,6},{5,7},{6,4},{7,5},{8,10},{9,11},{10,... | collective-permute-start | bytes 393224 | tf_op jit(solution)/shard_map/ppermute | solution.py:473
  87.4 0.7 collective-permute-start.11
  88.0 3.2 %collective-permute-start.15 = (bf16[8,256,128]{2,1,0:T(8,128)(2,1)S(1)}, bf16[8,256,128]{2,1,0:T(8,128)(2,1)}, u32[]{:S(2)}, u32[]{:S(2)}) collective-permute-start(bf16[8,256,128]{2,1,0:T(8,128)(2,1)S(1)} %get-tuple-element.28.z0_ref), channel_id=1, source_target_pairs={{0,96},{4,100},{8,104},{12,108},{16,112},{20,116},{24,120},{28,124... | collective-permute-start | bytes 1572872 | tf_op jit(solution)/shard_map/ppermute | solution.py:441
  91.2 10.1 %collective-permute-done.12 = bf16[4,32,512]{2,1,0:T(8,128)(2,1)S(1)} collective-permute-done((bf16[4,32,512]{2,1,0:T(8,128)(2,1)S(1)}, bf16[4,32,512]{2,1,0:T(8,128)(2,1)S(1)}, u32[]{:S(2)}, u32[]{:S(2)}) %collective-permute-start.12) | collective-permute-done | bytes 131104 | tf_op jit(solution)/shard_map/ppermute | solution.py:473
  101.3 2.7 %collective-permute-start.17 = (bf16[8,256,128]{2,1,0:T(8,128)(2,1)S(1)}, bf16[8,256,128]{2,1,0:T(8,128)(2,1)}, u32[]{:S(2)}, u32[]{:S(2)}) collective-permute-start(bf16[8,256,128]{2,1,0:T(8,128)(2,1)S(1)} %get-tuple-element.29.x0_ref), channel_id=1, source_target_pairs={{0,24},{4,28},{8,0},{12,4},{16,8},{20,12},{24,16},{28,20},{32,56},... | collective-permute-start | bytes 1572872 | tf_op jit(solution)/shard_map/ppermute | solution.py:441
  104.0 0.1 dynamic-slice_convert_fusion.1
  104.7 0.1 fusion.25
  104.8 1.3 %collective-permute-start.13 = (bf16[4,32,512]{2,1,0:T(8,128)(2,1)S(1)}, bf16[4,32,512]{2,1,0:T(8,128)(2,1)S(1)}, u32[]{:S(2)}, u32[]{:S(2)}) collective-permute-start(bf16[4,32,512]{2,1,0:T(8,128)(2,1)S(1)} %collective-permute-done.12), channel_id=1, source_target_pairs={{0,1},{1,0},{2,3},{3,2},{4,5},{5,4},{6,7},{7,6},{8,9},{9,8},{10,11... | collective-permute-start | bytes 393224 | tf_op jit(solution)/shard_map/ppermute | solution.py:474
  106.1 0.1 maximum_multiply_fusion
  106.3 0.1 mul.206
  106.4 1.5 %collective-permute-start.18 = (bf16[8,256,128]{2,1,0:T(8,128)(2,1)}, bf16[8,256,128]{2,1,0:T(8,128)(2,1)}, u32[]{:S(2)}, u32[]{:S(2)}) collective-permute-start(bf16[8,256,128]{2,1,0:T(8,128)(2,1)} %collective-permute-done.14.z1_ref), channel_id=1, source_target_pairs={{0,32},{4,36},{8,40},{12,44},{16,48},{20,52},{24,56},{28,60},{32,6... | collective-permute-start | bytes 1572872 | tf_op jit(solution)/shard_map/ppermute | solution.py:441
  107.9 0.1 dynamic-slice_convert_fusion
  108.0 0.1 mul.208
  108.1 0.1 fusion.1.inverse_ref
  108.3 0.1 stack.202.place_ref
  108.4 0.1 maximum_bitcast_fusion
  108.5 0.3 copy.23
  108.8 1.7 %collective-permute-done.15.z2_ref = bf16[8,256,128]{2,1,0:T(8,128)(2,1)} collective-permute-done((bf16[8,256,128]{2,1,0:T(8,128)(2,1)S(1)}, bf16[8,256,128]{2,1,0:T(8,128)(2,1)}, u32[]{:S(2)}, u32[]{:S(2)}) %collective-permute-start.15) | collective-permute-done | bytes 524320 | tf_op jit(solution)/shard_map/ppermute | solution.py:441
  110.4 3.8 %collective-permute-done.17.x2_ref = bf16[8,256,128]{2,1,0:T(8,128)(2,1)} collective-permute-done((bf16[8,256,128]{2,1,0:T(8,128)(2,1)S(1)}, bf16[8,256,128]{2,1,0:T(8,128)(2,1)}, u32[]{:S(2)}, u32[]{:S(2)}) %collective-permute-start.17) | collective-permute-done | bytes 524320 | tf_op jit(solution)/shard_map/ppermute | solution.py:441
  114.3 4.6 %early.1.part_ref = f32[1152,128]{1,0:T(8,128)S(1)} custom-call(s32[36]{0:T(128)S(1)} %stack.202.place_ref, bf16[512,512]{1,0:T(8,128)(2,1)S(1)} %bitcast.86, f32[1,128]{1,0:T(1,128)S(1)} %bitcast.95, f32[512,4]{1,0:T(8,128)S(1)} %fusion.1.inverse_ref, f32[1024,128]{1,0:T(8,128)S(1)} %copy-done, bf16[8,256,128]{2,1,0:T(8,128)(2,1)S(1)} %get-tuple-element.28.z0_ref, ...), custom_call_target="tpu_custom_call" | custom-call | flops 3000000000 | bytes 6291456 | tf_op jit(solution)/shard_map/early/pallas_call | solution.py:511
  118.9 0.8 copy-done.7
  119.7 1.5 %arrange.1 = bf16[4,512,256]{2,1,0:T(8,128)(2,1)} custom-call(bf16[128,16,256]{2,1,0:T(8,128)(2,1)S(1)} %all-to-all-done.1.back_ref), custom_call_target="tpu_custom_call" | custom-call | flops 500000000 | bytes 2097152 | tf_op jit(solution)/shard_map/arrange/pallas_call | solution.py:529
  121.2 1.1 collective-permute-done.18.z3_ref
  122.3 0.4 collective-permute-done.19.x3_ref
  122.6 1.1 copy-done.8
  123.7 5.6 %late.1 = f32[16,128,128]{2,1,0:T(8,128)} custom-call(s32[36]{0:T(128)S(1)} %stack.202.place_ref, bf16[512,512]{1,0:T(8,128)(2,1)S(1)} %bitcast.87, f32[1,128]{1,0:T(1,128)S(1)} %bitcast.96, f32[512,4]{1,0:T(8,128)S(1)} %fusion.1.inverse_ref, f32[1024,128]{1,0:T(8,128)S(1)} %copy-done, f32[1152,128]{1,0:T(8,128)S(1)} %copy-done.8, ...), custom_call_target="tpu_custom_call" | custom-call | flops 3000000000 | bytes 6291456 | tf_op jit(solution)/shard_map/late/pallas_call | solution.py:540
  (45 shorter events, 0.2 us)
Async XLA Ops:
  2.2 16.8 %collective-permute-start.1 = (bf16[336,256]{1,0:T(8,128)(2,1)S(1)}, bf16[336,256]{1,0:T(8,128)(2,1)S(1)}, u32[]{:S(2)}, u32[]{:S(2)}) collective-permute-start(bf16[336,256]{1,0:T(8,128)(2,1)S(1)} %pad_maximum_fusion.w0_ref), channel_id=1, source_target_pairs={{0,6},{1,7},{2,4},{3,5},{4,2},{5,3},{6,0},{7,1},{8,14},{9,15},{10,... | collective-permute-start | bytes 516104 | tf_op jit(solution)/shard_map/ppermute | solution.py:341
  5.9 13.6 %collective-permute-start = (bf16[336,256]{1,0:T(8,128)(2,1)S(1)}, bf16[336,256]{1,0:T(8,128)(2,1)S(1)}, u32[]{:S(2)}, u32[]{:S(2)}) collective-permute-start(bf16[336,256]{1,0:T(8,128)(2,1)S(1)} %pad_maximum_fusion.w0_ref), channel_id=1, source_target_pairs={{0,1},{1,0},{2,3},{3,2},{4,5},{5,4},{6,7},{7,6},{8,9},{9,8},{10,11... | collective-permute-start | bytes 516104 | tf_op jit(solution)/shard_map/ppermute | solution.py:344
  6.8 11.0 %copy-start.10 = (s32[512]{0:T(512)S(1)}, s32[512]{0:T(512)}, u32[]{:S(2)}) copy-start(s32[512]{0:T(512)} %param.17) | copy-start | bytes 6148
  6.8 11.7 %copy-start.9 = (bf16[256,2,32]{0,2,1:T(8,128)(2,1)S(1)}, bf16[256,2,32]{0,2,1:T(8,128)(2,1)}, u32[]{:S(2)}) copy-start(bf16[256,2,32]{0,2,1:T(8,128)(2,1)} %param.27) | copy-start | bytes 98308
  6.8 12.1 %copy-start.11 = (s32[512]{0:T(512)S(1)}, s32[512]{0:T(512)}, u32[]{:S(2)}) copy-start(s32[512]{0:T(512)} %param.18) | copy-start | bytes 6148
  8.2 27.0 %copy-start.1 = (f32[256]{0:T(256)S(1)}, f32[256]{0:T(256)}, u32[]{:S(2)}) copy-start(f32[256]{0:T(256)} %param.19) | copy-start | bytes 3076
  8.2 27.0 %copy-start.2 = (f32[256]{0:T(256)S(1)}, f32[256]{0:T(256)}, u32[]{:S(2)}) copy-start(f32[256]{0:T(256)} %param.20) | copy-start | bytes 3076
  8.2 26.9 %copy-start.3 = (f32[256]{0:T(256)S(1)}, f32[256]{0:T(256)}, u32[]{:S(2)}) copy-start(f32[256]{0:T(256)} %param.24) | copy-start | bytes 3076
  8.2 26.9 %copy-start.4 = (f32[256]{0:T(256)S(1)}, f32[256]{0:T(256)}, u32[]{:S(2)}) copy-start(f32[256]{0:T(256)} %param.25) | copy-start | bytes 3076
  8.2 26.9 %copy-start.5 = (f32[256]{0:T(256)S(1)}, f32[256]{0:T(256)}, u32[]{:S(2)}) copy-start(f32[256]{0:T(256)} %param.26) | copy-start | bytes 3076
  9.9 25.2 %all-to-all-start = ((bf16[32,64,256]{2,1,0:T(8,128)(2,1)}), bf16[32,64,256]{2,1,0:T(8,128)(2,1)S(1)}, u32[]{:S(2)}, u32[]{:S(2)}) async-start(bf16[32,64,256]{2,1,0:T(8,128)(2,1)} %bitcast.2), calls=%async_computation | async-start | bytes 2097152 | tf_op jit(solution)/shard_map/all_to_all | solution.py:355
  19.1 1.5 %collective-permute-start.2 = (bf16[336,256]{1,0:T(8,128)(2,1)S(1)}, bf16[336,256]{1,0:T(8,128)(2,1)S(1)}, u32[]{:S(2)}, u32[]{:S(2)}) collective-permute-start(bf16[336,256]{1,0:T(8,128)(2,1)S(1)} %collective-permute-done.1.w2_ref), channel_id=1, source_target_pairs={{0,1},{1,0},{2,3},{3,2},{4,5},{5,4},{6,7},{7,6},{8,9},{9,8},{10,11... | collective-permute-start | bytes 516104 | tf_op jit(solution)/shard_map/ppermute | solution.py:346
  50.8 63.5 %copy-start = (f32[1024,128]{1,0:T(8,128)S(1)}, f32[1024,128]{1,0:T(8,128)}, u32[]{:S(2)}) copy-start(f32[1024,128]{1,0:T(8,128)} %compact_ref.3) | copy-start | bytes 1572868
  50.8 63.5 %copy-start.6 = (f32[128]{0:T(128)S(1)}, f32[128]{0:T(128)}, u32[]{:S(2)}) copy-start(f32[128]{0:T(128)} %param.29) | copy-start | bytes 1540
  50.8 3.8 %collective-permute-start.3 = (bf16[2,256,128]{2,1,0:T(8,128)(2,1)S(1)}, bf16[2,256,128]{2,1,0:T(8,128)(2,1)S(1)}, u32[]{:S(2)}, u32[]{:S(2)}) collective-permute-start(bf16[2,256,128]{2,1,0:T(8,128)(2,1)S(1)} %get-tuple-element.23), channel_id=1, source_target_pairs={{0,4},{4,0},{8,12},{12,8},{16,20},{20,16},{24,28},{28,24},{32,36},... | collective-permute-start | bytes 393224 | tf_op jit(solution)/shard_map/ppermute | solution.py:441
  54.6 5.4 %collective-permute-start.6 = (bf16[2,256,128]{2,1,0:T(8,128)(2,1)S(1)}, bf16[2,256,128]{2,1,0:T(8,128)(2,1)S(1)}, u32[]{:S(2)}, u32[]{:S(2)}) collective-permute-start(bf16[2,256,128]{2,1,0:T(8,128)(2,1)S(1)} %pad_maximum_fusion.1.refs_0_), channel_id=1, source_target_pairs={{0,16},{4,20},{8,24},{12,28},{16,0},{20,4},{24,8},{28,12},{32,48},... | collective-permute-start | bytes 393224 | tf_op jit(solution)/shard_map/ppermute | solution.py:441
  54.7 6.0 %collective-permute-start.5 = (bf16[2,256,128]{2,1,0:T(8,128)(2,1)S(1)}, bf16[2,256,128]{2,1,0:T(8,128)(2,1)S(1)}, u32[]{:S(2)}, u32[]{:S(2)}) collective-permute-start(bf16[2,256,128]{2,1,0:T(8,128)(2,1)S(1)} %pad_maximum_fusion.1.refs_0_), channel_id=1, source_target_pairs={{0,24},{4,28},{8,0},{12,4},{16,8},{20,12},{24,16},{28,20},{32,56},... | collective-permute-start | bytes 393224 | tf_op jit(solution)/shard_map/ppermute | solution.py:441
  57.4 8.8 %collective-permute-start.4 = (bf16[2,256,128]{2,1,0:T(8,128)(2,1)S(1)}, bf16[2,256,128]{2,1,0:T(8,128)(2,1)S(1)}, u32[]{:S(2)}, u32[]{:S(2)}) collective-permute-start(bf16[2,256,128]{2,1,0:T(8,128)(2,1)S(1)} %pad_maximum_fusion.1.refs_0_), channel_id=1, source_target_pairs={{0,8},{4,12},{8,16},{12,20},{16,24},{20,28},{24,0},{28,4},{32,40},... | collective-permute-start | bytes 393224 | tf_op jit(solution)/shard_map/ppermute | solution.py:441
  57.4 8.7 %collective-permute-start.9 = (bf16[2,256,128]{2,1,0:T(8,128)(2,1)S(1)}, bf16[2,256,128]{2,1,0:T(8,128)(2,1)S(1)}, u32[]{:S(2)}, u32[]{:S(2)}) collective-permute-start(bf16[2,256,128]{2,1,0:T(8,128)(2,1)S(1)} %pad_maximum_fusion.2.refs_4_), channel_id=1, source_target_pairs={{0,64},{4,68},{8,72},{12,76},{16,80},{20,84},{24,88},{28,92},{32,9... | collective-permute-start | bytes 393224 | tf_op jit(solution)/shard_map/ppermute | solution.py:441
  58.0 8.2 %collective-permute-start.8 = (bf16[2,256,128]{2,1,0:T(8,128)(2,1)S(1)}, bf16[2,256,128]{2,1,0:T(8,128)(2,1)S(1)}, u32[]{:S(2)}, u32[]{:S(2)}) collective-permute-start(bf16[2,256,128]{2,1,0:T(8,128)(2,1)S(1)} %pad_maximum_fusion.2.refs_4_), channel_id=1, source_target_pairs={{0,96},{4,100},{8,104},{12,108},{16,112},{20,116},{24,120},{28,124... | collective-permute-start | bytes 393224 | tf_op jit(solution)/shard_map/ppermute | solution.py:441
  60.0 6.1 %collective-permute-start.7 = (bf16[2,256,128]{2,1,0:T(8,128)(2,1)S(1)}, bf16[2,256,128]{2,1,0:T(8,128)(2,1)S(1)}, u32[]{:S(2)}, u32[]{:S(2)}) collective-permute-start(bf16[2,256,128]{2,1,0:T(8,128)(2,1)S(1)} %pad_maximum_fusion.2.refs_4_), channel_id=1, source_target_pairs={{0,32},{4,36},{8,40},{12,44},{16,48},{20,52},{24,56},{28,60},{32,6... | collective-permute-start | bytes 393224 | tf_op jit(solution)/shard_map/ppermute | solution.py:441
  60.7 8.6 %collective-permute-start.10 = (bf16[4,32,512]{2,1,0:T(8,128)(2,1)S(1)}, bf16[4,32,512]{2,1,0:T(8,128)(2,1)S(1)}, u32[]{:S(2)}, u32[]{:S(2)}) collective-permute-start(bf16[4,32,512]{2,1,0:T(8,128)(2,1)S(1)} %get-tuple-element.26), channel_id=1, source_target_pairs={{0,0},{1,32},{2,64},{3,96},{4,4},{5,36},{6,68},{7,100},{8,8},{9,40... | collective-permute-start | bytes 393224 | tf_op jit(solution)/shard_map/ppermute | solution.py:431
  69.3 37.1 %collective-permute-start.14 = (bf16[8,256,128]{2,1,0:T(8,128)(2,1)S(1)}, bf16[8,256,128]{2,1,0:T(8,128)(2,1)}, u32[]{:S(2)}, u32[]{:S(2)}) collective-permute-start(bf16[8,256,128]{2,1,0:T(8,128)(2,1)S(1)} %get-tuple-element.28.z0_ref), channel_id=1, source_target_pairs={{0,32},{4,36},{8,40},{12,44},{16,48},{20,52},{24,56},{28,60},{32,6... | collective-permute-start | bytes 1572872 | tf_op jit(solution)/shard_map/ppermute | solution.py:441
  69.3 38.6 %collective-permute-start.16 = (bf16[8,256,128]{2,1,0:T(8,128)(2,1)S(1)}, bf16[8,256,128]{2,1,0:T(8,128)(2,1)}, u32[]{:S(2)}, u32[]{:S(2)}) collective-permute-start(bf16[8,256,128]{2,1,0:T(8,128)(2,1)S(1)} %get-tuple-element.29.x0_ref), channel_id=1, source_target_pairs={{0,8},{4,12},{8,16},{12,20},{16,24},{20,28},{24,0},{28,4},{32,40},... | collective-permute-start | bytes 1572872 | tf_op jit(solution)/shard_map/ppermute | solution.py:441
  69.5 50.2 %all-to-all-start.1 = ((bf16[128,16,256]{2,1,0:T(8,128)(2,1)}), bf16[128,16,256]{2,1,0:T(8,128)(2,1)S(1)}, u32[]{:S(2)}, u32[]{:S(2)}) async-start(bf16[128,16,256]{2,1,0:T(8,128)(2,1)} %bitcast.25), calls=%async_computation.1 | async-start | bytes 2097152 | tf_op jit(solution)/shard_map/all_to_all | solution.py:479
  84.4 16.9 %collective-permute-start.12 = (bf16[4,32,512]{2,1,0:T(8,128)(2,1)S(1)}, bf16[4,32,512]{2,1,0:T(8,128)(2,1)S(1)}, u32[]{:S(2)}, u32[]{:S(2)}) collective-permute-start(bf16[4,32,512]{2,1,0:T(8,128)(2,1)S(1)} %collective-permute-done.10), channel_id=1, source_target_pairs={{0,2},{1,3},{2,0},{3,1},{4,6},{5,7},{6,4},{7,5},{8,10},{9,11},{10,... | collective-permute-start | bytes 393224 | tf_op jit(solution)/shard_map/ppermute | solution.py:473
  87.4 17.4 %collective-permute-start.11 = (bf16[4,32,512]{2,1,0:T(8,128)(2,1)S(1)}, bf16[4,32,512]{2,1,0:T(8,128)(2,1)S(1)}, u32[]{:S(2)}, u32[]{:S(2)}) collective-permute-start(bf16[4,32,512]{2,1,0:T(8,128)(2,1)S(1)} %collective-permute-done.10), channel_id=1, source_target_pairs={{0,1},{1,0},{2,3},{3,2},{4,5},{5,4},{6,7},{7,6},{8,9},{9,8},{10,11... | collective-permute-start | bytes 393224 | tf_op jit(solution)/shard_map/ppermute | solution.py:472
  88.0 22.4 %collective-permute-start.15 = (bf16[8,256,128]{2,1,0:T(8,128)(2,1)S(1)}, bf16[8,256,128]{2,1,0:T(8,128)(2,1)}, u32[]{:S(2)}, u32[]{:S(2)}) collective-permute-start(bf16[8,256,128]{2,1,0:T(8,128)(2,1)S(1)} %get-tuple-element.28.z0_ref), channel_id=1, source_target_pairs={{0,96},{4,100},{8,104},{12,108},{16,112},{20,116},{24,120},{28,124... | collective-permute-start | bytes 1572872 | tf_op jit(solution)/shard_map/ppermute | solution.py:441
  101.3 12.9 %collective-permute-start.17 = (bf16[8,256,128]{2,1,0:T(8,128)(2,1)S(1)}, bf16[8,256,128]{2,1,0:T(8,128)(2,1)}, u32[]{:S(2)}, u32[]{:S(2)}) collective-permute-start(bf16[8,256,128]{2,1,0:T(8,128)(2,1)S(1)} %get-tuple-element.29.x0_ref), channel_id=1, source_target_pairs={{0,24},{4,28},{8,0},{12,4},{16,8},{20,12},{24,16},{28,20},{32,56},... | collective-permute-start | bytes 1572872 | tf_op jit(solution)/shard_map/ppermute | solution.py:441
  104.8 3.6 %collective-permute-start.13 = (bf16[4,32,512]{2,1,0:T(8,128)(2,1)S(1)}, bf16[4,32,512]{2,1,0:T(8,128)(2,1)S(1)}, u32[]{:S(2)}, u32[]{:S(2)}) collective-permute-start(bf16[4,32,512]{2,1,0:T(8,128)(2,1)S(1)} %collective-permute-done.12), channel_id=1, source_target_pairs={{0,1},{1,0},{2,3},{3,2},{4,5},{5,4},{6,7},{7,6},{8,9},{9,8},{10,11... | collective-permute-start | bytes 393224 | tf_op jit(solution)/shard_map/ppermute | solution.py:474
  106.4 15.9 %collective-permute-start.18 = (bf16[8,256,128]{2,1,0:T(8,128)(2,1)}, bf16[8,256,128]{2,1,0:T(8,128)(2,1)}, u32[]{:S(2)}, u32[]{:S(2)}) collective-permute-start(bf16[8,256,128]{2,1,0:T(8,128)(2,1)} %collective-permute-done.14.z1_ref), channel_id=1, source_target_pairs={{0,32},{4,36},{8,40},{12,44},{16,48},{20,52},{24,56},{28,60},{32,6... | collective-permute-start | bytes 1572872 | tf_op jit(solution)/shard_map/ppermute | solution.py:441
  107.9 14.7 %collective-permute-start.19 = (bf16[8,256,128]{2,1,0:T(8,128)(2,1)}, bf16[8,256,128]{2,1,0:T(8,128)(2,1)}, u32[]{:S(2)}, u32[]{:S(2)}) collective-permute-start(bf16[8,256,128]{2,1,0:T(8,128)(2,1)} %collective-permute-done.16.x1_ref), channel_id=1, source_target_pairs={{0,8},{4,12},{8,16},{12,20},{16,24},{20,28},{24,0},{28,4},{32,40},... | collective-permute-start | bytes 1572872 | tf_op jit(solution)/shard_map/ppermute | solution.py:441
  118.9 0.8 copy-start.7
  122.6 1.1 copy-start.8

commit v4 on v3

--- a/solution.py
+++ b/solution.py
@@ -107,24 +107,28 @@
             query = jnp.concatenate([q_ref[head * DH : (head + 1) * DH, cols], rest[:, cols]], 0)
             return jnp.dot(k_ref[head, :, : DH + 16], query, preferred_element_type=F32)
 
-        def attend(index, scores):
-            head, part = index // 1, index % 1
-            cols = slice(part * (seqs // 1), (part + 1) * (seqs // 1))
-            low, high = head * DH, (head + 1) * DH
+        def soften(scores):
             top = jnp.max(scores, 0, keepdims=True)
-            probs = jnp.exp2(scores - top).astype(BF16)
+            return jnp.exp2(scores - top).astype(BF16)
+
+        def mix(index, probs):
+            low, high = index * DH, (index + 1) * DH
             both = jnp.concatenate([v_ref[low:high, :], ones], 0)
             mixed = jnp.dot(both, probs, preferred_element_type=F32)
             scale = 1.0 / mixed[DH : DH + 1, :]
-            a_ref[low:high, cols] = (mixed[:DH, :] * scale * g_ref[low:high, cols]).astype(BF16)
-
-        count = chans // DH * 1
-        ahead = score(0)
+            a_ref[low:high, :] = (mixed[:DH, :] * scale * g_ref[low:high, :]).astype(BF16)
+
+        count = chans // DH
+        ahead, behind = score(0), None
         for index in range(count):
             now = ahead
             if index + 1 < count:
                 ahead = score(index + 1)
-            attend(index, now)
+            probs = soften(now)
+            if behind is not None:
+                mix(index - 1, behind)
+            behind = probs
+        mix(count - 1, behind)
         update = lax.dot_general(a_ref[...], weight(4), TN, preferred_element_type=F32)
         fresh = (x + update + out_bias_ref[...]).astype(BF16)
         wide = fresh.astype(F32)
@@ -141,7 +145,7 @@
         return 0
 
     right_scratch[...] = jnp.zeros_like(right_scratch)
-    lax.fori_loop(0, steps, body, 0)
+    lax.fori_loop(0, steps, body, 0, unroll=2)
     right_ref[...] = right_scratch[...].astype(BF16).reshape(right_ref.shape)
     for part in range(chans // 128):
         rows_ref[:, part * 128 : (part + 1) * 128] = rows_scratch[part].astype(BF16)
@@ -463,15 +467,14 @@
         ),
         name="join",
     )(*parts)
-    (*mids, left) = lax.optimization_barrier((*mids, left))
+    left_core = lax.ppermute(left, "head", swap_core)
+    left_far = lax.ppermute(left, "head", [(h, h ^ 2) for h in range(n_head)])
+    left_corner = lax.ppermute(left_far, "head", swap_core)
     z_pieces = second_stage(mids[0], 0)
     x_pieces = second_stage(mids[1], 1)
     z_pieces = (*z_pieces, shifted(z_pieces[1], 0, 1))
     x_pieces = (*x_pieces, shifted(x_pieces[1], 1, 1))
 
-    left_core = lax.ppermute(left, "head", swap_core)
-    left_far = lax.ppermute(left, "head", [(h, h ^ 2) for h in range(n_head)])
-    left_corner = lax.ppermute(left_far, "head", swap_core)
     i_rows = mine * n_head
     left = jnp.concatenate([left, left_core, left_far, left_corner], 0)
     left = jnp.swapaxes(left, 0, 1).reshape(CO * i_rows, seqs)

time: 130 us -> 124 us (0.954)
  the two profiles are of different devices: /device:TPU:1 before, /device:TPU:6 now
where the time goes in v4:
time: 124 us
  starting transfers between devices  45.3 us (37%)
  waiting for transfers between devices  40.7 us (33%)
  Pallas kernels  26.9 us (22%)
  local copies, waits for them, and re-layouts  6.27 us (5%)
  other arithmetic  2.81 us (2%)
  between operations  1.78 us (1%)
    ppermute x13, starting transfers between devices, shifted(): return lax.ppermute(value, 'dap', pairs)  21.3 us
    ppermute x13, waiting for transfers between devices, shifted(): return lax.ppermute(value, 'dap', pairs)  15.6 us
    pallas_call x1, Pallas kernels, per_device(): pl.pallas_call(attend_kernel, in_specs=[pl.BlockSpec(memory_space=pltpu.S...  15.2 us
    all_to_all x1, waiting for transfers between devices, per_device(): lax.all_to_all(block, 'dap', split_axis=0, concat_axis=0, tiled=True)  12.3 us
    ppermute x1, waiting for transfers between devices, per_device(): left_far = lax.ppermute(left, 'head', [(h, h ^ 2) for h in range(n_head)])  11.4 us
    all_to_all x1, starting transfers between devices, per_device(): lax.all_to_all(rows.reshape(n_dap * n_head, seqs * mine // (n_dap * n_hea...  8.67 us
    all_to_all x1, starting transfers between devices, per_device(): lax.all_to_all(block, 'dap', split_axis=0, concat_axis=0, tiled=True)  8.41 us
    pallas_call x1, Pallas kernels, per_device(): pl.pallas_call(late_kernel, in_specs=[pl.BlockSpec(memory_space=pltpu.SME...  5.6 us
  transfers between devices with their start and end apart: 22, of which 8 were waited for; matrix products, arithmetic and copies ran while one was open for 4% of the time, Pallas kernels for 5%

profile of v4, /device:TPU:6, one launch (start us, length us, event | category | flops | bytes accessed | tf_op | source)
XLA Modules:
  0.0 123.7 jit_solution(1118568789197301705)
XLA Ops:
  0.6 0.7 fusion.16
  1.3 0.9 pad_maximum_fusion.w0_ref
  2.2 3.1 %collective-permute-start.1 = (bf16[336,256]{1,0:T(8,128)(2,1)S(1)}, bf16[336,256]{1,0:T(8,128)(2,1)S(1)}, u32[]{:S(2)}, u32[]{:S(2)}) collective-permute-start(bf16[336,256]{1,0:T(8,128)(2,1)S(1)} %pad_maximum_fusion.w0_ref), channel_id=1, source_target_pairs={{0,6},{1,7},{2,4},{3,5},{4,2},{5,3},{6,0},{7,1},{8,14},{9,15},{10,... | collective-permute-start | bytes 516104 | tf_op jit(solution)/shard_map/ppermute | solution.py:345
  5.3 0.0 collective-permute-start
  5.4 1.3 %constant_dynamic-slice_fusion = bf16[16,128,256]{2,1,0:T(8,128)(2,1)S(1)} fusion(bf16[16,512,256]{2,1,0:T(8,128)(2,1)} %param.16, s32[]{:T(128)S(6)} %select_n.257), kind=kLoop, calls=%fused_computation.47 | loop fusion | bytes 2097156 | tf_op jit(solution)/shard_map/dynamic_slice | solution.py:356
  6.7 0.0 copy-start.1
  6.7 0.0 copy-start.2
  6.7 0.0 copy-start.3
  6.7 0.0 copy-start.4
  6.7 0.0 copy-start.5
  6.8 0.6 copy.24
  7.3 1.1 copy.19
  8.4 8.4 %all-to-all-start = ((bf16[32,64,256]{2,1,0:T(8,128)(2,1)}), bf16[32,64,256]{2,1,0:T(8,128)(2,1)S(1)}, u32[]{:S(2)}, u32[]{:S(2)}) async-start(bf16[32,64,256]{2,1,0:T(8,128)(2,1)} %bitcast.2), calls=%async_computation | async-start | bytes 2097152 | tf_op jit(solution)/shard_map/all_to_all | solution.py:359
  16.9 0.7 fusion.24
  17.6 0.1 mul.87
  17.7 0.1 mul.88
  17.7 0.1 copy.20
  17.9 0.1 copy.22.keep_col_ref
  18.0 0.1 dynamic_slice.24.amino_ref
  18.2 0.1 collective-permute-start.2
  18.3 1.4 %collective-permute-done.2.w3_ref = bf16[336,256]{1,0:T(8,128)(2,1)S(1)} collective-permute-done((bf16[336,256]{1,0:T(8,128)(2,1)S(1)}, bf16[336,256]{1,0:T(8,128)(2,1)S(1)}, u32[]{:S(2)}, u32[]{:S(2)}) %collective-permute-start.2) | collective-permute-done | bytes 172064 | tf_op jit(solution)/shard_map/ppermute | solution.py:350
  19.7 0.1 add.478.shift_ref
  19.8 12.3 %all-to-all-done.x_ref = bf16[32,64,256]{2,1,0:T(8,128)(2,1)S(1)} async-done(((bf16[32,64,256]{2,1,0:T(8,128)(2,1)}), bf16[32,64,256]{2,1,0:T(8,128)(2,1)S(1)}, u32[]{:S(2)}, u32[]{:S(2)}) %all-to-all-start) | async-done | bytes 1048608 | tf_op jit(solution)/shard_map/all_to_all | solution.py:359
  32.1 15.2 %attend.1 = (bf16[2048,256]{1,0:T(8,128)(2,1)}, bf16[4,32,512]{2,1,0:T(8,128)(2,1)S(1)}, bf16[2,256,128]{2,1,0:T(8,128)(2,1)S(1)}) custom-call(s32[4]{0:T(128)S(1)} %dynamic_slice.24.amino_ref, bf16[32,64,256]{2,1,0:T(8,128)(2,1)S(1)} %all-to-all-done.x_ref, bf16[336,256]{1,0:T(8,128)(2,1)S(1)} %pad_maximum_fusion.w0_ref, ...), custom_call_target="tpu_custom_call" | custom-call | flops 16000000000 | bytes 4194304 | tf_op jit(solution)/shard_map/attend/pallas_call | solution.py:373
  47.3 2.5 %collective-permute-start.7 = (bf16[2,256,128]{2,1,0:T(8,128)(2,1)S(1)}, bf16[2,256,128]{2,1,0:T(8,128)(2,1)S(1)}, u32[]{:S(2)}, u32[]{:S(2)}) collective-permute-start(bf16[2,256,128]{2,1,0:T(8,128)(2,1)S(1)} %get-tuple-element.21), channel_id=1, source_target_pairs={{0,4},{4,0},{8,12},{12,8},{16,20},{20,16},{24,28},{28,24},{32,36},... | collective-permute-start | bytes 393224 | tf_op jit(solution)/shard_map/ppermute | solution.py:445
  49.9 2.9 %collective-permute-done.7 = bf16[2,256,128]{2,1,0:T(8,128)(2,1)S(1)} collective-permute-done((bf16[2,256,128]{2,1,0:T(8,128)(2,1)S(1)}, bf16[2,256,128]{2,1,0:T(8,128)(2,1)S(1)}, u32[]{:S(2)}, u32[]{:S(2)}) %collective-permute-start.7) | collective-permute-done | bytes 131104 | tf_op jit(solution)/shard_map/ppermute | solution.py:445
  52.9 3.1 %collective-permute-start.10 = (bf16[2,256,128]{2,1,0:T(8,128)(2,1)S(1)}, bf16[2,256,128]{2,1,0:T(8,128)(2,1)S(1)}, u32[]{:S(2)}, u32[]{:S(2)}) collective-permute-start(bf16[2,256,128]{2,1,0:T(8,128)(2,1)S(1)} %pad_maximum_fusion.1.refs_0_), channel_id=1, source_target_pairs={{0,16},{4,20},{8,24},{12,28},{16,0},{20,4},{24,8},{28,12},{32,48},... | collective-permute-start | bytes 393224 | tf_op jit(solution)/shard_map/ppermute | solution.py:445
  55.9 0.8 collective-permute-start.9
  56.8 2.4 %collective-permute-start.8 = (bf16[2,256,128]{2,1,0:T(8,128)(2,1)S(1)}, bf16[2,256,128]{2,1,0:T(8,128)(2,1)S(1)}, u32[]{:S(2)}, u32[]{:S(2)}) collective-permute-start(bf16[2,256,128]{2,1,0:T(8,128)(2,1)S(1)} %pad_maximum_fusion.1.refs_0_), channel_id=1, source_target_pairs={{0,8},{4,12},{8,16},{12,20},{16,24},{20,28},{24,0},{28,4},{32,40},... | collective-permute-start | bytes 393224 | tf_op jit(solution)/shard_map/ppermute | solution.py:445
  59.2 0.9 collective-permute-start.13
  60.0 1.2 collective-permute-start.12
  61.2 0.8 collective-permute-start.11
  62.0 0.0 collective-permute-done.9.refs_2_
  62.1 0.7 collective-permute-start.3
  62.8 3.0 %collective-permute-done.13.refs_7_ = bf16[2,256,128]{2,1,0:T(8,128)(2,1)S(1)} collective-permute-done((bf16[2,256,128]{2,1,0:T(8,128)(2,1)S(1)}, bf16[2,256,128]{2,1,0:T(8,128)(2,1)S(1)}, u32[]{:S(2)}, u32[]{:S(2)}) %collective-permute-start.13) | collective-permute-done | bytes 131104 | tf_op jit(solution)/shard_map/ppermute | solution.py:445
  65.7 1.7 %collective-permute-done.11.refs_5_ = bf16[2,256,128]{2,1,0:T(8,128)(2,1)S(1)} collective-permute-done((bf16[2,256,128]{2,1,0:T(8,128)(2,1)S(1)}, bf16[2,256,128]{2,1,0:T(8,128)(2,1)S(1)}, u32[]{:S(2)}, u32[]{:S(2)}) %collective-permute-start.11) | collective-permute-done | bytes 131104 | tf_op jit(solution)/shard_map/ppermute | solution.py:445
  67.4 0.1 join.1
  67.4 0.3 collective-permute-start.14
  67.7 1.3 %collective-permute-start.16 = (bf16[8,256,128]{2,1,0:T(8,128)(2,1)S(1)}, bf16[8,256,128]{2,1,0:T(8,128)(2,1)}, u32[]{:S(2)}, u32[]{:S(2)}) collective-permute-start(bf16[8,256,128]{2,1,0:T(8,128)(2,1)S(1)} %get-tuple-element.23.x0_ref), channel_id=1, source_target_pairs={{0,8},{4,12},{8,16},{12,20},{16,24},{20,28},{24,0},{28,4},{32,40},... | collective-permute-start | bytes 1572872 | tf_op jit(solution)/shard_map/ppermute | solution.py:445
  69.1 8.7 %all-to-all-start.1 = ((bf16[128,16,256]{2,1,0:T(8,128)(2,1)}), bf16[128,16,256]{2,1,0:T(8,128)(2,1)S(1)}, u32[]{:S(2)}, u32[]{:S(2)}) async-start(bf16[128,16,256]{2,1,0:T(8,128)(2,1)} %bitcast.25), calls=%async_computation.1 | async-start | bytes 2097152 | tf_op jit(solution)/shard_map/all_to_all | solution.py:482
  77.7 3.1 %collective-permute-start.5 = (bf16[4,32,512]{2,1,0:T(8,128)(2,1)S(1)}, bf16[4,32,512]{2,1,0:T(8,128)(2,1)S(1)}, u32[]{:S(2)}, u32[]{:S(2)}) collective-permute-start(bf16[4,32,512]{2,1,0:T(8,128)(2,1)S(1)} %collective-permute-done.3), channel_id=1, source_target_pairs={{0,2},{1,3},{2,0},{3,1},{4,6},{5,7},{6,4},{7,5},{8,10},{9,11},{10,... | collective-permute-start | bytes 393224 | tf_op jit(solution)/shard_map/ppermute | solution.py:471
  80.8 3.5 %collective-permute-start.15 = (bf16[8,256,128]{2,1,0:T(8,128)(2,1)S(1)}, bf16[8,256,128]{2,1,0:T(8,128)(2,1)}, u32[]{:S(2)}, u32[]{:S(2)}) collective-permute-start(bf16[8,256,128]{2,1,0:T(8,128)(2,1)S(1)} %get-tuple-element.22.z0_ref), channel_id=1, source_target_pairs={{0,96},{4,100},{8,104},{12,108},{16,112},{20,116},{24,120},{28,124... | collective-permute-start | bytes 1572872 | tf_op jit(solution)/shard_map/ppermute | solution.py:445
  84.3 11.4 %collective-permute-done.5 = bf16[4,32,512]{2,1,0:T(8,128)(2,1)S(1)} collective-permute-done((bf16[4,32,512]{2,1,0:T(8,128)(2,1)S(1)}, bf16[4,32,512]{2,1,0:T(8,128)(2,1)S(1)}, u32[]{:S(2)}, u32[]{:S(2)}) %collective-permute-start.5) | collective-permute-done | bytes 131104 | tf_op jit(solution)/shard_map/ppermute | solution.py:471
  95.7 0.5 collective-permute-start.17
  96.3 0.1 dynamic-slice_convert_fusion.1
  97.0 0.1 fusion.25
  97.1 0.0 collective-permute-start.6
  97.1 0.1 maximum_multiply_fusion
  97.3 0.1 mul.206
  97.4 1.4 %collective-permute-start.18 = (bf16[8,256,128]{2,1,0:T(8,128)(2,1)}, bf16[8,256,128]{2,1,0:T(8,128)(2,1)}, u32[]{:S(2)}, u32[]{:S(2)}) collective-permute-start(bf16[8,256,128]{2,1,0:T(8,128)(2,1)} %collective-permute-done.14.z1_ref), channel_id=1, source_target_pairs={{0,32},{4,36},{8,40},{12,44},{16,48},{20,52},{24,56},{28,60},{32,6... | collective-permute-start | bytes 1572872 | tf_op jit(solution)/shard_map/ppermute | solution.py:445
  98.9 2.5 %collective-permute-start.19 = (bf16[8,256,128]{2,1,0:T(8,128)(2,1)}, bf16[8,256,128]{2,1,0:T(8,128)(2,1)}, u32[]{:S(2)}, u32[]{:S(2)}) collective-permute-start(bf16[8,256,128]{2,1,0:T(8,128)(2,1)} %collective-permute-done.16.x1_ref), channel_id=1, source_target_pairs={{0,8},{4,12},{8,16},{12,20},{16,24},{20,28},{24,0},{28,4},{32,40},... | collective-permute-start | bytes 1572872 | tf_op jit(solution)/shard_map/ppermute | solution.py:445
  101.4 0.1 dynamic-slice_convert_fusion
  101.4 0.1 mul.208
  101.5 0.1 fusion.1.inverse_ref
  101.7 0.1 stack.202.place_ref
  101.8 0.1 maximum_bitcast_fusion
  101.9 0.3 copy.23
  102.2 1.1 collective-permute-done.15.z2_ref
  103.3 6.8 %collective-permute-done.17.x2_ref = bf16[8,256,128]{2,1,0:T(8,128)(2,1)} collective-permute-done((bf16[8,256,128]{2,1,0:T(8,128)(2,1)S(1)}, bf16[8,256,128]{2,1,0:T(8,128)(2,1)}, u32[]{:S(2)}, u32[]{:S(2)}) %collective-permute-start.17) | collective-permute-done | bytes 524320 | tf_op jit(solution)/shard_map/ppermute | solution.py:445
  110.2 4.6 %early.1.part_ref = f32[1152,128]{1,0:T(8,128)S(1)} custom-call(s32[36]{0:T(128)S(1)} %stack.202.place_ref, bf16[512,512]{1,0:T(8,128)(2,1)S(1)} %bitcast.86, f32[1,128]{1,0:T(1,128)S(1)} %bitcast.95, f32[512,4]{1,0:T(8,128)S(1)} %fusion.1.inverse_ref, f32[1024,128]{1,0:T(8,128)S(1)} %copy-done, bf16[8,256,128]{2,1,0:T(8,128)(2,1)S(1)} %get-tuple-element.22.z0_ref, ...), custom_call_target="tpu_custom_call" | custom-call | flops 3000000000 | bytes 6291456 | tf_op jit(solution)/shard_map/early/pallas_call | solution.py:514
  114.8 0.8 copy-done.7
  115.6 1.5 %arrange.1 = bf16[4,512,256]{2,1,0:T(8,128)(2,1)} custom-call(bf16[128,16,256]{2,1,0:T(8,128)(2,1)S(1)} %all-to-all-done.1.back_ref), custom_call_target="tpu_custom_call" | custom-call | flops 500000000 | bytes 2097152 | tf_op jit(solution)/shard_map/arrange/pallas_call | solution.py:532
  117.1 1.1 copy-done.8
  118.1 5.6 %late.1 = f32[16,128,128]{2,1,0:T(8,128)} custom-call(s32[36]{0:T(128)S(1)} %stack.202.place_ref, bf16[512,512]{1,0:T(8,128)(2,1)S(1)} %bitcast.87, f32[1,128]{1,0:T(1,128)S(1)} %bitcast.96, f32[512,4]{1,0:T(8,128)S(1)} %fusion.1.inverse_ref, f32[1024,128]{1,0:T(8,128)S(1)} %copy-done, f32[1152,128]{1,0:T(8,128)S(1)} %copy-done.8, ...), custom_call_target="tpu_custom_call" | custom-call | flops 3000000000 | bytes 6291456 | tf_op jit(solution)/shard_map/late/pallas_call | solution.py:543
  (45 shorter events, 0.2 us)
Async XLA Ops:
  2.2 15.9 %collective-permute-start.1 = (bf16[336,256]{1,0:T(8,128)(2,1)S(1)}, bf16[336,256]{1,0:T(8,128)(2,1)S(1)}, u32[]{:S(2)}, u32[]{:S(2)}) collective-permute-start(bf16[336,256]{1,0:T(8,128)(2,1)S(1)} %pad_maximum_fusion.w0_ref), channel_id=1, source_target_pairs={{0,6},{1,7},{2,4},{3,5},{4,2},{5,3},{6,0},{7,1},{8,14},{9,15},{10,... | collective-permute-start | bytes 516104 | tf_op jit(solution)/shard_map/ppermute | solution.py:345
  5.3 12.9 %collective-permute-start = (bf16[336,256]{1,0:T(8,128)(2,1)S(1)}, bf16[336,256]{1,0:T(8,128)(2,1)S(1)}, u32[]{:S(2)}, u32[]{:S(2)}) collective-permute-start(bf16[336,256]{1,0:T(8,128)(2,1)S(1)} %pad_maximum_fusion.w0_ref), channel_id=1, source_target_pairs={{0,1},{1,0},{2,3},{3,2},{4,5},{5,4},{6,7},{7,6},{8,9},{9,8},{10,11... | collective-permute-start | bytes 516104 | tf_op jit(solution)/shard_map/ppermute | solution.py:348
  5.3 11.6 %copy-start.10 = (s32[512]{0:T(512)S(1)}, s32[512]{0:T(512)}, u32[]{:S(2)}) copy-start(s32[512]{0:T(512)} %param.17) | copy-start | bytes 6148
  5.3 12.2 %copy-start.9 = (bf16[256,2,32]{0,2,1:T(8,128)(2,1)S(1)}, bf16[256,2,32]{0,2,1:T(8,128)(2,1)}, u32[]{:S(2)}) copy-start(bf16[256,2,32]{0,2,1:T(8,128)(2,1)} %param.27) | copy-start | bytes 98308
  5.3 12.7 %copy-start.11 = (s32[512]{0:T(512)S(1)}, s32[512]{0:T(512)}, u32[]{:S(2)}) copy-start(s32[512]{0:T(512)} %param.18) | copy-start | bytes 6148
  6.7 25.4 %copy-start.1 = (f32[256]{0:T(256)S(1)}, f32[256]{0:T(256)}, u32[]{:S(2)}) copy-start(f32[256]{0:T(256)} %param.19) | copy-start | bytes 3076
  6.7 25.4 %copy-start.2 = (f32[256]{0:T(256)S(1)}, f32[256]{0:T(256)}, u32[]{:S(2)}) copy-start(f32[256]{0:T(256)} %param.20) | copy-start | bytes 3076
  6.7 25.4 %copy-start.3 = (f32[256]{0:T(256)S(1)}, f32[256]{0:T(256)}, u32[]{:S(2)}) copy-start(f32[256]{0:T(256)} %param.24) | copy-start | bytes 3076
  6.7 25.4 %copy-start.4 = (f32[256]{0:T(256)S(1)}, f32[256]{0:T(256)}, u32[]{:S(2)}) copy-start(f32[256]{0:T(256)} %param.25) | copy-start | bytes 3076
  6.7 25.4 %copy-start.5 = (f32[256]{0:T(256)S(1)}, f32[256]{0:T(256)}, u32[]{:S(2)}) copy-start(f32[256]{0:T(256)} %param.26) | copy-start | bytes 3076
  8.4 23.7 %all-to-all-start = ((bf16[32,64,256]{2,1,0:T(8,128)(2,1)}), bf16[32,64,256]{2,1,0:T(8,128)(2,1)S(1)}, u32[]{:S(2)}, u32[]{:S(2)}) async-start(bf16[32,64,256]{2,1,0:T(8,128)(2,1)} %bitcast.2), calls=%async_computation | async-start | bytes 2097152 | tf_op jit(solution)/shard_map/all_to_all | solution.py:359
  18.2 1.5 %collective-permute-start.2 = (bf16[336,256]{1,0:T(8,128)(2,1)S(1)}, bf16[336,256]{1,0:T(8,128)(2,1)S(1)}, u32[]{:S(2)}, u32[]{:S(2)}) collective-permute-start(bf16[336,256]{1,0:T(8,128)(2,1)S(1)} %collective-permute-done.1.w2_ref), channel_id=1, source_target_pairs={{0,1},{1,0},{2,3},{3,2},{4,5},{5,4},{6,7},{7,6},{8,9},{9,8},{10,11... | collective-permute-start | bytes 516104 | tf_op jit(solution)/shard_map/ppermute | solution.py:350
  47.3 62.8 %copy-start = (f32[1024,128]{1,0:T(8,128)S(1)}, f32[1024,128]{1,0:T(8,128)}, u32[]{:S(2)}) copy-start(f32[1024,128]{1,0:T(8,128)} %compact_ref.3) | copy-start | bytes 1572868
  47.3 62.8 %copy-start.6 = (f32[128]{0:T(128)S(1)}, f32[128]{0:T(128)}, u32[]{:S(2)}) copy-start(f32[128]{0:T(128)} %param.29) | copy-start | bytes 1540
  47.3 5.5 %collective-permute-start.7 = (bf16[2,256,128]{2,1,0:T(8,128)(2,1)S(1)}, bf16[2,256,128]{2,1,0:T(8,128)(2,1)S(1)}, u32[]{:S(2)}, u32[]{:S(2)}) collective-permute-start(bf16[2,256,128]{2,1,0:T(8,128)(2,1)S(1)} %get-tuple-element.21), channel_id=1, source_target_pairs={{0,4},{4,0},{8,12},{12,8},{16,20},{20,16},{24,28},{28,24},{32,36},... | collective-permute-start | bytes 393224 | tf_op jit(solution)/shard_map/ppermute | solution.py:445
  52.9 8.3 %collective-permute-start.10 = (bf16[2,256,128]{2,1,0:T(8,128)(2,1)S(1)}, bf16[2,256,128]{2,1,0:T(8,128)(2,1)S(1)}, u32[]{:S(2)}, u32[]{:S(2)}) collective-permute-start(bf16[2,256,128]{2,1,0:T(8,128)(2,1)S(1)} %pad_maximum_fusion.1.refs_0_), channel_id=1, source_target_pairs={{0,16},{4,20},{8,24},{12,28},{16,0},{20,4},{24,8},{28,12},{32,48},... | collective-permute-start | bytes 393224 | tf_op jit(solution)/shard_map/ppermute | solution.py:445
  55.9 6.2 %collective-permute-start.9 = (bf16[2,256,128]{2,1,0:T(8,128)(2,1)S(1)}, bf16[2,256,128]{2,1,0:T(8,128)(2,1)S(1)}, u32[]{:S(2)}, u32[]{:S(2)}) collective-permute-start(bf16[2,256,128]{2,1,0:T(8,128)(2,1)S(1)} %pad_maximum_fusion.1.refs_0_), channel_id=1, source_target_pairs={{0,24},{4,28},{8,0},{12,4},{16,8},{20,12},{24,16},{28,20},{32,56},... | collective-permute-start | bytes 393224 | tf_op jit(solution)/shard_map/ppermute | solution.py:445
  56.8 6.0 %collective-permute-start.8 = (bf16[2,256,128]{2,1,0:T(8,128)(2,1)S(1)}, bf16[2,256,128]{2,1,0:T(8,128)(2,1)S(1)}, u32[]{:S(2)}, u32[]{:S(2)}) collective-permute-start(bf16[2,256,128]{2,1,0:T(8,128)(2,1)S(1)} %pad_maximum_fusion.1.refs_0_), channel_id=1, source_target_pairs={{0,8},{4,12},{8,16},{12,20},{16,24},{20,28},{24,0},{28,4},{32,40},... | collective-permute-start | bytes 393224 | tf_op jit(solution)/shard_map/ppermute | solution.py:445
  59.2 6.6 %collective-permute-start.13 = (bf16[2,256,128]{2,1,0:T(8,128)(2,1)S(1)}, bf16[2,256,128]{2,1,0:T(8,128)(2,1)S(1)}, u32[]{:S(2)}, u32[]{:S(2)}) collective-permute-start(bf16[2,256,128]{2,1,0:T(8,128)(2,1)S(1)} %pad_maximum_fusion.2.refs_4_), channel_id=1, source_target_pairs={{0,64},{4,68},{8,72},{12,76},{16,80},{20,84},{24,88},{28,92},{32,9... | collective-permute-start | bytes 393224 | tf_op jit(solution)/shard_map/ppermute | solution.py:445
  60.0 5.7 %collective-permute-start.12 = (bf16[2,256,128]{2,1,0:T(8,128)(2,1)S(1)}, bf16[2,256,128]{2,1,0:T(8,128)(2,1)S(1)}, u32[]{:S(2)}, u32[]{:S(2)}) collective-permute-start(bf16[2,256,128]{2,1,0:T(8,128)(2,1)S(1)} %pad_maximum_fusion.2.refs_4_), channel_id=1, source_target_pairs={{0,96},{4,100},{8,104},{12,108},{16,112},{20,116},{24,120},{28,124... | collective-permute-start | bytes 393224 | tf_op jit(solution)/shard_map/ppermute | solution.py:445
  61.2 6.2 %collective-permute-start.11 = (bf16[2,256,128]{2,1,0:T(8,128)(2,1)S(1)}, bf16[2,256,128]{2,1,0:T(8,128)(2,1)S(1)}, u32[]{:S(2)}, u32[]{:S(2)}) collective-permute-start(bf16[2,256,128]{2,1,0:T(8,128)(2,1)S(1)} %pad_maximum_fusion.2.refs_4_), channel_id=1, source_target_pairs={{0,32},{4,36},{8,40},{12,44},{16,48},{20,52},{24,56},{28,60},{32,6... | collective-permute-start | bytes 393224 | tf_op jit(solution)/shard_map/ppermute | solution.py:445
  62.1 15.6 %collective-permute-start.3 = (bf16[4,32,512]{2,1,0:T(8,128)(2,1)S(1)}, bf16[4,32,512]{2,1,0:T(8,128)(2,1)S(1)}, u32[]{:S(2)}, u32[]{:S(2)}) collective-permute-start(bf16[4,32,512]{2,1,0:T(8,128)(2,1)S(1)} %get-tuple-element.20), channel_id=1, source_target_pairs={{0,0},{1,32},{2,64},{3,96},{4,4},{5,36},{6,68},{7,100},{8,8},{9,40... | collective-permute-start | bytes 393224 | tf_op jit(solution)/shard_map/ppermute | solution.py:435
  67.4 30.0 %collective-permute-start.14 = (bf16[8,256,128]{2,1,0:T(8,128)(2,1)S(1)}, bf16[8,256,128]{2,1,0:T(8,128)(2,1)}, u32[]{:S(2)}, u32[]{:S(2)}) collective-permute-start(bf16[8,256,128]{2,1,0:T(8,128)(2,1)S(1)} %get-tuple-element.22.z0_ref), channel_id=1, source_target_pairs={{0,32},{4,36},{8,40},{12,44},{16,48},{20,52},{24,56},{28,60},{32,6... | collective-permute-start | bytes 1572872 | tf_op jit(solution)/shard_map/ppermute | solution.py:445
  67.7 31.2 %collective-permute-start.16 = (bf16[8,256,128]{2,1,0:T(8,128)(2,1)S(1)}, bf16[8,256,128]{2,1,0:T(8,128)(2,1)}, u32[]{:S(2)}, u32[]{:S(2)}) collective-permute-start(bf16[8,256,128]{2,1,0:T(8,128)(2,1)S(1)} %get-tuple-element.23.x0_ref), channel_id=1, source_target_pairs={{0,8},{4,12},{8,16},{12,20},{16,24},{20,28},{24,0},{28,4},{32,40},... | collective-permute-start | bytes 1572872 | tf_op jit(solution)/shard_map/ppermute | solution.py:445
  69.1 46.5 %all-to-all-start.1 = ((bf16[128,16,256]{2,1,0:T(8,128)(2,1)}), bf16[128,16,256]{2,1,0:T(8,128)(2,1)S(1)}, u32[]{:S(2)}, u32[]{:S(2)}) async-start(bf16[128,16,256]{2,1,0:T(8,128)(2,1)} %bitcast.25), calls=%async_computation.1 | async-start | bytes 2097152 | tf_op jit(solution)/shard_map/all_to_all | solution.py:482
  77.7 18.0 %collective-permute-start.5 = (bf16[4,32,512]{2,1,0:T(8,128)(2,1)S(1)}, bf16[4,32,512]{2,1,0:T(8,128)(2,1)S(1)}, u32[]{:S(2)}, u32[]{:S(2)}) collective-permute-start(bf16[4,32,512]{2,1,0:T(8,128)(2,1)S(1)} %collective-permute-done.3), channel_id=1, source_target_pairs={{0,2},{1,3},{2,0},{3,1},{4,6},{5,7},{6,4},{7,5},{8,10},{9,11},{10,... | collective-permute-start | bytes 393224 | tf_op jit(solution)/shard_map/ppermute | solution.py:471
  80.8 16.3 %collective-permute-start.4 = (bf16[4,32,512]{2,1,0:T(8,128)(2,1)S(1)}, bf16[4,32,512]{2,1,0:T(8,128)(2,1)S(1)}, u32[]{:S(2)}, u32[]{:S(2)}) collective-permute-start(bf16[4,32,512]{2,1,0:T(8,128)(2,1)S(1)} %collective-permute-done.3), channel_id=1, source_target_pairs={{0,1},{1,0},{2,3},{3,2},{4,5},{5,4},{6,7},{7,6},{8,9},{9,8},{10,11... | collective-permute-start | bytes 393224 | tf_op jit(solution)/shard_map/ppermute | solution.py:470
  80.8 22.5 %collective-permute-start.15 = (bf16[8,256,128]{2,1,0:T(8,128)(2,1)S(1)}, bf16[8,256,128]{2,1,0:T(8,128)(2,1)}, u32[]{:S(2)}, u32[]{:S(2)}) collective-permute-start(bf16[8,256,128]{2,1,0:T(8,128)(2,1)S(1)} %get-tuple-element.22.z0_ref), channel_id=1, source_target_pairs={{0,96},{4,100},{8,104},{12,108},{16,112},{20,116},{24,120},{28,124... | collective-permute-start | bytes 1572872 | tf_op jit(solution)/shard_map/ppermute | solution.py:445
  95.7 14.4 %collective-permute-start.17 = (bf16[8,256,128]{2,1,0:T(8,128)(2,1)S(1)}, bf16[8,256,128]{2,1,0:T(8,128)(2,1)}, u32[]{:S(2)}, u32[]{:S(2)}) collective-permute-start(bf16[8,256,128]{2,1,0:T(8,128)(2,1)S(1)} %get-tuple-element.23.x0_ref), channel_id=1, source_target_pairs={{0,24},{4,28},{8,0},{12,4},{16,8},{20,12},{24,16},{28,20},{32,56},... | collective-permute-start | bytes 1572872 | tf_op jit(solution)/shard_map/ppermute | solution.py:445
  97.1 4.7 %collective-permute-start.6 = (bf16[4,32,512]{2,1,0:T(8,128)(2,1)S(1)}, bf16[4,32,512]{2,1,0:T(8,128)(2,1)S(1)}, u32[]{:S(2)}, u32[]{:S(2)}) collective-permute-start(bf16[4,32,512]{2,1,0:T(8,128)(2,1)S(1)} %collective-permute-done.5), channel_id=1, source_target_pairs={{0,1},{1,0},{2,3},{3,2},{4,5},{5,4},{6,7},{7,6},{8,9},{9,8},{10,11... | collective-permute-start | bytes 393224 | tf_op jit(solution)/shard_map/ppermute | solution.py:472
  97.4 19.7 %collective-permute-start.18 = (bf16[8,256,128]{2,1,0:T(8,128)(2,1)}, bf16[8,256,128]{2,1,0:T(8,128)(2,1)}, u32[]{:S(2)}, u32[]{:S(2)}) collective-permute-start(bf16[8,256,128]{2,1,0:T(8,128)(2,1)} %collective-permute-done.14.z1_ref), channel_id=1, source_target_pairs={{0,32},{4,36},{8,40},{12,44},{16,48},{20,52},{24,56},{28,60},{32,6... | collective-permute-start | bytes 1572872 | tf_op jit(solution)/shard_map/ppermute | solution.py:445
  98.9 18.2 %collective-permute-start.19 = (bf16[8,256,128]{2,1,0:T(8,128)(2,1)}, bf16[8,256,128]{2,1,0:T(8,128)(2,1)}, u32[]{:S(2)}, u32[]{:S(2)}) collective-permute-start(bf16[8,256,128]{2,1,0:T(8,128)(2,1)} %collective-permute-done.16.x1_ref), channel_id=1, source_target_pairs={{0,8},{4,12},{8,16},{12,20},{16,24},{20,28},{24,0},{28,4},{32,40},... | collective-permute-start | bytes 1572872 | tf_op jit(solution)/shard_map/ppermute | solution.py:445
  114.7 0.8 copy-start.7
  117.1 1.1 copy-start.8

commit v5 on v4

--- a/solution.py
+++ b/solution.py
@@ -162,8 +162,7 @@
 
 
 def project(slots, groups, z_refs, x_refs, left_ref, bias_ref, inverse_ref, compact_ref,
-            place_ref, mid_ref, weight_ref, store):
-    lanes = z_refs[0].shape[2]
+            place_ref, mid_ref, weight_ref, store, lanes):
     depth = bias_ref.shape[1]
     inner = lanes // CO
     rows = left_ref.shape[0] // CO
@@ -258,7 +257,18 @@
         part_ref[at : at + rows, :] = value
 
     project(EARLY, 3, (z0_ref, z1_ref, z2_ref), (x0_ref, x1_ref, x2_ref), left_ref, bias_ref,
-            inverse_ref, compact_ref, place_ref, mid_ref, weight_ref, store)
+            inverse_ref, compact_ref, place_ref, mid_ref, weight_ref, store,
+            lanes=z0_ref.shape[2])
+
+
+class Tail:
+    def __init__(self, first, *refs):
+        self.first, self.refs = first, refs
+
+    def __getitem__(self, index):
+        index -= self.first
+        count = self.refs[0].shape[0]
+        return self.refs[index // count][index % count]
 
 
 def late_kernel(
@@ -271,16 +281,21 @@
     z0_ref,
     z1_ref,
     z2_ref,
-    z3_ref,
+    za_ref,
+    zb_ref,
     x0_ref,
     x1_ref,
     x2_ref,
-    x3_ref,
+    xa_ref,
+    xb_ref,
     out_ref,
     mid_ref,
     weight_ref,
     turn_ref,
 ):
+    first = 3 * z0_ref.shape[0]
+    z_refs = (*[Tail(first, ref) for ref in (z0_ref, z1_ref, z2_ref)], Tail(0, za_ref, zb_ref))
+    x_refs = (*[Tail(first, ref) for ref in (x0_ref, x1_ref, x2_ref)], Tail(0, xa_ref, xb_ref))
     rows = left_ref.shape[0] // CO
     inner = z0_ref.shape[2] // CO
 
@@ -288,8 +303,8 @@
         at = pl.multiple_of((place * inner + k) * rows, rows)
         turn_ref[pl.ds(at, rows), :] = value
 
-    project(LATE, 2, (z0_ref, z1_ref, z2_ref, z3_ref), (x0_ref, x1_ref, x2_ref, x3_ref),
-            left_ref, bias_ref, inverse_ref, compact_ref, place_ref, mid_ref, weight_ref, store)
+    project(LATE, 2, z_refs, x_refs, left_ref, bias_ref, inverse_ref, compact_ref, place_ref,
+            mid_ref, weight_ref, store, lanes=z0_ref.shape[2])
     block = inner * rows
     for n, (dz, dx, dy) in enumerate(EARLY):
         at = pl.multiple_of(place_ref[(dz * 4 + dx) * 2 + dy] * block, block)
@@ -300,7 +315,7 @@
         out_ref[head * inner + i % inner] = turn_ref[pl.ds(i, columns, stride=rows), :]
 
 
-def whole():
+def whole(shape):
     return pl.BlockSpec(memory_space=pltpu.VMEM)
 
 
@@ -374,20 +389,24 @@
         attend_kernel,
         in_specs=[
             pl.BlockSpec(memory_space=pltpu.SMEM),
-            whole(),
-            *[whole()] * n_head,
-            whole(),
-            whole(),
-            whole(),
-            whole(),
-            whole(),
-            whole(),
-            whole(),
-            whole(),
-            whole(),
-            whole(),
-        ],
-        out_specs=[whole(), whole(), whole()],
+            whole(block.shape),
+            *[whole(bundle.shape)] * n_head,
+            whole((chans, 1)),
+            whole((1, chans)),
+            whole((1, chans)),
+            whole((1, chans)),
+            whole((1, chans)),
+            whole((1, chans)),
+            whole((seqs, 1)),
+            whole((1, seqs)),
+            whole((mine, chans, lanes)),
+            whole((CO, chans)),
+        ],
+        out_specs=[
+            whole((seqs * mine, chans)),
+            whole((mine, CO, seqs)),
+            whole((2, seqs // 2, lanes)),
+        ],
         out_shape=[
             jax.ShapeDtypeStruct((seqs * mine, chans), BF16),
             jax.ShapeDtypeStruct((mine, CO, seqs), BF16),
@@ -472,8 +491,13 @@
     left_corner = lax.ppermute(left_far, "head", swap_core)
     z_pieces = second_stage(mids[0], 0)
     x_pieces = second_stage(mids[1], 1)
-    z_pieces = (*z_pieces, shifted(z_pieces[1], 0, 1))
-    x_pieces = (*x_pieces, shifted(x_pieces[1], 1, 1))
+    half = len(STEPS) * ny // 2
+
+    def forward(pieces, axis):
+        return (*pieces, shifted(pieces[1][:half], axis, 1), shifted(pieces[2][half:], axis, -1))
+
+    z_pieces = forward(z_pieces, 0)
+    x_pieces = forward(x_pieces, 1)
 
     i_rows = mine * n_head
     left = jnp.concatenate([left, left_core, left_far, left_corner], 0)
@@ -540,11 +564,18 @@
         ),
         name="arrange",
     )(back)
+    early, alignment = lax.optimization_barrier((early, alignment))
+    part_specs = [
+        pl.BlockSpec((ny, *z_pieces[0].shape[1:]), lambda _: (len(STEPS) - 1, 0, 0))
+    ] * 3 + [pl.BlockSpec(memory_space=pltpu.VMEM)] * 2
     pair = pl.pallas_call(
         late_kernel,
+        grid=(1,),
         in_specs=[
             pl.BlockSpec(memory_space=pltpu.SMEM),
-            *[pl.BlockSpec(memory_space=pltpu.VMEM)] * 13,
+            *[pl.BlockSpec(memory_space=pltpu.VMEM)] * 5,
+            *part_specs,
+            *part_specs,
         ],
         out_specs=pl.BlockSpec(memory_space=pltpu.VMEM),
         out_shape=jax.ShapeDtypeStruct((i_rows, col_width, depth), F32),

time: 124 us -> 132 us (1.065)
  the two profiles are of different devices: /device:TPU:6 before, /device:TPU:0 now
where the time goes in v5:
time: 132 us
  starting transfers between devices  48.6 us (37%)
  waiting for transfers between devices  39.3 us (30%)
  Pallas kernels  27.3 us (21%)
  local copies, waits for them, and re-layouts  12.1 us (9%)
  other arithmetic  2.81 us (2%)
  between operations  1.79 us (1%)
    ppermute x15, starting transfers between devices, shifted(): return lax.ppermute(value, 'dap', pairs)  24.7 us
    ppermute x15, waiting for transfers between devices, shifted(): return lax.ppermute(value, 'dap', pairs)  22.8 us
    pallas_call x1, Pallas kernels, per_device(): pl.pallas_call(attend_kernel, in_specs=[pl.BlockSpec(memory_space=pltpu.S...  15.2 us
    all_to_all x1, waiting for transfers between devices, per_device(): lax.all_to_all(block, 'dap', split_axis=0, concat_axis=0, tiled=True)  15.1 us
    all_to_all x1, starting transfers between devices, per_device(): lax.all_to_all(rows.reshape(n_dap * n_head, seqs * mine // (n_dap * n_hea...  8.58 us
    all_to_all x1, starting transfers between devices, per_device(): lax.all_to_all(block, 'dap', split_axis=0, concat_axis=0, tiled=True)  8.16 us
    pallas_call x1, Pallas kernels, per_device(): pl.pallas_call(late_kernel, grid=(1,), in_specs=[pl.BlockSpec(memory_spac...  5.11 us
    unnamed x27, local copies, waits for them, and re-layouts  4.58 us
  transfers between devices with their start and end apart: 24, of which 7 were waited for; matrix products, arithmetic and copies ran while one was open for 7% of the time, Pallas kernels for 5%

profile of v5, /device:TPU:0, one launch (start us, length us, event | category | flops | bytes accessed | tf_op | source)
XLA Modules:
  0.0 131.9 jit_solution(18142935264994520130)
XLA Ops:
  0.6 0.7 fusion.16
  1.3 0.9 pad_maximum_fusion.w0_ref
  2.2 0.1 collective-permute-start
  2.3 3.2 %collective-permute-start.1 = (bf16[336,256]{1,0:T(8,128)(2,1)S(1)}, bf16[336,256]{1,0:T(8,128)(2,1)S(1)}, u32[]{:S(2)}, u32[]{:S(2)}) collective-permute-start(bf16[336,256]{1,0:T(8,128)(2,1)S(1)} %pad_maximum_fusion.w0_ref), channel_id=1, source_target_pairs={{0,6},{1,7},{2,4},{3,5},{4,2},{5,3},{6,0},{7,1},{8,14},{9,15},{10,... | collective-permute-start | bytes 516104 | tf_op jit(solution)/shard_map/ppermute | solution.py:360
  5.6 1.3 constant_dynamic-slice_fusion
  6.9 0.6 copy.24
  7.5 1.1 copy.19
  8.6 8.2 %all-to-all-start = ((bf16[32,64,256]{2,1,0:T(8,128)(2,1)}), bf16[32,64,256]{2,1,0:T(8,128)(2,1)S(1)}, u32[]{:S(2)}, u32[]{:S(2)}) async-start(bf16[32,64,256]{2,1,0:T(8,128)(2,1)} %bitcast.97), calls=%async_computation | async-start | bytes 2097152 | tf_op jit(solution)/shard_map/all_to_all | solution.py:374
  16.8 0.7 fusion.24
  17.5 0.1 copy.22.keep_col_ref
  17.7 0.1 copy.20
  17.8 0.1 mul.190
  17.9 0.1 mul.191
  18.0 0.1 dynamic_slice.24.amino_ref
  18.1 0.1 collective-permute-start.2
  18.2 1.4 %collective-permute-done.2.w3_ref = bf16[336,256]{1,0:T(8,128)(2,1)S(1)} collective-permute-done((bf16[336,256]{1,0:T(8,128)(2,1)S(1)}, bf16[336,256]{1,0:T(8,128)(2,1)S(1)}, u32[]{:S(2)}, u32[]{:S(2)}) %collective-permute-start.2) | collective-permute-done | bytes 172064 | tf_op jit(solution)/shard_map/ppermute | solution.py:365
  19.6 0.1 add.478.shift_ref
  19.8 15.1 %all-to-all-done.x_ref = bf16[32,64,256]{2,1,0:T(8,128)(2,1)S(1)} async-done(((bf16[32,64,256]{2,1,0:T(8,128)(2,1)}), bf16[32,64,256]{2,1,0:T(8,128)(2,1)S(1)}, u32[]{:S(2)}, u32[]{:S(2)}) %all-to-all-start) | async-done | bytes 1048608 | tf_op jit(solution)/shard_map/all_to_all | solution.py:374
  34.9 15.2 %attend.1 = (bf16[2048,256]{1,0:T(8,128)(2,1)}, bf16[4,32,512]{2,1,0:T(8,128)(2,1)S(1)}, bf16[2,256,128]{2,1,0:T(8,128)(2,1)S(1)}) custom-call(s32[4]{0:T(128)S(1)} %dynamic_slice.24.amino_ref, bf16[32,64,256]{2,1,0:T(8,128)(2,1)S(1)} %all-to-all-done.x_ref, bf16[336,256]{1,0:T(8,128)(2,1)S(1)} %pad_maximum_fusion.w0_ref, ...), custom_call_target="tpu_custom_call" | custom-call | flops 16000000000 | bytes 4194304 | tf_op jit(solution)/shard_map/attend/pallas_call | solution.py:388
  50.1 0.7 collective-permute-start.3
  50.8 0.4 collective-permute-start.7
  51.2 5.7 %collective-permute-done.7 = bf16[2,256,128]{2,1,0:T(8,128)(2,1)S(1)} collective-permute-done((bf16[2,256,128]{2,1,0:T(8,128)(2,1)S(1)}, bf16[2,256,128]{2,1,0:T(8,128)(2,1)S(1)}, u32[]{:S(2)}, u32[]{:S(2)}) %collective-permute-start.7) | collective-permute-done | bytes 131104 | tf_op jit(solution)/shard_map/ppermute | solution.py:464
  57.0 0.7 collective-permute-start.8
  57.7 2.6 %collective-permute-start.9 = (bf16[2,256,128]{2,1,0:T(8,128)(2,1)S(1)}, bf16[2,256,128]{2,1,0:T(8,128)(2,1)S(1)}, u32[]{:S(2)}, u32[]{:S(2)}) collective-permute-start(bf16[2,256,128]{2,1,0:T(8,128)(2,1)S(1)} %pad_maximum_fusion.1.refs_0_), channel_id=1, source_target_pairs={{0,24},{4,28},{8,0},{12,4},{16,8},{20,12},{24,16},{28,20},{32,56},... | collective-permute-start | bytes 393224 | tf_op jit(solution)/shard_map/ppermute | solution.py:464
  60.3 8.6 %all-to-all-start.1 = ((bf16[128,16,256]{2,1,0:T(8,128)(2,1)}), bf16[128,16,256]{2,1,0:T(8,128)(2,1)S(1)}, u32[]{:S(2)}, u32[]{:S(2)}) async-start(bf16[128,16,256]{2,1,0:T(8,128)(2,1)} %bitcast.65), calls=%async_computation.1 | async-start | bytes 2097152 | tf_op jit(solution)/shard_map/all_to_all | solution.py:506
  68.8 2.5 %collective-permute-start.10 = (bf16[2,256,128]{2,1,0:T(8,128)(2,1)S(1)}, bf16[2,256,128]{2,1,0:T(8,128)(2,1)S(1)}, u32[]{:S(2)}, u32[]{:S(2)}) collective-permute-start(bf16[2,256,128]{2,1,0:T(8,128)(2,1)S(1)} %pad_maximum_fusion.1.refs_0_), channel_id=1, source_target_pairs={{0,16},{4,20},{8,24},{12,28},{16,0},{20,4},{24,8},{28,12},{32,48},... | collective-permute-start | bytes 393224 | tf_op jit(solution)/shard_map/ppermute | solution.py:464
  71.4 1.7 %collective-permute-start.11 = (bf16[2,256,128]{2,1,0:T(8,128)(2,1)S(1)}, bf16[2,256,128]{2,1,0:T(8,128)(2,1)S(1)}, u32[]{:S(2)}, u32[]{:S(2)}) collective-permute-start(bf16[2,256,128]{2,1,0:T(8,128)(2,1)S(1)} %pad_maximum_fusion.2.refs_4_), channel_id=1, source_target_pairs={{0,32},{4,36},{8,40},{12,44},{16,48},{20,52},{24,56},{28,60},{32,6... | collective-permute-start | bytes 393224 | tf_op jit(solution)/shard_map/ppermute | solution.py:464
  73.1 2.0 %collective-permute-start.12 = (bf16[2,256,128]{2,1,0:T(8,128)(2,1)S(1)}, bf16[2,256,128]{2,1,0:T(8,128)(2,1)S(1)}, u32[]{:S(2)}, u32[]{:S(2)}) collective-permute-start(bf16[2,256,128]{2,1,0:T(8,128)(2,1)S(1)} %pad_maximum_fusion.2.refs_4_), channel_id=1, source_target_pairs={{0,96},{4,100},{8,104},{12,108},{16,112},{20,116},{24,120},{28,124... | collective-permute-start | bytes 393224 | tf_op jit(solution)/shard_map/ppermute | solution.py:464
  75.1 1.8 %collective-permute-start.13 = (bf16[2,256,128]{2,1,0:T(8,128)(2,1)S(1)}, bf16[2,256,128]{2,1,0:T(8,128)(2,1)S(1)}, u32[]{:S(2)}, u32[]{:S(2)}) collective-permute-start(bf16[2,256,128]{2,1,0:T(8,128)(2,1)S(1)} %pad_maximum_fusion.2.refs_4_), channel_id=1, source_target_pairs={{0,64},{4,68},{8,72},{12,76},{16,80},{20,84},{24,88},{28,92},{32,9... | collective-permute-start | bytes 393224 | tf_op jit(solution)/shard_map/ppermute | solution.py:464
  76.9 3.1 %collective-permute-start.5 = (bf16[4,32,512]{2,1,0:T(8,128)(2,1)S(1)}, bf16[4,32,512]{2,1,0:T(8,128)(2,1)S(1)}, u32[]{:S(2)}, u32[]{:S(2)}) collective-permute-start(bf16[4,32,512]{2,1,0:T(8,128)(2,1)S(1)} %collective-permute-done.3), channel_id=1, source_target_pairs={{0,2},{1,3},{2,0},{3,1},{4,6},{5,7},{6,4},{7,5},{8,10},{9,11},{10,... | collective-permute-start | bytes 393224 | tf_op jit(solution)/shard_map/ppermute | solution.py:490
  80.0 5.6 %collective-permute-done.10.refs_3_ = bf16[2,256,128]{2,1,0:T(8,128)(2,1)S(1)} collective-permute-done((bf16[2,256,128]{2,1,0:T(8,128)(2,1)S(1)}, bf16[2,256,128]{2,1,0:T(8,128)(2,1)S(1)}, u32[]{:S(2)}, u32[]{:S(2)}) %collective-permute-start.10) | collective-permute-done | bytes 131104 | tf_op jit(solution)/shard_map/ppermute | solution.py:464
  85.7 1.6 %collective-permute-done.11.refs_5_ = bf16[2,256,128]{2,1,0:T(8,128)(2,1)S(1)} collective-permute-done((bf16[2,256,128]{2,1,0:T(8,128)(2,1)S(1)}, bf16[2,256,128]{2,1,0:T(8,128)(2,1)S(1)}, u32[]{:S(2)}, u32[]{:S(2)}) %collective-permute-start.11) | collective-permute-done | bytes 131104 | tf_op jit(solution)/shard_map/ppermute | solution.py:464
  87.2 3.1 %collective-permute-done.13.refs_7_ = bf16[2,256,128]{2,1,0:T(8,128)(2,1)S(1)} collective-permute-done((bf16[2,256,128]{2,1,0:T(8,128)(2,1)S(1)}, bf16[2,256,128]{2,1,0:T(8,128)(2,1)S(1)}, u32[]{:S(2)}, u32[]{:S(2)}) %collective-permute-start.13) | collective-permute-done | bytes 131104 | tf_op jit(solution)/shard_map/ppermute | solution.py:464
  90.3 1.1 join.1
  91.4 0.9 collective-permute-start.14
  92.3 2.3 %collective-permute-start.15 = (bf16[8,256,128]{2,1,0:T(8,128)(2,1)}, bf16[8,256,128]{2,1,0:T(8,128)(2,1)S(1)}, u32[]{:S(2)}, u32[]{:S(2)}) collective-permute-start(bf16[8,256,128]{2,1,0:T(8,128)(2,1)} %get-tuple-element.23.z0_ref), channel_id=1, source_target_pairs={{0,96},{4,100},{8,104},{12,108},{16,112},{20,116},{24,120},{28,124... | collective-permute-start | bytes 1572872 | tf_op jit(solution)/shard_map/ppermute | solution.py:464
  94.6 1.2 collective-permute-start.16
  95.8 2.0 %collective-permute-start.17 = (bf16[8,256,128]{2,1,0:T(8,128)(2,1)}, bf16[8,256,128]{2,1,0:T(8,128)(2,1)}, u32[]{:S(2)}, u32[]{:S(2)}) collective-permute-start(bf16[8,256,128]{2,1,0:T(8,128)(2,1)} %get-tuple-element.24.x0_ref), channel_id=1, source_target_pairs={{0,24},{4,28},{8,0},{12,4},{16,8},{20,12},{24,16},{28,20},{32,56},... | collective-permute-start | bytes 1572872 | tf_op jit(solution)/shard_map/ppermute | solution.py:464
  97.9 0.1 dynamic-slice_convert_fusion.1
  97.9 0.1 fusion.25
  98.0 0.0 collective-permute-start.6
  98.1 0.1 dynamic-slice_convert_fusion
  98.3 0.1 mul.208
  99.0 0.1 maximum_multiply_fusion
  99.1 0.1 mul.206
  99.2 0.1 fusion.1.inverse_ref
  99.3 0.1 stack.190.place_ref
  99.5 0.1 maximum_bitcast_fusion
  99.5 0.3 copy.23
  99.8 6.7 %collective-permute-done.14.z1_ref = bf16[8,256,128]{2,1,0:T(8,128)(2,1)S(1)} collective-permute-done((bf16[8,256,128]{2,1,0:T(8,128)(2,1)}, bf16[8,256,128]{2,1,0:T(8,128)(2,1)S(1)}, u32[]{:S(2)}, u32[]{:S(2)}) %collective-permute-start.14) | collective-permute-done | bytes 524320 | tf_op jit(solution)/shard_map/ppermute | solution.py:464
  106.6 0.7 slice.90
  107.3 0.7 slice.91
  108.0 3.2 %collective-permute-start.19 = (bf16[4,256,128]{2,1,0:T(8,128)(2,1)}, bf16[4,256,128]{2,1,0:T(8,128)(2,1)}, u32[]{:S(2)}, u32[]{:S(2)}) collective-permute-start(bf16[4,256,128]{2,1,0:T(8,128)(2,1)} %slice.91), channel_id=1, source_target_pairs={{0,96},{4,100},{8,104},{12,108},{16,112},{20,116},{24,120},{28,124... | collective-permute-start | bytes 786440 | tf_op jit(solution)/shard_map/ppermute | solution.py:464
  111.2 0.7 slice.92
  111.9 1.3 %collective-permute-start.20 = (bf16[4,256,128]{2,1,0:T(8,128)(2,1)}, bf16[4,256,128]{2,1,0:T(8,128)(2,1)}, u32[]{:S(2)}, u32[]{:S(2)}) collective-permute-start(bf16[4,256,128]{2,1,0:T(8,128)(2,1)} %slice.92), channel_id=1, source_target_pairs={{0,8},{4,12},{8,16},{12,20},{16,24},{20,28},{24,0},{28,4},{32,40},... | collective-permute-start | bytes 786440 | tf_op jit(solution)/shard_map/ppermute | solution.py:464
  113.3 1.7 %slice.93 = bf16[4,256,128]{2,1,0:T(8,128)(2,1)} slice(bf16[8,256,128]{2,1,0:T(8,128)(2,1)} %collective-permute-done.17.x2_ref), slice={[4:8], [0:256], [0:128]} | slice | bytes 524288 | tf_op jit(solution)/shard_map/slice | solution.py:497
  115.0 1.9 %collective-permute-start.21 = (bf16[4,256,128]{2,1,0:T(8,128)(2,1)}, bf16[4,256,128]{2,1,0:T(8,128)(2,1)}, u32[]{:S(2)}, u32[]{:S(2)}) collective-permute-start(bf16[4,256,128]{2,1,0:T(8,128)(2,1)} %slice.93), channel_id=1, source_target_pairs={{0,24},{4,28},{8,0},{12,4},{16,8},{20,12},{24,16},{28,20},{32,56},... | collective-permute-start | bytes 786440 | tf_op jit(solution)/shard_map/ppermute | solution.py:464
  116.9 1.0 copy-done
  117.9 4.4 %early.1.part_ref = f32[1152,128]{1,0:T(8,128)S(1)} custom-call(s32[36]{0:T(128)S(1)} %stack.190.place_ref, bf16[512,512]{1,0:T(8,128)(2,1)S(1)} %bitcast.86, f32[1,128]{1,0:T(1,128)S(1)} %bitcast.95, f32[512,4]{1,0:T(8,128)S(1)} %fusion.1.inverse_ref, f32[1024,128]{1,0:T(8,128)S(1)} %copy-done, bf16[8,256,128]{2,1,0:T(8,128)(2,1)} %get-tuple-element.23.z0_ref, ...), custom_call_target="tpu_custom_call" | custom-call | flops 3000000000 | bytes 6291456 | tf_op jit(solution)/shard_map/early/pallas_call | solution.py:538
  122.3 0.8 copy-done.8
  123.2 1.5 %arrange.1 = bf16[4,512,256]{2,1,0:T(8,128)(2,1)} custom-call(bf16[128,16,256]{2,1,0:T(8,128)(2,1)S(1)} %all-to-all-done.1.back_ref), custom_call_target="tpu_custom_call" | custom-call | flops 500000000 | bytes 2097152 | tf_op jit(solution)/shard_map/arrange/pallas_call | solution.py:556
  124.7 1.0 copy-done.1
  125.7 1.1 copy-done.9
  126.8 5.1 %late.1 = f32[16,128,128]{2,1,0:T(8,128)} custom-call(s32[36]{0:T(128)S(1)} %stack.190.place_ref, bf16[512,512]{1,0:T(8,128)(2,1)S(1)} %bitcast.87, f32[1,128]{1,0:T(1,128)S(1)} %bitcast.96, f32[512,4]{1,0:T(8,128)S(1)} %fusion.1.inverse_ref, f32[1024,128]{1,0:T(8,128)S(1)} %copy-done.1, f32[1152,128]{1,0:T(8,128)S(1)} %copy-done.9, ...), custom_call_target="tpu_custom_call" | custom-call | flops 3000000000 | bytes 6291456 | tf_op jit(solution)/shard_map/late/pallas_call | solution.py:571
  (55 shorter events, 0.3 us)
Async XLA Ops:
  2.2 16.0 %collective-permute-start = (bf16[336,256]{1,0:T(8,128)(2,1)S(1)}, bf16[336,256]{1,0:T(8,128)(2,1)S(1)}, u32[]{:S(2)}, u32[]{:S(2)}) collective-permute-start(bf16[336,256]{1,0:T(8,128)(2,1)S(1)} %pad_maximum_fusion.w0_ref), channel_id=1, source_target_pairs={{0,1},{1,0},{2,3},{3,2},{4,5},{5,4},{6,7},{7,6},{8,9},{9,8},{10,11... | collective-permute-start | bytes 516104 | tf_op jit(solution)/shard_map/ppermute | solution.py:363
  2.3 15.8 %collective-permute-start.1 = (bf16[336,256]{1,0:T(8,128)(2,1)S(1)}, bf16[336,256]{1,0:T(8,128)(2,1)S(1)}, u32[]{:S(2)}, u32[]{:S(2)}) collective-permute-start(bf16[336,256]{1,0:T(8,128)(2,1)S(1)} %pad_maximum_fusion.w0_ref), channel_id=1, source_target_pairs={{0,6},{1,7},{2,4},{3,5},{4,2},{5,3},{6,0},{7,1},{8,14},{9,15},{10,... | collective-permute-start | bytes 516104 | tf_op jit(solution)/shard_map/ppermute | solution.py:360
  5.5 11.3 %copy-start.11 = (s32[512]{0:T(512)S(1)}, s32[512]{0:T(512)}, u32[]{:S(2)}) copy-start(s32[512]{0:T(512)} %param.17) | copy-start | bytes 6148
  5.5 12.1 %copy-start.10 = (bf16[256,2,32]{0,2,1:T(8,128)(2,1)S(1)}, bf16[256,2,32]{0,2,1:T(8,128)(2,1)}, u32[]{:S(2)}) copy-start(bf16[256,2,32]{0,2,1:T(8,128)(2,1)} %param.27) | copy-start | bytes 98308
  5.6 12.4 %copy-start.12 = (s32[512]{0:T(512)S(1)}, s32[512]{0:T(512)}, u32[]{:S(2)}) copy-start(s32[512]{0:T(512)} %param.18) | copy-start | bytes 6148
  6.9 28.0 %copy-start.2 = (f32[256]{0:T(256)S(1)}, f32[256]{0:T(256)}, u32[]{:S(2)}) copy-start(f32[256]{0:T(256)} %param.19) | copy-start | bytes 3076
  6.9 28.0 %copy-start.3 = (f32[256]{0:T(256)S(1)}, f32[256]{0:T(256)}, u32[]{:S(2)}) copy-start(f32[256]{0:T(256)} %param.20) | copy-start | bytes 3076
  6.9 28.0 %copy-start.4 = (f32[256]{0:T(256)S(1)}, f32[256]{0:T(256)}, u32[]{:S(2)}) copy-start(f32[256]{0:T(256)} %param.24) | copy-start | bytes 3076
  6.9 28.0 %copy-start.5 = (f32[256]{0:T(256)S(1)}, f32[256]{0:T(256)}, u32[]{:S(2)}) copy-start(f32[256]{0:T(256)} %param.25) | copy-start | bytes 3076
  6.9 28.0 %copy-start.6 = (f32[256]{0:T(256)S(1)}, f32[256]{0:T(256)}, u32[]{:S(2)}) copy-start(f32[256]{0:T(256)} %param.26) | copy-start | bytes 3076
  8.6 26.3 %all-to-all-start = ((bf16[32,64,256]{2,1,0:T(8,128)(2,1)}), bf16[32,64,256]{2,1,0:T(8,128)(2,1)S(1)}, u32[]{:S(2)}, u32[]{:S(2)}) async-start(bf16[32,64,256]{2,1,0:T(8,128)(2,1)} %bitcast.97), calls=%async_computation | async-start | bytes 2097152 | tf_op jit(solution)/shard_map/all_to_all | solution.py:374
  18.1 1.5 %collective-permute-start.2 = (bf16[336,256]{1,0:T(8,128)(2,1)S(1)}, bf16[336,256]{1,0:T(8,128)(2,1)S(1)}, u32[]{:S(2)}, u32[]{:S(2)}) collective-permute-start(bf16[336,256]{1,0:T(8,128)(2,1)S(1)} %collective-permute-done.1.w2_ref), channel_id=1, source_target_pairs={{0,1},{1,0},{2,3},{3,2},{4,5},{5,4},{6,7},{7,6},{8,9},{9,8},{10,11... | collective-permute-start | bytes 516104 | tf_op jit(solution)/shard_map/ppermute | solution.py:365
  50.1 23.0 %collective-permute-start.3 = (bf16[4,32,512]{2,1,0:T(8,128)(2,1)S(1)}, bf16[4,32,512]{2,1,0:T(8,128)(2,1)S(1)}, u32[]{:S(2)}, u32[]{:S(2)}) collective-permute-start(bf16[4,32,512]{2,1,0:T(8,128)(2,1)S(1)} %get-tuple-element.21), channel_id=1, source_target_pairs={{0,0},{1,32},{2,64},{3,96},{4,4},{5,36},{6,68},{7,100},{8,8},{9,40... | collective-permute-start | bytes 393224 | tf_op jit(solution)/shard_map/ppermute | solution.py:454
  50.8 6.1 %collective-permute-start.7 = (bf16[2,256,128]{2,1,0:T(8,128)(2,1)S(1)}, bf16[2,256,128]{2,1,0:T(8,128)(2,1)S(1)}, u32[]{:S(2)}, u32[]{:S(2)}) collective-permute-start(bf16[2,256,128]{2,1,0:T(8,128)(2,1)S(1)} %get-tuple-element.22), channel_id=1, source_target_pairs={{0,4},{4,0},{8,12},{12,8},{16,20},{20,16},{24,28},{28,24},{32,36},... | collective-permute-start | bytes 393224 | tf_op jit(solution)/shard_map/ppermute | solution.py:464
  57.0 18.2 %collective-permute-start.8 = (bf16[2,256,128]{2,1,0:T(8,128)(2,1)S(1)}, bf16[2,256,128]{2,1,0:T(8,128)(2,1)S(1)}, u32[]{:S(2)}, u32[]{:S(2)}) collective-permute-start(bf16[2,256,128]{2,1,0:T(8,128)(2,1)S(1)} %pad_maximum_fusion.1.refs_0_), channel_id=1, source_target_pairs={{0,8},{4,12},{8,16},{12,20},{16,24},{20,28},{24,0},{28,4},{32,40},... | collective-permute-start | bytes 393224 | tf_op jit(solution)/shard_map/ppermute | solution.py:464
  57.7 19.2 %collective-permute-start.9 = (bf16[2,256,128]{2,1,0:T(8,128)(2,1)S(1)}, bf16[2,256,128]{2,1,0:T(8,128)(2,1)S(1)}, u32[]{:S(2)}, u32[]{:S(2)}) collective-permute-start(bf16[2,256,128]{2,1,0:T(8,128)(2,1)S(1)} %pad_maximum_fusion.1.refs_0_), channel_id=1, source_target_pairs={{0,24},{4,28},{8,0},{12,4},{16,8},{20,12},{24,16},{28,20},{32,56},... | collective-permute-start | bytes 393224 | tf_op jit(solution)/shard_map/ppermute | solution.py:464
  60.3 56.6 %copy-start.7 = (f32[128]{0:T(128)S(1)}, f32[128]{0:T(128)}, u32[]{:S(2)}) copy-start(f32[128]{0:T(128)} %param.29) | copy-start | bytes 1540
  60.3 62.9 %all-to-all-start.1 = ((bf16[128,16,256]{2,1,0:T(8,128)(2,1)}), bf16[128,16,256]{2,1,0:T(8,128)(2,1)S(1)}, u32[]{:S(2)}, u32[]{:S(2)}) async-start(bf16[128,16,256]{2,1,0:T(8,128)(2,1)} %bitcast.65), calls=%async_computation.1 | async-start | bytes 2097152 | tf_op jit(solution)/shard_map/all_to_all | solution.py:506
  68.8 16.8 %collective-permute-start.10 = (bf16[2,256,128]{2,1,0:T(8,128)(2,1)S(1)}, bf16[2,256,128]{2,1,0:T(8,128)(2,1)S(1)}, u32[]{:S(2)}, u32[]{:S(2)}) collective-permute-start(bf16[2,256,128]{2,1,0:T(8,128)(2,1)S(1)} %pad_maximum_fusion.1.refs_0_), channel_id=1, source_target_pairs={{0,16},{4,20},{8,24},{12,28},{16,0},{20,4},{24,8},{28,12},{32,48},... | collective-permute-start | bytes 393224 | tf_op jit(solution)/shard_map/ppermute | solution.py:464
  71.4 15.8 %collective-permute-start.11 = (bf16[2,256,128]{2,1,0:T(8,128)(2,1)S(1)}, bf16[2,256,128]{2,1,0:T(8,128)(2,1)S(1)}, u32[]{:S(2)}, u32[]{:S(2)}) collective-permute-start(bf16[2,256,128]{2,1,0:T(8,128)(2,1)S(1)} %pad_maximum_fusion.2.refs_4_), channel_id=1, source_target_pairs={{0,32},{4,36},{8,40},{12,44},{16,48},{20,52},{24,56},{28,60},{32,6... | collective-permute-start | bytes 393224 | tf_op jit(solution)/shard_map/ppermute | solution.py:464
  73.1 14.1 %collective-permute-start.12 = (bf16[2,256,128]{2,1,0:T(8,128)(2,1)S(1)}, bf16[2,256,128]{2,1,0:T(8,128)(2,1)S(1)}, u32[]{:S(2)}, u32[]{:S(2)}) collective-permute-start(bf16[2,256,128]{2,1,0:T(8,128)(2,1)S(1)} %pad_maximum_fusion.2.refs_4_), channel_id=1, source_target_pairs={{0,96},{4,100},{8,104},{12,108},{16,112},{20,116},{24,120},{28,124... | collective-permute-start | bytes 393224 | tf_op jit(solution)/shard_map/ppermute | solution.py:464
  75.1 15.2 %collective-permute-start.13 = (bf16[2,256,128]{2,1,0:T(8,128)(2,1)S(1)}, bf16[2,256,128]{2,1,0:T(8,128)(2,1)S(1)}, u32[]{:S(2)}, u32[]{:S(2)}) collective-permute-start(bf16[2,256,128]{2,1,0:T(8,128)(2,1)S(1)} %pad_maximum_fusion.2.refs_4_), channel_id=1, source_target_pairs={{0,64},{4,68},{8,72},{12,76},{16,80},{20,84},{24,88},{28,92},{32,9... | collective-permute-start | bytes 393224 | tf_op jit(solution)/shard_map/ppermute | solution.py:464
  76.9 18.9 %collective-permute-start.5 = (bf16[4,32,512]{2,1,0:T(8,128)(2,1)S(1)}, bf16[4,32,512]{2,1,0:T(8,128)(2,1)S(1)}, u32[]{:S(2)}, u32[]{:S(2)}) collective-permute-start(bf16[4,32,512]{2,1,0:T(8,128)(2,1)S(1)} %collective-permute-done.3), channel_id=1, source_target_pairs={{0,2},{1,3},{2,0},{3,1},{4,6},{5,7},{6,4},{7,5},{8,10},{9,11},{10,... | collective-permute-start | bytes 393224 | tf_op jit(solution)/shard_map/ppermute | solution.py:490
  85.7 12.4 %collective-permute-start.4 = (bf16[4,32,512]{2,1,0:T(8,128)(2,1)S(1)}, bf16[4,32,512]{2,1,0:T(8,128)(2,1)S(1)}, u32[]{:S(2)}, u32[]{:S(2)}) collective-permute-start(bf16[4,32,512]{2,1,0:T(8,128)(2,1)S(1)} %collective-permute-done.3), channel_id=1, source_target_pairs={{0,1},{1,0},{2,3},{3,2},{4,5},{5,4},{6,7},{7,6},{8,9},{9,8},{10,11... | collective-permute-start | bytes 393224 | tf_op jit(solution)/shard_map/ppermute | solution.py:489
  91.4 15.2 %collective-permute-start.14 = (bf16[8,256,128]{2,1,0:T(8,128)(2,1)}, bf16[8,256,128]{2,1,0:T(8,128)(2,1)S(1)}, u32[]{:S(2)}, u32[]{:S(2)}) collective-permute-start(bf16[8,256,128]{2,1,0:T(8,128)(2,1)} %get-tuple-element.23.z0_ref), channel_id=1, source_target_pairs={{0,32},{4,36},{8,40},{12,44},{16,48},{20,52},{24,56},{28,60},{32,6... | collective-permute-start | bytes 1572872 | tf_op jit(solution)/shard_map/ppermute | solution.py:464
  92.3 15.0 %collective-permute-start.15 = (bf16[8,256,128]{2,1,0:T(8,128)(2,1)}, bf16[8,256,128]{2,1,0:T(8,128)(2,1)S(1)}, u32[]{:S(2)}, u32[]{:S(2)}) collective-permute-start(bf16[8,256,128]{2,1,0:T(8,128)(2,1)} %get-tuple-element.23.z0_ref), channel_id=1, source_target_pairs={{0,96},{4,100},{8,104},{12,108},{16,112},{20,116},{24,120},{28,124... | collective-permute-start | bytes 1572872 | tf_op jit(solution)/shard_map/ppermute | solution.py:464
  94.6 16.6 %collective-permute-start.16 = (bf16[8,256,128]{2,1,0:T(8,128)(2,1)}, bf16[8,256,128]{2,1,0:T(8,128)(2,1)S(1)}, u32[]{:S(2)}, u32[]{:S(2)}) collective-permute-start(bf16[8,256,128]{2,1,0:T(8,128)(2,1)} %get-tuple-element.24.x0_ref), channel_id=1, source_target_pairs={{0,8},{4,12},{8,16},{12,20},{16,24},{20,28},{24,0},{28,4},{32,40},... | collective-permute-start | bytes 1572872 | tf_op jit(solution)/shard_map/ppermute | solution.py:464
  95.8 17.5 %collective-permute-start.17 = (bf16[8,256,128]{2,1,0:T(8,128)(2,1)}, bf16[8,256,128]{2,1,0:T(8,128)(2,1)}, u32[]{:S(2)}, u32[]{:S(2)}) collective-permute-start(bf16[8,256,128]{2,1,0:T(8,128)(2,1)} %get-tuple-element.24.x0_ref), channel_id=1, source_target_pairs={{0,24},{4,28},{8,0},{12,4},{16,8},{20,12},{24,16},{28,20},{32,56},... | collective-permute-start | bytes 1572872 | tf_op jit(solution)/shard_map/ppermute | solution.py:464
  98.0 1.4 %collective-permute-start.6 = (bf16[4,32,512]{2,1,0:T(8,128)(2,1)S(1)}, bf16[4,32,512]{2,1,0:T(8,128)(2,1)S(1)}, u32[]{:S(2)}, u32[]{:S(2)}) collective-permute-start(bf16[4,32,512]{2,1,0:T(8,128)(2,1)S(1)} %collective-permute-done.5), channel_id=1, source_target_pairs={{0,1},{1,0},{2,3},{3,2},{4,5},{5,4},{6,7},{7,6},{8,9},{9,8},{10,11... | collective-permute-start | bytes 393224 | tf_op jit(solution)/shard_map/ppermute | solution.py:491
  107.3 17.4 %collective-permute-start.18 = (bf16[4,256,128]{2,1,0:T(8,128)(2,1)}, bf16[4,256,128]{2,1,0:T(8,128)(2,1)}, u32[]{:S(2)}, u32[]{:S(2)}) collective-permute-start(bf16[4,256,128]{2,1,0:T(8,128)(2,1)} %slice.90), channel_id=1, source_target_pairs={{0,32},{4,36},{8,40},{12,44},{16,48},{20,52},{24,56},{28,60},{32,6... | collective-permute-start | bytes 786440 | tf_op jit(solution)/shard_map/ppermute | solution.py:464
  108.0 16.7 %collective-permute-start.19 = (bf16[4,256,128]{2,1,0:T(8,128)(2,1)}, bf16[4,256,128]{2,1,0:T(8,128)(2,1)}, u32[]{:S(2)}, u32[]{:S(2)}) collective-permute-start(bf16[4,256,128]{2,1,0:T(8,128)(2,1)} %slice.91), channel_id=1, source_target_pairs={{0,96},{4,100},{8,104},{12,108},{16,112},{20,116},{24,120},{28,124... | collective-permute-start | bytes 786440 | tf_op jit(solution)/shard_map/ppermute | solution.py:464
  111.9 12.7 %collective-permute-start.20 = (bf16[4,256,128]{2,1,0:T(8,128)(2,1)}, bf16[4,256,128]{2,1,0:T(8,128)(2,1)}, u32[]{:S(2)}, u32[]{:S(2)}) collective-permute-start(bf16[4,256,128]{2,1,0:T(8,128)(2,1)} %slice.92), channel_id=1, source_target_pairs={{0,8},{4,12},{8,16},{12,20},{16,24},{20,28},{24,0},{28,4},{32,40},... | collective-permute-start | bytes 786440 | tf_op jit(solution)/shard_map/ppermute | solution.py:464
  115.0 9.7 %collective-permute-start.21 = (bf16[4,256,128]{2,1,0:T(8,128)(2,1)}, bf16[4,256,128]{2,1,0:T(8,128)(2,1)}, u32[]{:S(2)}, u32[]{:S(2)}) collective-permute-start(bf16[4,256,128]{2,1,0:T(8,128)(2,1)} %slice.93), channel_id=1, source_target_pairs={{0,24},{4,28},{8,0},{12,4},{16,8},{20,12},{24,16},{28,20},{32,56},... | collective-permute-start | bytes 786440 | tf_op jit(solution)/shard_map/ppermute | solution.py:464
  116.9 1.0 copy-start
  122.3 0.8 copy-start.8
  124.7 1.0 copy-start.1
  125.7 1.1 copy-start.9

commit v6 on v5

--- a/solution.py
+++ b/solution.py
@@ -385,6 +385,26 @@
     row = lambda v: v.reshape(1, chans)
     lanes = mine * CO
     depth = pair_weight.shape[1]
+    i_rows = mine * n_head
+    total = jnp.sum(homolog).astype(F32)
+    row_keep = lax.dynamic_slice_in_dim(amino, dap_id * i_rows, i_rows).astype(F32)
+    heads = [head_id ^ flip for flip in range(n_head)]
+    row_keep = jnp.concatenate(
+        [lax.dynamic_slice_in_dim(row_keep, h * mine, mine) for h in heads]
+    )
+    col_keep = lax.dynamic_slice_in_dim(amino, head_id * col_width, col_width).astype(F32)
+    norm = jnp.maximum(
+        total * row_keep[None, :, None] * col_keep.reshape(n_dap, 1, mine), 1.0
+    )
+    inverse = (1.0 / norm).reshape(n_dap * i_rows, mine)
+    places = []
+    for dz in STEPS:
+        for dx in STEPS:
+            for dy in range(ny):
+                at_z, at_x, at_y = (zi + dz) % nz, (xi + dx) % nx, (yi + dy) % ny
+                places.append((at_x * ny + at_y) * nz + at_z)
+    place = jnp.stack([*places, *heads]).astype(jnp.int32)
+    block, inverse, place = lax.optimization_barrier((block, inverse, place))
     rows, left, right = pl.pallas_call(
         attend_kernel,
         in_specs=[
@@ -499,7 +519,6 @@
     z_pieces = forward(z_pieces, 0)
     x_pieces = forward(x_pieces, 1)
 
-    i_rows = mine * n_head
     left = jnp.concatenate([left, left_core, left_far, left_corner], 0)
     left = jnp.swapaxes(left, 0, 1).reshape(CO * i_rows, seqs)
 
@@ -511,25 +530,8 @@
         tiled=True,
     )
     own = own_seqs // n_head
-    total = jnp.sum(homolog).astype(F32)
-    row_keep = lax.dynamic_slice_in_dim(amino, dap_id * i_rows, i_rows).astype(F32)
-    heads = [head_id ^ flip for flip in range(n_head)]
-    row_keep = jnp.concatenate(
-        [lax.dynamic_slice_in_dim(row_keep, h * mine, mine) for h in heads]
-    )
-    col_keep = lax.dynamic_slice_in_dim(amino, head_id * col_width, col_width).astype(F32)
-    norm = jnp.maximum(
-        total * row_keep[None, :, None] * col_keep.reshape(n_dap, 1, mine), 1.0
-    )
-    inverse = (1.0 / norm).reshape(n_dap * i_rows, mine)
-    places = []
-    for dz in STEPS:
-        for dx in STEPS:
-            for dy in range(ny):
-                at_z, at_x, at_y = (zi + dz) % nz, (xi + dx) % nx, (yi + dy) % ny
-                places.append((at_x * ny + at_y) * nz + at_z)
     shared = (
-        jnp.stack([*places, *heads]).astype(jnp.int32),
+        place,
         left,
         pair_bias.reshape(1, depth),
         inverse,
@@ -564,7 +566,6 @@
         ),
         name="arrange",
     )(back)
-    early, alignment = lax.optimization_barrier((early, alignment))
     part_specs = [
         pl.BlockSpec((ny, *z_pieces[0].shape[1:]), lambda _: (len(STEPS) - 1, 0, 0))
     ] * 3 + [pl.BlockSpec(memory_space=pltpu.VMEM)] * 2

time: 132 us -> 130 us (0.985)
  starting transfers between devices: 48.6 us -> 43.5 us
  local copies, waits for them, and re-layouts: 12.1 us -> 14.5 us
  waiting for transfers between devices: 39.3 us -> 41.5 us
  Pallas kernels: 27.3 us -> 25.3 us
    all_to_all x1, starting transfers between devices: 8.58 us -> 4.63 us  [per_device(): lax.all_to_all(rows.reshape(n_dap * n_head, seqs * mine // (n_dap * n_hea...]
    unnamed x27 -> x39, local copies, waits for them, and re-layouts: 4.58 us -> 7.82 us
    ppermute x1, waiting for transfers between devices: 0.01 us -> 3.11 us  [per_device(): left_far = lax.ppermute(left, 'head', [(h, h ^ 2) for h in range(n_head)])]
    ppermute x15, waiting for transfers between devices: 22.8 us -> 20.6 us  [shifted(): return lax.ppermute(value, 'dap', pairs)]
    ppermute x15, starting transfers between devices: 24.7 us -> 23 us  [shifted(): return lax.ppermute(value, 'dap', pairs)]
    ppermute x1, waiting for transfers between devices: 0.01 us -> 1.35 us  [per_device(): left_core = lax.ppermute(left, 'head', swap_core)]
  transfers between devices with their start and end apart: 24 -> 24, of which waited for: 7 -> 11; matrix products, arithmetic and copies ran while one was open for 7% -> 6% of each run, Pallas kernels for 5% -> 4%
where the time goes in v6:
time: 130 us; the launch traced here: 129 us
  starting transfers between devices  43.5 us (33%)
  waiting for transfers between devices  41.5 us (32%)
  Pallas kernels  25.3 us (19%)
  local copies, waits for them, and re-layouts  14.5 us (11%)
  other arithmetic  2.79 us (2%)
  between operations  1.75 us (1%)
    ppermute x15, starting transfers between devices, shifted(): return lax.ppermute(value, 'dap', pairs)  23 us
    ppermute x15, waiting for transfers between devices, shifted(): return lax.ppermute(value, 'dap', pairs)  20.6 us
    pallas_call x1, Pallas kernels, per_device(): pl.pallas_call(attend_kernel, in_specs=[pl.BlockSpec(memory_space=pltpu.S...  15.2 us
    all_to_all x1, waiting for transfers between devices, per_device(): lax.all_to_all(block, 'dap', split_axis=0, concat_axis=0, tiled=True)  14 us
    all_to_all x1, starting transfers between devices, per_device(): lax.all_to_all(block, 'dap', split_axis=0, concat_axis=0, tiled=True)  8.16 us
    unnamed x39, local copies, waits for them, and re-layouts  7.82 us
    pallas_call x1, Pallas kernels, per_device(): pl.pallas_call(late_kernel, grid=(1,), in_specs=[pl.BlockSpec(memory_spac...  4.94 us
    all_to_all x1, starting transfers between devices, per_device(): lax.all_to_all(rows.reshape(n_dap * n_head, seqs * mine // (n_dap * n_hea...  4.63 us
  transfers between devices with their start and end apart: 24, of which 11 were waited for; matrix products, arithmetic and copies ran while one was open for 6% of the time, Pallas kernels for 4%

profile of v6, /device:TPU:0, one launch (start us, length us, event | category | flops | bytes accessed | tf_op | source)
XLA Modules:
  0.0 129.3 jit_solution(11067840941032290607)
XLA Ops:
  0.6 0.7 fusion.16
  1.3 0.9 pad_maximum_fusion.w0_ref
  2.2 3.2 %collective-permute-start.1 = (bf16[336,256]{1,0:T(8,128)(2,1)S(1)}, bf16[336,256]{1,0:T(8,128)(2,1)S(1)}, u32[]{:S(2)}, u32[]{:S(2)}) collective-permute-start(bf16[336,256]{1,0:T(8,128)(2,1)S(1)} %pad_maximum_fusion.w0_ref), channel_id=1, source_target_pairs={{0,6},{1,7},{2,4},{3,5},{4,2},{5,3},{6,0},{7,1},{8,14},{9,15},{10,... | collective-permute-start | bytes 516104 | tf_op jit(solution)/shard_map/ppermute | solution.py:360
  5.5 1.3 %constant_dynamic-slice_fusion = bf16[16,128,256]{2,1,0:T(8,128)(2,1)S(1)} fusion(bf16[16,512,256]{2,1,0:T(8,128)(2,1)} %param.16, s32[]{:T(128)S(6)} %select_n.257), kind=kLoop, calls=%fused_computation.47 | loop fusion | bytes 2097156 | tf_op jit(solution)/shard_map/dynamic_slice | solution.py:371
  6.9 0.6 copy.24
  7.5 1.0 copy.19
  8.5 8.2 %all-to-all-start = ((bf16[32,64,256]{2,1,0:T(8,128)(2,1)}), bf16[32,64,256]{2,1,0:T(8,128)(2,1)S(1)}, u32[]{:S(2)}, u32[]{:S(2)}) async-start(bf16[32,64,256]{2,1,0:T(8,128)(2,1)} %bitcast.97), calls=%async_computation | async-start | bytes 2097152 | tf_op jit(solution)/shard_map/all_to_all | solution.py:374
  16.9 0.1 dynamic_slice.24.amino_ref
  17.0 0.1 dynamic-slice_convert_fusion.1
  17.1 0.6 fusion.24
  18.4 0.1 mul.205
  18.5 0.1 fusion.25
  18.5 0.1 maximum_multiply_fusion
  18.6 0.1 mul.186
  18.7 0.1 dynamic-slice_convert_fusion
  18.8 0.1 mul.188
  18.9 0.1 copy.20
  19.0 0.1 copy.22.keep_col_ref
  19.2 0.1 fusion.1.inverse_ref
  19.4 0.1 stack.190.place_ref
  19.5 0.3 collective-permute-start.2
  19.8 1.2 collective-permute-done.2.w3_ref
  21.0 0.1 add.478.shift_ref
  21.2 14.0 %all-to-all-done.x_ref = bf16[32,64,256]{2,1,0:T(8,128)(2,1)S(1)} async-done(((bf16[32,64,256]{2,1,0:T(8,128)(2,1)}), bf16[32,64,256]{2,1,0:T(8,128)(2,1)S(1)}, u32[]{:S(2)}, u32[]{:S(2)}) %all-to-all-start) | async-done | bytes 1048608 | tf_op jit(solution)/shard_map/all_to_all | solution.py:374
  35.2 15.2 %attend.1 = (bf16[2048,256]{1,0:T(8,128)(2,1)}, bf16[4,32,512]{2,1,0:T(8,128)(2,1)S(1)}, bf16[2,256,128]{2,1,0:T(8,128)(2,1)S(1)}) custom-call(s32[4]{0:T(128)S(1)} %dynamic_slice.24.amino_ref, bf16[32,64,256]{2,1,0:T(8,128)(2,1)S(1)} %all-to-all-done.x_ref, bf16[336,256]{1,0:T(8,128)(2,1)S(1)} %pad_maximum_fusion.w0_ref, ...), custom_call_target="tpu_custom_call" | custom-call | flops 16000000000 | bytes 4194304 | tf_op jit(solution)/shard_map/attend/pallas_call | solution.py:408
  50.4 0.3 collective-permute-start.7
  50.7 4.6 %collective-permute-done.7 = bf16[2,256,128]{2,1,0:T(8,128)(2,1)S(1)} collective-permute-done((bf16[2,256,128]{2,1,0:T(8,128)(2,1)S(1)}, bf16[2,256,128]{2,1,0:T(8,128)(2,1)S(1)}, u32[]{:S(2)}, u32[]{:S(2)}) %collective-permute-start.7) | collective-permute-done | bytes 131104 | tf_op jit(solution)/shard_map/ppermute | solution.py:484
  55.4 1.0 collective-permute-start.10
  56.4 2.3 %collective-permute-start.9 = (bf16[2,256,128]{2,1,0:T(8,128)(2,1)S(1)}, bf16[2,256,128]{2,1,0:T(8,128)(2,1)S(1)}, u32[]{:S(2)}, u32[]{:S(2)}) collective-permute-start(bf16[2,256,128]{2,1,0:T(8,128)(2,1)S(1)} %pad_maximum_fusion.1.refs_0_), channel_id=1, source_target_pairs={{0,24},{4,28},{8,0},{12,4},{16,8},{20,12},{24,16},{28,20},{32,56},... | collective-permute-start | bytes 393224 | tf_op jit(solution)/shard_map/ppermute | solution.py:484
  58.7 4.6 %all-to-all-start.1 = ((bf16[128,16,256]{2,1,0:T(8,128)(2,1)}), bf16[128,16,256]{2,1,0:T(8,128)(2,1)S(1)}, u32[]{:S(2)}, u32[]{:S(2)}) async-start(bf16[128,16,256]{2,1,0:T(8,128)(2,1)} %bitcast.62), calls=%async_computation.1 | async-start | bytes 2097152 | tf_op jit(solution)/shard_map/all_to_all | solution.py:525
  63.4 0.9 collective-permute-start.8
  64.3 3.8 %collective-permute-start.13 = (bf16[2,256,128]{2,1,0:T(8,128)(2,1)S(1)}, bf16[2,256,128]{2,1,0:T(8,128)(2,1)S(1)}, u32[]{:S(2)}, u32[]{:S(2)}) collective-permute-start(bf16[2,256,128]{2,1,0:T(8,128)(2,1)S(1)} %pad_maximum_fusion.2.refs_4_), channel_id=1, source_target_pairs={{0,64},{4,68},{8,72},{12,76},{16,80},{20,84},{24,88},{28,92},{32,9... | collective-permute-start | bytes 393224 | tf_op jit(solution)/shard_map/ppermute | solution.py:484
  68.1 0.9 collective-permute-start.12
  69.0 1.1 collective-permute-start.11
  70.1 0.7 collective-permute-start.3
  70.8 9.0 %collective-permute-done.8.refs_1_ = bf16[2,256,128]{2,1,0:T(8,128)(2,1)S(1)} collective-permute-done((bf16[2,256,128]{2,1,0:T(8,128)(2,1)S(1)}, bf16[2,256,128]{2,1,0:T(8,128)(2,1)S(1)}, u32[]{:S(2)}, u32[]{:S(2)}) %collective-permute-start.8) | collective-permute-done | bytes 131104 | tf_op jit(solution)/shard_map/ppermute | solution.py:484
  79.8 1.8 %collective-permute-done.13.refs_7_ = bf16[2,256,128]{2,1,0:T(8,128)(2,1)S(1)} collective-permute-done((bf16[2,256,128]{2,1,0:T(8,128)(2,1)S(1)}, bf16[2,256,128]{2,1,0:T(8,128)(2,1)S(1)}, u32[]{:S(2)}, u32[]{:S(2)}) %collective-permute-start.13) | collective-permute-done | bytes 131104 | tf_op jit(solution)/shard_map/ppermute | solution.py:484
  81.6 2.9 %collective-permute-done.12.refs_6_ = bf16[2,256,128]{2,1,0:T(8,128)(2,1)S(1)} collective-permute-done((bf16[2,256,128]{2,1,0:T(8,128)(2,1)S(1)}, bf16[2,256,128]{2,1,0:T(8,128)(2,1)S(1)}, u32[]{:S(2)}, u32[]{:S(2)}) %collective-permute-start.12) | collective-permute-done | bytes 131104 | tf_op jit(solution)/shard_map/ppermute | solution.py:484
  84.6 3.6 %collective-permute-start.15 = (bf16[8,256,128]{2,1,0:T(8,128)(2,1)S(1)}, bf16[8,256,128]{2,1,0:T(8,128)(2,1)S(1)}, u32[]{:S(2)}, u32[]{:S(2)}) collective-permute-start(bf16[8,256,128]{2,1,0:T(8,128)(2,1)S(1)} %get-tuple-element.28.z0_ref), channel_id=1, source_target_pairs={{0,96},{4,100},{8,104},{12,108},{16,112},{20,116},{24,120},{28,124... | collective-permute-start | bytes 1572872 | tf_op jit(solution)/shard_map/ppermute | solution.py:484
  88.2 2.6 %collective-permute-start.17 = (bf16[8,256,128]{2,1,0:T(8,128)(2,1)S(1)}, bf16[8,256,128]{2,1,0:T(8,128)(2,1)S(1)}, u32[]{:S(2)}, u32[]{:S(2)}) collective-permute-start(bf16[8,256,128]{2,1,0:T(8,128)(2,1)S(1)} %get-tuple-element.29.x0_ref), channel_id=1, source_target_pairs={{0,24},{4,28},{8,0},{12,4},{16,8},{20,12},{24,16},{28,20},{32,56},... | collective-permute-start | bytes 1572872 | tf_op jit(solution)/shard_map/ppermute | solution.py:484
  90.8 3.4 %collective-permute-start.5 = (bf16[4,32,512]{2,1,0:T(8,128)(2,1)S(1)}, bf16[4,32,512]{2,1,0:T(8,128)(2,1)S(1)}, u32[]{:S(2)}, u32[]{:S(2)}) collective-permute-start(bf16[4,32,512]{2,1,0:T(8,128)(2,1)S(1)} %collective-permute-done.3), channel_id=1, source_target_pairs={{0,2},{1,3},{2,0},{3,1},{4,6},{5,7},{6,4},{7,5},{8,10},{9,11},{10,... | collective-permute-start | bytes 393224 | tf_op jit(solution)/shard_map/ppermute | solution.py:510
  94.2 3.1 %collective-permute-done.5 = bf16[4,32,512]{2,1,0:T(8,128)(2,1)S(1)} collective-permute-done((bf16[4,32,512]{2,1,0:T(8,128)(2,1)S(1)}, bf16[4,32,512]{2,1,0:T(8,128)(2,1)S(1)}, u32[]{:S(2)}, u32[]{:S(2)}) %collective-permute-start.5) | collective-permute-done | bytes 131104 | tf_op jit(solution)/shard_map/ppermute | solution.py:510
  97.3 1.3 %collective-permute-done.4 = bf16[4,32,512]{2,1,0:T(8,128)(2,1)S(1)} collective-permute-done((bf16[4,32,512]{2,1,0:T(8,128)(2,1)S(1)}, bf16[4,32,512]{2,1,0:T(8,128)(2,1)S(1)}, u32[]{:S(2)}, u32[]{:S(2)}) %collective-permute-start.4) | collective-permute-done | bytes 131104 | tf_op jit(solution)/shard_map/ppermute | solution.py:509
  98.6 0.1 collective-permute-start.6
  98.8 1.2 collective-permute-done.6
  100.0 0.3 copy.23
  100.4 0.7 slice.91
  101.1 3.2 %collective-permute-start.19 = (bf16[4,256,128]{2,1,0:T(8,128)(2,1)}, bf16[4,256,128]{2,1,0:T(8,128)(2,1)}, u32[]{:S(2)}, u32[]{:S(2)}) collective-permute-start(bf16[4,256,128]{2,1,0:T(8,128)(2,1)} %slice.91), channel_id=1, source_target_pairs={{0,96},{4,100},{8,104},{12,108},{16,112},{20,116},{24,120},{28,124... | collective-permute-start | bytes 786440 | tf_op jit(solution)/shard_map/ppermute | solution.py:484
  104.3 0.7 slice.90
  105.0 0.7 slice.93
  105.8 3.2 %collective-permute-start.21 = (bf16[4,256,128]{2,1,0:T(8,128)(2,1)}, bf16[4,256,128]{2,1,0:T(8,128)(2,1)}, u32[]{:S(2)}, u32[]{:S(2)}) collective-permute-start(bf16[4,256,128]{2,1,0:T(8,128)(2,1)} %slice.93), channel_id=1, source_target_pairs={{0,24},{4,28},{8,0},{12,4},{16,8},{20,12},{24,16},{28,20},{32,56},... | collective-permute-start | bytes 786440 | tf_op jit(solution)/shard_map/ppermute | solution.py:484
  109.0 0.8 slice.92
  109.8 0.1 copy-done
  109.9 1.0 copy-done.2
  110.9 3.6 %early.1.part_ref = f32[1152,128]{1,0:T(8,128)S(1)} custom-call(s32[36]{0:T(128)S(1)} %stack.190.place_ref, bf16[512,512]{1,0:T(8,128)(2,1)S(1)} %bitcast.86, f32[1,128]{1,0:T(1,128)S(1)} %bitcast.95, f32[512,4]{1,0:T(8,128)S(1)} %fusion.1.inverse_ref, f32[1024,128]{1,0:T(8,128)S(1)} %copy-done.2, bf16[8,256,128]{2,1,0:T(8,128)(2,1)S(1)} %get-tuple-element.28.z0_ref, ...), custom_call_target="tpu_custom_call" | custom-call | flops 3000000000 | bytes 6291456 | tf_op jit(solution)/shard_map/early/pallas_call | solution.py:540
  114.5 0.8 copy-done.14
  115.3 1.5 %arrange.1 = bf16[4,512,256]{2,1,0:T(8,128)(2,1)} custom-call(bf16[128,16,256]{2,1,0:T(8,128)(2,1)S(1)} %all-to-all-done.1.back_ref), custom_call_target="tpu_custom_call" | custom-call | flops 500000000 | bytes 2097152 | tf_op jit(solution)/shard_map/arrange/pallas_call | solution.py:558
  116.9 2.2 %collective-permute-done.20.xa_ref = bf16[4,256,128]{2,1,0:T(8,128)(2,1)} collective-permute-done((bf16[4,256,128]{2,1,0:T(8,128)(2,1)}, bf16[4,256,128]{2,1,0:T(8,128)(2,1)}, u32[]{:S(2)}, u32[]{:S(2)}) %collective-permute-start.20) | collective-permute-done | bytes 262176 | tf_op jit(solution)/shard_map/ppermute | solution.py:484
  119.1 1.0 copy-done.1
  120.1 1.0 copy-done.3
  121.2 1.0 copy-done.5
  122.2 1.0 copy-done.7
  123.3 1.1 copy-done.15
  124.3 4.9 %late.1 = f32[16,128,128]{2,1,0:T(8,128)} custom-call(s32[36]{0:T(128)S(1)} %stack.190.place_ref, bf16[512,512]{1,0:T(8,128)(2,1)S(1)} %bitcast.87, f32[1,128]{1,0:T(1,128)S(1)} %bitcast.96, f32[512,4]{1,0:T(8,128)S(1)} %fusion.1.inverse_ref, f32[1024,128]{1,0:T(8,128)S(1)} %copy-done.3, f32[1152,128]{1,0:T(8,128)S(1)} %copy-done.15, ...), custom_call_target="tpu_custom_call" | custom-call | flops 3000000000 | bytes 6291456 | tf_op jit(solution)/shard_map/late/pallas_call | solution.py:572
  (67 shorter events, 0.5 us)
Async XLA Ops:
  2.2 17.3 %collective-permute-start.1 = (bf16[336,256]{1,0:T(8,128)(2,1)S(1)}, bf16[336,256]{1,0:T(8,128)(2,1)S(1)}, u32[]{:S(2)}, u32[]{:S(2)}) collective-permute-start(bf16[336,256]{1,0:T(8,128)(2,1)S(1)} %pad_maximum_fusion.w0_ref), channel_id=1, source_target_pairs={{0,6},{1,7},{2,4},{3,5},{4,2},{5,3},{6,0},{7,1},{8,14},{9,15},{10,... | collective-permute-start | bytes 516104 | tf_op jit(solution)/shard_map/ppermute | solution.py:360
  5.5 14.4 %collective-permute-start = (bf16[336,256]{1,0:T(8,128)(2,1)S(1)}, bf16[336,256]{1,0:T(8,128)(2,1)S(1)}, u32[]{:S(2)}, u32[]{:S(2)}) collective-permute-start(bf16[336,256]{1,0:T(8,128)(2,1)S(1)} %pad_maximum_fusion.w0_ref), channel_id=1, source_target_pairs={{0,1},{1,0},{2,3},{3,2},{4,5},{5,4},{6,7},{7,6},{8,9},{9,8},{10,11... | collective-permute-start | bytes 516104 | tf_op jit(solution)/shard_map/ppermute | solution.py:363
  5.5 11.5 %copy-start.18 = (s32[512]{0:T(512)S(1)}, s32[512]{0:T(512)}, u32[]{:S(2)}) copy-start(s32[512]{0:T(512)} %param.18) | copy-start | bytes 6148
  5.5 11.6 %copy-start.17 = (s32[512]{0:T(512)S(1)}, s32[512]{0:T(512)}, u32[]{:S(2)}) copy-start(s32[512]{0:T(512)} %param.17) | copy-start | bytes 6148
  5.5 13.3 %copy-start.16 = (bf16[256,2,32]{0,2,1:T(8,128)(2,1)S(1)}, bf16[256,2,32]{0,2,1:T(8,128)(2,1)}, u32[]{:S(2)}) copy-start(bf16[256,2,32]{0,2,1:T(8,128)(2,1)} %param.27) | copy-start | bytes 98308
  6.8 28.4 %copy-start.8 = (f32[256]{0:T(256)S(1)}, f32[256]{0:T(256)}, u32[]{:S(2)}) copy-start(f32[256]{0:T(256)} %param.19) | copy-start | bytes 3076
  6.8 28.4 %copy-start.9 = (f32[256]{0:T(256)S(1)}, f32[256]{0:T(256)}, u32[]{:S(2)}) copy-start(f32[256]{0:T(256)} %param.20) | copy-start | bytes 3076
  6.8 28.4 %copy-start.10 = (f32[256]{0:T(256)S(1)}, f32[256]{0:T(256)}, u32[]{:S(2)}) copy-start(f32[256]{0:T(256)} %param.24) | copy-start | bytes 3076
  6.8 28.3 %copy-start.11 = (f32[256]{0:T(256)S(1)}, f32[256]{0:T(256)}, u32[]{:S(2)}) copy-start(f32[256]{0:T(256)} %param.25) | copy-start | bytes 3076
  6.9 28.3 %copy-start.12 = (f32[256]{0:T(256)S(1)}, f32[256]{0:T(256)}, u32[]{:S(2)}) copy-start(f32[256]{0:T(256)} %param.26) | copy-start | bytes 3076
  8.5 26.7 %all-to-all-start = ((bf16[32,64,256]{2,1,0:T(8,128)(2,1)}), bf16[32,64,256]{2,1,0:T(8,128)(2,1)S(1)}, u32[]{:S(2)}, u32[]{:S(2)}) async-start(bf16[32,64,256]{2,1,0:T(8,128)(2,1)} %bitcast.97), calls=%async_computation | async-start | bytes 2097152 | tf_op jit(solution)/shard_map/all_to_all | solution.py:374
  19.5 1.5 %collective-permute-start.2 = (bf16[336,256]{1,0:T(8,128)(2,1)S(1)}, bf16[336,256]{1,0:T(8,128)(2,1)S(1)}, u32[]{:S(2)}, u32[]{:S(2)}) collective-permute-start(bf16[336,256]{1,0:T(8,128)(2,1)S(1)} %collective-permute-done.1.w2_ref), channel_id=1, source_target_pairs={{0,1},{1,0},{2,3},{3,2},{4,5},{5,4},{6,7},{7,6},{8,9},{9,8},{10,11... | collective-permute-start | bytes 516104 | tf_op jit(solution)/shard_map/ppermute | solution.py:365
  50.4 59.5 %copy-start.13 = (f32[128]{0:T(128)S(1)}, f32[128]{0:T(128)}, u32[]{:S(2)}) copy-start(f32[128]{0:T(128)} %param.29) | copy-start | bytes 1540
  50.4 5.0 %collective-permute-start.7 = (bf16[2,256,128]{2,1,0:T(8,128)(2,1)S(1)}, bf16[2,256,128]{2,1,0:T(8,128)(2,1)S(1)}, u32[]{:S(2)}, u32[]{:S(2)}) collective-permute-start(bf16[2,256,128]{2,1,0:T(8,128)(2,1)S(1)} %get-tuple-element.27), channel_id=1, source_target_pairs={{0,4},{4,0},{8,12},{12,8},{16,20},{20,16},{24,28},{28,24},{32,36},... | collective-permute-start | bytes 393224 | tf_op jit(solution)/shard_map/ppermute | solution.py:484
  55.4 13.6 %collective-permute-start.10 = (bf16[2,256,128]{2,1,0:T(8,128)(2,1)S(1)}, bf16[2,256,128]{2,1,0:T(8,128)(2,1)S(1)}, u32[]{:S(2)}, u32[]{:S(2)}) collective-permute-start(bf16[2,256,128]{2,1,0:T(8,128)(2,1)S(1)} %pad_maximum_fusion.1.refs_0_), channel_id=1, source_target_pairs={{0,16},{4,20},{8,24},{12,28},{16,0},{20,4},{24,8},{28,12},{32,48},... | collective-permute-start | bytes 393224 | tf_op jit(solution)/shard_map/ppermute | solution.py:484
  56.4 13.6 %collective-permute-start.9 = (bf16[2,256,128]{2,1,0:T(8,128)(2,1)S(1)}, bf16[2,256,128]{2,1,0:T(8,128)(2,1)S(1)}, u32[]{:S(2)}, u32[]{:S(2)}) collective-permute-start(bf16[2,256,128]{2,1,0:T(8,128)(2,1)S(1)} %pad_maximum_fusion.1.refs_0_), channel_id=1, source_target_pairs={{0,24},{4,28},{8,0},{12,4},{16,8},{20,12},{24,16},{28,20},{32,56},... | collective-permute-start | bytes 393224 | tf_op jit(solution)/shard_map/ppermute | solution.py:484
  58.7 56.6 %all-to-all-start.1 = ((bf16[128,16,256]{2,1,0:T(8,128)(2,1)}), bf16[128,16,256]{2,1,0:T(8,128)(2,1)S(1)}, u32[]{:S(2)}, u32[]{:S(2)}) async-start(bf16[128,16,256]{2,1,0:T(8,128)(2,1)} %bitcast.62), calls=%async_computation.1 | async-start | bytes 2097152 | tf_op jit(solution)/shard_map/all_to_all | solution.py:525
  63.4 16.4 %collective-permute-start.8 = (bf16[2,256,128]{2,1,0:T(8,128)(2,1)S(1)}, bf16[2,256,128]{2,1,0:T(8,128)(2,1)S(1)}, u32[]{:S(2)}, u32[]{:S(2)}) collective-permute-start(bf16[2,256,128]{2,1,0:T(8,128)(2,1)S(1)} %pad_maximum_fusion.1.refs_0_), channel_id=1, source_target_pairs={{0,8},{4,12},{8,16},{12,20},{16,24},{20,28},{24,0},{28,4},{32,40},... | collective-permute-start | bytes 393224 | tf_op jit(solution)/shard_map/ppermute | solution.py:484
  64.3 17.3 %collective-permute-start.13 = (bf16[2,256,128]{2,1,0:T(8,128)(2,1)S(1)}, bf16[2,256,128]{2,1,0:T(8,128)(2,1)S(1)}, u32[]{:S(2)}, u32[]{:S(2)}) collective-permute-start(bf16[2,256,128]{2,1,0:T(8,128)(2,1)S(1)} %pad_maximum_fusion.2.refs_4_), channel_id=1, source_target_pairs={{0,64},{4,68},{8,72},{12,76},{16,80},{20,84},{24,88},{28,92},{32,9... | collective-permute-start | bytes 393224 | tf_op jit(solution)/shard_map/ppermute | solution.py:484
  68.1 16.4 %collective-permute-start.12 = (bf16[2,256,128]{2,1,0:T(8,128)(2,1)S(1)}, bf16[2,256,128]{2,1,0:T(8,128)(2,1)S(1)}, u32[]{:S(2)}, u32[]{:S(2)}) collective-permute-start(bf16[2,256,128]{2,1,0:T(8,128)(2,1)S(1)} %pad_maximum_fusion.2.refs_4_), channel_id=1, source_target_pairs={{0,96},{4,100},{8,104},{12,108},{16,112},{20,116},{24,120},{28,124... | collective-permute-start | bytes 393224 | tf_op jit(solution)/shard_map/ppermute | solution.py:484
  69.0 15.5 %collective-permute-start.11 = (bf16[2,256,128]{2,1,0:T(8,128)(2,1)S(1)}, bf16[2,256,128]{2,1,0:T(8,128)(2,1)S(1)}, u32[]{:S(2)}, u32[]{:S(2)}) collective-permute-start(bf16[2,256,128]{2,1,0:T(8,128)(2,1)S(1)} %pad_maximum_fusion.2.refs_4_), channel_id=1, source_target_pairs={{0,32},{4,36},{8,40},{12,44},{16,48},{20,52},{24,56},{28,60},{32,6... | collective-permute-start | bytes 393224 | tf_op jit(solution)/shard_map/ppermute | solution.py:484
  70.1 20.7 %collective-permute-start.3 = (bf16[4,32,512]{2,1,0:T(8,128)(2,1)S(1)}, bf16[4,32,512]{2,1,0:T(8,128)(2,1)S(1)}, u32[]{:S(2)}, u32[]{:S(2)}) collective-permute-start(bf16[4,32,512]{2,1,0:T(8,128)(2,1)S(1)} %get-tuple-element.25), channel_id=1, source_target_pairs={{0,0},{1,32},{2,64},{3,96},{4,4},{5,36},{6,68},{7,100},{8,8},{9,40... | collective-permute-start | bytes 393224 | tf_op jit(solution)/shard_map/ppermute | solution.py:474
  84.6 25.2 %copy-start.4 = (bf16[8,256,128]{2,1,0:T(8,128)(2,1)}, bf16[8,256,128]{2,1,0:T(8,128)(2,1)S(1)}, u32[]{:S(2)}) copy-start(bf16[8,256,128]{2,1,0:T(8,128)(2,1)S(1)} %get-tuple-element.28.z0_ref) | copy-start | bytes 1572868
  84.6 25.2 %copy-start.6 = (bf16[8,256,128]{2,1,0:T(8,128)(2,1)}, bf16[8,256,128]{2,1,0:T(8,128)(2,1)S(1)}, u32[]{:S(2)}) copy-start(bf16[8,256,128]{2,1,0:T(8,128)(2,1)S(1)} %get-tuple-element.29.x0_ref) | copy-start | bytes 1572868
  84.6 15.8 %collective-permute-start.15 = (bf16[8,256,128]{2,1,0:T(8,128)(2,1)S(1)}, bf16[8,256,128]{2,1,0:T(8,128)(2,1)S(1)}, u32[]{:S(2)}, u32[]{:S(2)}) collective-permute-start(bf16[8,256,128]{2,1,0:T(8,128)(2,1)S(1)} %get-tuple-element.28.z0_ref), channel_id=1, source_target_pairs={{0,96},{4,100},{8,104},{12,108},{16,112},{20,116},{24,120},{28,124... | collective-permute-start | bytes 1572872 | tf_op jit(solution)/shard_map/ppermute | solution.py:484
  88.2 16.2 %collective-permute-start.14 = (bf16[8,256,128]{2,1,0:T(8,128)(2,1)S(1)}, bf16[8,256,128]{2,1,0:T(8,128)(2,1)S(1)}, u32[]{:S(2)}, u32[]{:S(2)}) collective-permute-start(bf16[8,256,128]{2,1,0:T(8,128)(2,1)S(1)} %get-tuple-element.28.z0_ref), channel_id=1, source_target_pairs={{0,32},{4,36},{8,40},{12,44},{16,48},{20,52},{24,56},{28,60},{32,6... | collective-permute-start | bytes 1572872 | tf_op jit(solution)/shard_map/ppermute | solution.py:484
  88.2 16.9 %collective-permute-start.17 = (bf16[8,256,128]{2,1,0:T(8,128)(2,1)S(1)}, bf16[8,256,128]{2,1,0:T(8,128)(2,1)S(1)}, u32[]{:S(2)}, u32[]{:S(2)}) collective-permute-start(bf16[8,256,128]{2,1,0:T(8,128)(2,1)S(1)} %get-tuple-element.29.x0_ref), channel_id=1, source_target_pairs={{0,24},{4,28},{8,0},{12,4},{16,8},{20,12},{24,16},{28,20},{32,56},... | collective-permute-start | bytes 1572872 | tf_op jit(solution)/shard_map/ppermute | solution.py:484
  90.8 18.2 %collective-permute-start.16 = (bf16[8,256,128]{2,1,0:T(8,128)(2,1)S(1)}, bf16[8,256,128]{2,1,0:T(8,128)(2,1)S(1)}, u32[]{:S(2)}, u32[]{:S(2)}) collective-permute-start(bf16[8,256,128]{2,1,0:T(8,128)(2,1)S(1)} %get-tuple-element.29.x0_ref), channel_id=1, source_target_pairs={{0,8},{4,12},{8,16},{12,20},{16,24},{20,28},{24,0},{28,4},{32,40},... | collective-permute-start | bytes 1572872 | tf_op jit(solution)/shard_map/ppermute | solution.py:484
  90.8 6.5 %collective-permute-start.5 = (bf16[4,32,512]{2,1,0:T(8,128)(2,1)S(1)}, bf16[4,32,512]{2,1,0:T(8,128)(2,1)S(1)}, u32[]{:S(2)}, u32[]{:S(2)}) collective-permute-start(bf16[4,32,512]{2,1,0:T(8,128)(2,1)S(1)} %collective-permute-done.3), channel_id=1, source_target_pairs={{0,2},{1,3},{2,0},{3,1},{4,6},{5,7},{6,4},{7,5},{8,10},{9,11},{10,... | collective-permute-start | bytes 393224 | tf_op jit(solution)/shard_map/ppermute | solution.py:510
  97.3 1.3 %collective-permute-start.4 = (bf16[4,32,512]{2,1,0:T(8,128)(2,1)S(1)}, bf16[4,32,512]{2,1,0:T(8,128)(2,1)S(1)}, u32[]{:S(2)}, u32[]{:S(2)}) collective-permute-start(bf16[4,32,512]{2,1,0:T(8,128)(2,1)S(1)} %collective-permute-done.3), channel_id=1, source_target_pairs={{0,1},{1,0},{2,3},{3,2},{4,5},{5,4},{6,7},{7,6},{8,9},{9,8},{10,11... | collective-permute-start | bytes 393224 | tf_op jit(solution)/shard_map/ppermute | solution.py:509
  98.6 1.3 %collective-permute-start.6 = (bf16[4,32,512]{2,1,0:T(8,128)(2,1)S(1)}, bf16[4,32,512]{2,1,0:T(8,128)(2,1)S(1)}, u32[]{:S(2)}, u32[]{:S(2)}) collective-permute-start(bf16[4,32,512]{2,1,0:T(8,128)(2,1)S(1)} %collective-permute-done.5), channel_id=1, source_target_pairs={{0,1},{1,0},{2,3},{3,2},{4,5},{5,4},{6,7},{7,6},{8,9},{9,8},{10,11... | collective-permute-start | bytes 393224 | tf_op jit(solution)/shard_map/ppermute | solution.py:511
  101.1 15.8 %collective-permute-start.19 = (bf16[4,256,128]{2,1,0:T(8,128)(2,1)}, bf16[4,256,128]{2,1,0:T(8,128)(2,1)}, u32[]{:S(2)}, u32[]{:S(2)}) collective-permute-start(bf16[4,256,128]{2,1,0:T(8,128)(2,1)} %slice.91), channel_id=1, source_target_pairs={{0,96},{4,100},{8,104},{12,108},{16,112},{20,116},{24,120},{28,124... | collective-permute-start | bytes 786440 | tf_op jit(solution)/shard_map/ppermute | solution.py:484
  105.0 11.8 %collective-permute-start.18 = (bf16[4,256,128]{2,1,0:T(8,128)(2,1)}, bf16[4,256,128]{2,1,0:T(8,128)(2,1)}, u32[]{:S(2)}, u32[]{:S(2)}) collective-permute-start(bf16[4,256,128]{2,1,0:T(8,128)(2,1)} %slice.90), channel_id=1, source_target_pairs={{0,32},{4,36},{8,40},{12,44},{16,48},{20,52},{24,56},{28,60},{32,6... | collective-permute-start | bytes 786440 | tf_op jit(solution)/shard_map/ppermute | solution.py:484
  105.8 11.1 %collective-permute-start.21 = (bf16[4,256,128]{2,1,0:T(8,128)(2,1)}, bf16[4,256,128]{2,1,0:T(8,128)(2,1)}, u32[]{:S(2)}, u32[]{:S(2)}) collective-permute-start(bf16[4,256,128]{2,1,0:T(8,128)(2,1)} %slice.93), channel_id=1, source_target_pairs={{0,24},{4,28},{8,0},{12,4},{16,8},{20,12},{24,16},{28,20},{32,56},... | collective-permute-start | bytes 786440 | tf_op jit(solution)/shard_map/ppermute | solution.py:484
  109.0 0.9 copy-start
  109.8 9.3 %collective-permute-start.20 = (bf16[4,256,128]{2,1,0:T(8,128)(2,1)}, bf16[4,256,128]{2,1,0:T(8,128)(2,1)}, u32[]{:S(2)}, u32[]{:S(2)}) collective-permute-start(bf16[4,256,128]{2,1,0:T(8,128)(2,1)} %slice.92), channel_id=1, source_target_pairs={{0,8},{4,12},{8,16},{12,20},{16,24},{20,28},{24,0},{28,4},{32,40},... | collective-permute-start | bytes 786440 | tf_op jit(solution)/shard_map/ppermute | solution.py:484
  109.9 1.0 copy-start.2
  114.5 0.8 copy-start.14
  119.1 1.0 copy-start.1
  120.1 1.0 copy-start.3
  121.2 1.0 copy-start.5
  122.2 1.0 copy-start.7
  123.3 1.1 copy-start.15
